TPU v7x, 128 devices: a whole 4x4x4 slice. The times are simulated.
128 devices in a mesh: gx: 4 (over y), gy: 4 (over x_hi, core), gz: 8 (over z, x_lo).
Axes of the slice: x: 4 (x_hi: 2, x_lo: 2; x = x_hi * 2 + x_lo), y: 4, z: 4, core: 2. Of those that a mesh axis runs over, the one named last changes fastest.
Arguments:
- offset: float32 [3, 32, 32, 1024], P(None, 'gx', 'gy', 'gz'), may hold values from -0.25 to 0.25
- velocity: float32 [3, 32, 32, 1024], P(None, 'gx', 'gy', 'gz'), may hold values from -3 to 3
- spin: float32 [3, 32, 32, 1024], P(None, 'gx', 'gy', 'gz'), may hold values from -3 to 3
- radius: float32 [32, 32, 1024], P('gx', 'gy', 'gz'), may hold values from 0.62 to 0.82
- history: float32 [6, 3, 32, 32, 1024], P(None, None, 'gx', 'gy', 'gz'), may hold values from -0.3 to 0.3
- contacts: int32 [6, 32, 32, 1024], P(None, 'gx', 'gy', 'gz'), may hold values from -1 to 8, as said below
- leaving: int32 [4, 4, 8, 64], P('gx', 'gy', 'gz'), may hold values from -1 to 8191, as said below
Outputs:
- new_offset: float32 [3, 32, 32, 1024], P(None, 'gx', 'gy', 'gz')
- new_velocity: float32 [3, 32, 32, 1024], P(None, 'gx', 'gy', 'gz')
- new_spin: float32 [3, 32, 32, 1024], P(None, 'gx', 'gy', 'gz')
- new_history: float32 [6, 3, 32, 32, 1024], P(None, None, 'gx', 'gy', 'gz')
- arrivals: float32 [28, 4, 4, 8, 64], P(None, 'gx', 'gy', 'gz')
Inputs may be any that keep to these rules, and one draw needn't show every extreme that they name: `contacts`: the live codes of one particle are distinct. `leaving`: each block's live entries are distinct cells with z index 0 or 1 within the block, listed first and followed by -1; at most 64 are live, and some block has 64 live.
All inputs are finite; a program needn't handle non-finite values.
Results may differ from a plain program's by a relative error of at most 0.0003.
Values sent between devices are 32-bit elements; how exact they have to be, the bound alone decides.
A program may use at most 512 MiB of HBM per device.

v0:
```python
import jax
import jax.numpy as jnp
from jax import lax
from jax.sharding import PartitionSpec as P

forward_dirs = [
    [1, 0, 0],
    [0, 1, 0],
    [0, 0, 1],
    [1, 1, 0],
    [1, -1, 0],
    [1, 0, 1],
    [1, 0, -1],
    [0, 1, 1],
    [0, 1, -1],
]
stiff_normal = 10.0
damp_normal = 2.0
stiff_shear = 8.0
damp_shear = 1.5
friction = 0.4
shear_floor = 0.05
time_step = 0.05
gravity = 1.0


def padded_2(cells, sides, width):
    for axis, dim in sides:
        count = lax.axis_size(axis)
        ends = count - 1
        head = lax.slice_in_dim(cells, 0, width, axis=dim)
        tail = lax.slice_in_dim(cells, cells.shape[dim] - width, cells.shape[dim], axis=dim)
        cells = jnp.concatenate(
            [
                lax.ppermute(tail, axis, [(i, (i + 1) % count) for i in range(ends)]),
                cells,
                lax.ppermute(head, axis, [((i + 1) % count, i) for i in range(ends)]),
            ],
            axis=dim,
        )
    return cells


def from_behind(block, axis, distance):
    devices = range(lax.axis_size(axis))
    route = [(i - distance, i) for i in devices if i - distance in devices]
    return lax.ppermute(block, axis, route)


def cross_product(first_vec, second_vec):
    return jnp.stack(
        [
            first_vec[1] * second_vec[2] - first_vec[2] * second_vec[1],
            first_vec[2] * second_vec[0] - first_vec[0] * second_vec[2],
            first_vec[0] * second_vec[1] - first_vec[1] * second_vec[0],
        ],
        0,
    )


def contact_pair(centers, partner, direction, shear):
    separation = direction + partner[0:3] - centers[0:3]
    distance = jnp.sqrt(jnp.sum(separation * separation, 0))
    normal = separation / distance
    radius_center = centers[9]
    radius_partner = partner[9]
    radius_sum = radius_center + radius_partner
    intersection = jnp.maximum(radius_sum - distance, 0.0)
    contact = jnp.sqrt(radius_center * radius_partner / radius_sum * intersection)
    relative = (
        partner[3:6]
        - centers[3:6]
        - cross_product(radius_center * centers[6:9] + radius_partner * partner[6:9], normal)
    )
    approach = jnp.sum(relative * normal, 0)
    sliding = relative - approach * normal
    repulsion = jnp.maximum(
        stiff_normal * contact * intersection - damp_normal * contact * approach, 0.0
    )
    spring = shear - jnp.sum(shear * normal, 0) * normal + time_step * sliding
    trial_force = stiff_shear * contact * spring + damp_shear * contact * sliding
    magnitude = jnp.sqrt(jnp.sum(trial_force * trial_force, 0))
    factor = jnp.minimum(1.0, friction * repulsion / jnp.maximum(magnitude, shear_floor))
    tangent = factor * trial_force
    pair_force = tangent - repulsion * normal
    twisting = cross_product(normal, tangent)
    return (pair_force, radius_center * twisting, radius_partner * twisting, factor * spring)


def contact_terms(centers, shear, codes, source, margin):
    count_x, count_y, count_z = centers.shape[1:]
    channels = source.shape[0]
    windows = []
    for step_dir in forward_dirs:
        begin = (0, margin + step_dir[0], margin + step_dir[1], margin + step_dir[2])
        finish = (channels, begin[1] + count_x, begin[2] + count_y, begin[3] + count_z)
        windows.append((begin, lax.slice(source, begin, finish)))
    own_terms = jnp.zeros((6, count_x, count_y, count_z), jnp.float32)
    per_dir = [jnp.zeros((6, count_x, count_y, count_z), jnp.float32) for step_dir in forward_dirs]
    springs = []
    for which_slot in range(codes.shape[0]):
        slot_code = codes[which_slot]
        slot_live = slot_code >= 0
        chosen = jnp.maximum(slot_code, 0)
        partner = jnp.zeros((channels, count_x, count_y, count_z), jnp.float32)
        direction = jnp.zeros((3, count_x, count_y, count_z), jnp.float32)
        for number, step_dir in enumerate(forward_dirs):
            picked_here = (chosen == number)[None]
            partner = partner + jnp.where(picked_here, windows[number][1], 0.0)
            direction = direction + jnp.where(
                picked_here, jnp.asarray(step_dir, jnp.float32).reshape(3, 1, 1, 1), 0.0
            )
        pair_force, torque_center, torque_partner, spring = contact_pair(
            centers, partner, direction, shear[which_slot]
        )
        own_terms = own_terms + jnp.where(
            slot_live[None], jnp.concatenate([pair_force, torque_center], 0), 0.0
        )
        reaction = jnp.where(
            slot_live[None], jnp.concatenate([-pair_force, torque_partner], 0), 0.0
        )
        for number in range(len(forward_dirs)):
            per_dir[number] = per_dir[number] + jnp.where((chosen == number)[None], reaction, 0.0)
        springs.append(jnp.where(slot_live[None], spring, 0.0))
    partner_terms = jnp.zeros((6,) + source.shape[1:], jnp.float32)
    for number in range(len(forward_dirs)):
        begin = windows[number][0]
        widths = (
            (0, 0),
            (begin[1], source.shape[1] - begin[1] - count_x),
            (begin[2], source.shape[2] - begin[2] - count_y),
            (begin[3], source.shape[3] - begin[3] - count_z),
        )
        partner_terms = partner_terms + jnp.pad(per_dir[number], widths)
    return (own_terms, partner_terms, jnp.stack(springs, 0))


def fold_rims(extended, axis_dim):
    length = extended.shape[axis_dim]
    middle = lax.slice_in_dim(extended, 2, length - 2, axis=axis_dim)
    lower = lax.slice_in_dim(extended, 0, 1, axis=axis_dim)
    upper = lax.slice_in_dim(extended, length - 1, length, axis=axis_dim)
    inner = middle.shape[axis_dim]
    return jnp.concatenate(
        [
            lax.slice_in_dim(middle, 0, 1, axis=axis_dim) + lower,
            lax.slice_in_dim(middle, 1, inner - 1, axis=axis_dim),
            lax.slice_in_dim(middle, inner - 1, inner, axis=axis_dim) + upper,
        ],
        axis_dim,
    )


def on_device(offset, velocity, spin, radius, history, contacts, leaving):
    cells_x, cells_y, cells_z = radius.shape
    slot_count = contacts.shape[0]
    fields = jnp.concatenate([offset, velocity, spin, radius[None]], 0)
    padded = padded_2(fields, (("gx", 1), ("gy", 2), ("gz", 3)), 1)
    own_terms, partner_terms, springs = contact_terms(fields, history, contacts, padded, 1)
    extended = padded_2(partner_terms, (("gx", 1), ("gy", 2), ("gz", 3)), 1)
    returned = fold_rims(fold_rims(fold_rims(extended, 1), 2), 3)
    totals = own_terms + returned
    particle_mass = radius**3
    downward = jnp.asarray([0.0, 0.0, -gravity], dtype=jnp.float32).reshape(3, 1, 1, 1)
    moved_velocity = velocity + time_step * (totals[0:3] / particle_mass + downward)
    moved_spin = spin + time_step * totals[3:6] / (0.4 * particle_mass * radius * radius)
    moved_offset = offset + time_step * moved_velocity
    bottom_shape = (cells_x, cells_y, 2)
    coord_x = jnp.broadcast_to(
        (lax.axis_index("gx") * cells_x + jnp.arange(cells_x, dtype=jnp.int32)).astype(jnp.float32)[
            :, None, None
        ],
        bottom_shape,
    )
    coord_y = jnp.broadcast_to(
        (lax.axis_index("gy") * cells_y + jnp.arange(cells_y, dtype=jnp.int32)).astype(jnp.float32)[
            None, :, None
        ],
        bottom_shape,
    )
    coord_z = jnp.broadcast_to(
        (lax.axis_index("gz") * cells_z + jnp.arange(2, dtype=jnp.int32)).astype(jnp.float32)[
            None, None, :
        ],
        bottom_shape,
    )
    bottom_position = jnp.stack([coord_x, coord_y, coord_z], 0) + moved_offset[:, :, :, 0:2]
    bottom_count = cells_x * cells_y * 2
    pieces = [
        bottom_position,
        moved_velocity[:, :, :, 0:2],
        moved_spin[:, :, :, 0:2],
        radius[None, :, :, 0:2],
        springs[:, :, :, :, 0:2].reshape(3 * slot_count, cells_x, cells_y, 2),
    ]
    bottom_rows = jnp.concatenate(
        [piece.reshape(piece.shape[0], bottom_count) for piece in pieces], 0
    )
    leave_index = leaving.reshape(-1)
    leave_live = leave_index >= 0
    picked = jnp.maximum(leave_index, 0)
    candidate = picked // cells_z * 2 + picked % cells_z
    selector = jnp.logical_and(
        jnp.arange(bottom_count, dtype=jnp.int32)[:, None] == candidate[None, :],
        leave_live[None, :],
    ).astype(jnp.float32)
    outbox = jnp.dot(
        bottom_rows, selector, precision=lax.Precision.HIGHEST, preferred_element_type=jnp.float32
    )
    arrivals = from_behind(outbox, "gz", -1)
    arrivals = arrivals.reshape(outbox.shape[0], 1, 1, 1, outbox.shape[1])
    departed = jnp.sum(selector, 1).reshape(cells_x, cells_y, 2)
    staying = jnp.concatenate(
        [1.0 - departed, jnp.ones((cells_x, cells_y, cells_z - 2), jnp.float32)], 2
    )
    return (
        moved_offset * staying,
        moved_velocity * staying,
        moved_spin * staying,
        springs * staying,
        arrivals,
    )


def solution(mesh):
    placed = (
        P(None, "gx", "gy", "gz"),
        P(None, "gx", "gy", "gz"),
        P(None, "gx", "gy", "gz"),
        P("gx", "gy", "gz"),
        P(None, None, "gx", "gy", "gz"),
        P(None, "gx", "gy", "gz"),
        P("gx", "gy", "gz", None),
    )
    return jax.shard_map(
        on_device,
        mesh=mesh,
        in_specs=placed,
        out_specs=(
            P(None, "gx", "gy", "gz"),
            P(None, "gx", "gy", "gz"),
            P(None, "gx", "gy", "gz"),
            P(None, None, "gx", "gy", "gz"),
            P(None, "gx", "gy", "gz", None),
        ),
        check_vma=False,
    )
```

profile of v0, /device:TPU:1, one launch (start us, length us, event | category | flops | bytes accessed | tf_op | source)
XLA Modules:
  0.0 104.5 jit_solution(9344083458529529004)
XLA Ops:
  1.5 1.3 %collective-permute-start = (f32[10,1,8,128]{3,2,1,0:T(8,128)S(1)}, f32[10,1,8,128]{3,2,1,0:T(8,128)S(1)}, u32[]{:S(2)}, u32[]{:S(2)}) collective-permute-start(f32[10,1,8,128]{3,2,1,0:T(8,128)S(1)} %get-tuple-element.147), channel_id=1, source_target_pairs={{32,0},{64,32},{96,64},{33,1},{65,33},{97,65},{34,2},{66,34},{98,6... | collective-permute-start | bytes 122888 | tf_op jit(solution)/shard_map/ppermute | solution.py:37
  2.8 4.6 %collective-permute-start.1 = (f32[10,1,8,128]{3,2,1,0:T(8,128)S(1)}, f32[10,1,8,128]{3,2,1,0:T(8,128)S(1)}, u32[]{:S(2)}, u32[]{:S(2)}) collective-permute-start(f32[10,1,8,128]{3,2,1,0:T(8,128)S(1)} %get-tuple-element.146), channel_id=1, source_target_pairs={{0,32},{32,64},{64,96},{1,33},{33,65},{65,97},{2,34},{34,66},{66,9... | collective-permute-start | bytes 122888 | tf_op jit(solution)/shard_map/ppermute | solution.py:35
  12.6 1.2 %pad_maximum_fusion.32 = (f32[10,10,1,128]{3,2,1,0:T(1,128)S(1)}, f32[10,10,1,128]{3,2,1,0:T(1,128)S(1)}) fusion(f32[10,1,8,128]{3,2,1,0:T(8,128)S(1)} %collective-permute-done, f32[10,1,8,128]{3,2,1,0:T(8,128)S(1)} %collective-permute-done.1, f32[1,8,8,128]{3,2,1,0:T(8,128)} %bitcast.285, f32[3,8,8,128]{3,2,1,0:T(8,128)} %param.64, ...), kind=kLoop, calls=%fused_computation.195 | loop fusion | flops 128000 | bytes 512000 | tf_op jit(solution)/shard_map/concatenate | solution.py:33
  13.8 3.2 %collective-permute-start.2 = (f32[10,10,1,128]{3,2,1,0:T(1,128)S(1)}, f32[10,10,1,128]{3,2,1,0:T(1,128)S(1)}, u32[]{:S(2)}, u32[]{:S(2)}) collective-permute-start(f32[10,10,1,128]{3,2,1,0:T(1,128)S(1)} %get-tuple-element.143), channel_id=1, source_target_pairs={{8,0},{16,8},{24,16},{9,1},{17,9},{25,17},{10,2},{18,10},{26,18},{... | collective-permute-start | bytes 153608 | tf_op jit(solution)/shard_map/ppermute | solution.py:37
  17.0 4.7 %collective-permute-start.3 = (f32[10,10,1,128]{3,2,1,0:T(1,128)S(1)}, f32[10,10,1,128]{3,2,1,0:T(1,128)S(1)}, u32[]{:S(2)}, u32[]{:S(2)}) collective-permute-start(f32[10,10,1,128]{3,2,1,0:T(1,128)S(1)} %get-tuple-element.142), channel_id=1, source_target_pairs={{0,8},{8,16},{16,24},{1,9},{9,17},{17,25},{2,10},{10,18},{18,26},{... | collective-permute-start | bytes 153608 | tf_op jit(solution)/shard_map/ppermute | solution.py:35
  21.7 1.2 %collective-permute-done.3 = f32[10,10,1,128]{3,2,1,0:T(1,128)S(1)} collective-permute-done((f32[10,10,1,128]{3,2,1,0:T(1,128)S(1)}, f32[10,10,1,128]{3,2,1,0:T(1,128)S(1)}, u32[]{:S(2)}, u32[]{:S(2)}) %collective-permute-start.3) | collective-permute-done | bytes 51232 | tf_op jit(solution)/shard_map/ppermute | solution.py:35
  24.0 1.3 %collective-permute-start.4 = (f32[10,10,10,1]{2,3,1,0:T(1,128)S(1)}, f32[10,10,10,1]{2,3,1,0:T(1,128)S(1)}, u32[]{:S(2)}, u32[]{:S(2)}) collective-permute-start(f32[10,10,10,1]{2,3,1,0:T(1,128)S(1)} %copy.361), channel_id=1, source_target_pairs={{1,0},{2,1},{3,2},{4,3},{5,4},{6,5},{7,6},{9,8},{10,9},{11,10},{12... | collective-permute-start | bytes 12008 | tf_op jit(solution)/shard_map/ppermute | solution.py:37
  26.0 4.0 %collective-permute-start.5 = (f32[10,10,10,1]{2,3,1,0:T(1,128)S(1)}, f32[10,10,10,1]{2,3,1,0:T(1,128)S(1)}, u32[]{:S(2)}, u32[]{:S(2)}) collective-permute-start(f32[10,10,10,1]{2,3,1,0:T(1,128)S(1)} %copy.362), channel_id=1, source_target_pairs={{0,1},{1,2},{2,3},{3,4},{4,5},{5,6},{6,7},{8,9},{9,10},{10,11},{11... | collective-permute-start | bytes 12008 | tf_op jit(solution)/shard_map/ppermute | solution.py:35
  33.4 2.3 %pad_maximum_fusion = (f32[10,10,10,129]{3,2,1,0:T(8,128)S(1)}, f32[10,10,10,129]{3,2,1,0:T(8,128)S(1)}) fusion(f32[10,10,10,1]{3,2,1,0:T(8,128)S(1)} %copy.343, f32[10,10,1,128]{3,2,1,0:T(1,128)S(1)} %collective-permute-done.2, f32[10,1,8,128]{3,2,1,0:T(8,128)S(1)} %collective-permute-done, f32[1,8,8,128]{3,2,1,0:T(8,128)S(1)} %bitcast.288, ...), kind=kLoop, calls=%fused_computation | loop fusion | flops 2064000 | bytes 1552000 | tf_op jit(solution)/shard_map/concatenate | solution.py:33
  51.0 1.4 %pad_add_fusion = f32[6,10,10,130]{3,2,1,0:T(8,128)S(1)} fusion(f32[6,8,8,128]{3,2,1,0:T(8,128)S(1)} %select_add_fusion.6, f32[6,8,8,128]{3,2,1,0:T(8,128)S(1)} %select_add_fusion.7, f32[6,8,8,128]{3,2,1,0:T(8,128)S(1)} %select_add_fusion.8, f32[6,8,8,128]{3,2,1,0:T(8,128)S(1)} %select_add_fusion.9, f32[6,8,8,128]{3,2,1,0:T(8,128)S(1)} %select_add_fusion.10, ...), kind=kLoop, calls=%fused_computation.4 | loop fusion | flops 624000 | bytes 2081472 | tf_op jit(solution)/shard_map/add | solution.py:134
  52.4 3.2 %collective-permute-start.6 = (f32[6,1,10,130]{3,2,1,0:T(8,128)S(1)}, f32[6,1,10,130]{3,2,1,0:T(8,128)S(1)}, u32[]{:S(2)}, u32[]{:S(2)}) collective-permute-start(f32[6,1,10,130]{3,2,1,0:T(8,128)S(1)} %get-tuple-element.128), channel_id=1, source_target_pairs={{0,32},{32,64},{64,96},{1,33},{33,65},{65,97},{2,34},{34,66},{66,9... | collective-permute-start | bytes 93608 | tf_op jit(solution)/shard_map/ppermute | solution.py:35
  55.6 1.3 %collective-permute-start.7 = (f32[6,1,10,130]{3,2,1,0:T(8,128)S(1)}, f32[6,1,10,130]{3,2,1,0:T(8,128)S(1)}, u32[]{:S(2)}, u32[]{:S(2)}) collective-permute-start(f32[6,1,10,130]{3,2,1,0:T(8,128)S(1)} %get-tuple-element.129), channel_id=1, source_target_pairs={{32,0},{64,32},{96,64},{33,1},{65,33},{97,65},{34,2},{66,34},{98,6... | collective-permute-start | bytes 93608 | tf_op jit(solution)/shard_map/ppermute | solution.py:37
  57.2 3.7 %collective-permute-done.7 = f32[6,1,10,130]{3,2,1,0:T(8,128)S(1)} collective-permute-done((f32[6,1,10,130]{3,2,1,0:T(8,128)S(1)}, f32[6,1,10,130]{3,2,1,0:T(8,128)S(1)}, u32[]{:S(2)}, u32[]{:S(2)}) %collective-permute-start.7) | collective-permute-done | bytes 31232 | tf_op jit(solution)/shard_map/ppermute | solution.py:37
  61.1 7.7 %collective-permute-start.8 = (f32[6,12,1,130]{3,2,1,0:T(1,128)S(1)}, f32[6,12,1,130]{3,2,1,0:T(1,128)S(1)}, u32[]{:S(2)}, u32[]{:S(2)}) collective-permute-start(f32[6,12,1,130]{3,2,1,0:T(1,128)S(1)} %get-tuple-element.126), channel_id=1, source_target_pairs={{0,8},{8,16},{16,24},{1,9},{9,17},{17,25},{2,10},{10,18},{18,26},{... | collective-permute-start | bytes 112328 | tf_op jit(solution)/shard_map/ppermute | solution.py:35
  68.9 1.9 %collective-permute-start.9 = (f32[6,12,1,130]{3,2,1,0:T(1,128)S(1)}, f32[6,12,1,130]{3,2,1,0:T(1,128)S(1)}, u32[]{:S(2)}, u32[]{:S(2)}) collective-permute-start(f32[6,12,1,130]{3,2,1,0:T(1,128)S(1)} %get-tuple-element.127), channel_id=1, source_target_pairs={{8,0},{16,8},{24,16},{9,1},{17,9},{25,17},{10,2},{18,10},{26,18},{... | collective-permute-start | bytes 112328 | tf_op jit(solution)/shard_map/ppermute | solution.py:37
  70.9 5.2 %collective-permute-done.9 = f32[6,12,1,130]{3,2,1,0:T(1,128)S(1)} collective-permute-done((f32[6,12,1,130]{3,2,1,0:T(1,128)S(1)}, f32[6,12,1,130]{3,2,1,0:T(1,128)S(1)}, u32[]{:S(2)}, u32[]{:S(2)}) %collective-permute-start.9) | collective-permute-done | bytes 37472 | tf_op jit(solution)/shard_map/ppermute | solution.py:37
  78.0 2.2 %copy.346 = f32[6,12,12,1]{2,3,1,0:T(1,128)} copy(f32[6,12,12,1]{3,2,1,0:T(8,128)} %get-tuple-element.124) | data formatting | bytes 6912 | tf_op jit(solution)/shard_map/slice | solution.py:32
  80.2 4.0 %collective-permute-start.10 = (f32[6,12,12,1]{2,3,1,0:T(1,128)}, f32[6,12,12,1]{2,3,1,0:T(1,128)}, u32[]{:S(2)}, u32[]{:S(2)}) collective-permute-start(f32[6,12,12,1]{2,3,1,0:T(1,128)} %copy.346), channel_id=1, source_target_pairs={{0,1},{1,2},{2,3},{3,4},{4,5},{5,6},{6,7},{8,9},{9,10},{10,11},{11... | collective-permute-start | bytes 10376 | tf_op jit(solution)/shard_map/ppermute | solution.py:35
  85.3 1.3 %collective-permute-start.11 = (f32[6,12,12,1]{2,3,1,0:T(1,128)}, f32[6,12,12,1]{2,3,1,0:T(1,128)}, u32[]{:S(2)}, u32[]{:S(2)}) collective-permute-start(f32[6,12,12,1]{2,3,1,0:T(1,128)} %copy.347), channel_id=1, source_target_pairs={{1,0},{2,1},{3,2},{4,3},{5,4},{6,5},{7,6},{9,8},{10,9},{11,10},{12... | collective-permute-start | bytes 10376 | tf_op jit(solution)/shard_map/ppermute | solution.py:37
  87.9 1.3 %copy.348 = f32[6,12,12,1]{3,2,1,0:T(8,128)S(1)} copy(f32[6,12,12,1]{2,3,1,0:T(1,128)} %collective-permute-done.10) | data formatting | bytes 6912 | tf_op jit(solution)/shard_map/ppermute | solution.py:35
  89.2 1.9 %collective-permute-done.11 = f32[6,12,12,1]{2,3,1,0:T(1,128)} collective-permute-done((f32[6,12,12,1]{2,3,1,0:T(1,128)}, f32[6,12,12,1]{2,3,1,0:T(1,128)}, u32[]{:S(2)}, u32[]{:S(2)}) %collective-permute-start.11) | collective-permute-done | bytes 3488 | tf_op jit(solution)/shard_map/ppermute | solution.py:37
  91.1 1.3 %copy.349 = f32[6,12,12,1]{3,2,1,0:T(8,128)S(1)} copy(f32[6,12,12,1]{2,3,1,0:T(1,128)} %collective-permute-done.11) | data formatting | bytes 6912 | tf_op jit(solution)/shard_map/ppermute | solution.py:37
  98.5 1.3 %collective-permute-start.12 = (f32[28,64]{1,0:T(8,128)S(1)}, f32[28,64]{1,0:T(8,128)S(1)}, u32[]{:S(2)}, u32[]{:S(2)}) collective-permute-start(f32[28,64]{1,0:T(8,128)S(1)} %fusion.54), channel_id=1, source_target_pairs={{1,0},{2,1},{3,2},{4,3},{5,4},{6,5},{7,6},{9,8},{10,9},{11,10},{12... | collective-permute-start | bytes 21512 | tf_op jit(solution)/shard_map/ppermute | solution.py:47
  100.6 3.2 %collective-permute-done.12 = f32[28,64]{1,0:T(8,128)S(1)} collective-permute-done((f32[28,64]{1,0:T(8,128)S(1)}, f32[28,64]{1,0:T(8,128)S(1)}, u32[]{:S(2)}, u32[]{:S(2)}) %collective-permute-start.12) | collective-permute-done | bytes 7200 | tf_op jit(solution)/shard_map/ppermute | solution.py:47
  (217 shorter events, 37.9 us)
Async XLA Ops:
  0.6 22.2 %copy-start.3 = (f32[8,8,128]{2,1,0:T(8,128)S(1)}, f32[8,8,128]{2,1,0:T(8,128)}, u32[]{:S(2)}) copy-start(f32[8,8,128]{2,1,0:T(8,128)} %param.65) | copy-start | bytes 98308
  0.6 22.2 %copy-start = (f32[3,8,8,128]{3,2,1,0:T(8,128)S(1)}, f32[3,8,8,128]{3,2,1,0:T(8,128)}, u32[]{:S(2)}) copy-start(f32[3,8,8,128]{3,2,1,0:T(8,128)} %param.62) | copy-start | bytes 294916
  0.7 22.2 %copy-start.2 = (f32[3,8,8,128]{3,2,1,0:T(8,128)S(1)}, f32[3,8,8,128]{3,2,1,0:T(8,128)}, u32[]{:S(2)}) copy-start(f32[3,8,8,128]{3,2,1,0:T(8,128)} %param.63) | copy-start | bytes 294916
  0.7 22.2 %copy-start.1 = (f32[3,8,8,128]{3,2,1,0:T(8,128)S(1)}, f32[3,8,8,128]{3,2,1,0:T(8,128)}, u32[]{:S(2)}) copy-start(f32[3,8,8,128]{3,2,1,0:T(8,128)} %param.64) | copy-start | bytes 294916
  1.5 11.0 %collective-permute-start = (f32[10,1,8,128]{3,2,1,0:T(8,128)S(1)}, f32[10,1,8,128]{3,2,1,0:T(8,128)S(1)}, u32[]{:S(2)}, u32[]{:S(2)}) collective-permute-start(f32[10,1,8,128]{3,2,1,0:T(8,128)S(1)} %get-tuple-element.147), channel_id=1, source_target_pairs={{32,0},{64,32},{96,64},{33,1},{65,33},{97,65},{34,2},{66,34},{98,6... | collective-permute-start | bytes 122888 | tf_op jit(solution)/shard_map/ppermute | solution.py:37
  2.8 9.7 %collective-permute-start.1 = (f32[10,1,8,128]{3,2,1,0:T(8,128)S(1)}, f32[10,1,8,128]{3,2,1,0:T(8,128)S(1)}, u32[]{:S(2)}, u32[]{:S(2)}) collective-permute-start(f32[10,1,8,128]{3,2,1,0:T(8,128)S(1)} %get-tuple-element.146), channel_id=1, source_target_pairs={{0,32},{32,64},{64,96},{1,33},{33,65},{65,97},{2,34},{34,66},{66,9... | collective-permute-start | bytes 122888 | tf_op jit(solution)/shard_map/ppermute | solution.py:35
  13.8 7.9 %collective-permute-start.2 = (f32[10,10,1,128]{3,2,1,0:T(1,128)S(1)}, f32[10,10,1,128]{3,2,1,0:T(1,128)S(1)}, u32[]{:S(2)}, u32[]{:S(2)}) collective-permute-start(f32[10,10,1,128]{3,2,1,0:T(1,128)S(1)} %get-tuple-element.143), channel_id=1, source_target_pairs={{8,0},{16,8},{24,16},{9,1},{17,9},{25,17},{10,2},{18,10},{26,18},{... | collective-permute-start | bytes 153608 | tf_op jit(solution)/shard_map/ppermute | solution.py:37
  17.0 5.8 %collective-permute-start.3 = (f32[10,10,1,128]{3,2,1,0:T(1,128)S(1)}, f32[10,10,1,128]{3,2,1,0:T(1,128)S(1)}, u32[]{:S(2)}, u32[]{:S(2)}) collective-permute-start(f32[10,10,1,128]{3,2,1,0:T(1,128)S(1)} %get-tuple-element.142), channel_id=1, source_target_pairs={{0,8},{8,16},{16,24},{1,9},{9,17},{17,25},{2,10},{10,18},{18,26},{... | collective-permute-start | bytes 153608 | tf_op jit(solution)/shard_map/ppermute | solution.py:35
  24.0 7.9 %collective-permute-start.4 = (f32[10,10,10,1]{2,3,1,0:T(1,128)S(1)}, f32[10,10,10,1]{2,3,1,0:T(1,128)S(1)}, u32[]{:S(2)}, u32[]{:S(2)}) collective-permute-start(f32[10,10,10,1]{2,3,1,0:T(1,128)S(1)} %copy.361), channel_id=1, source_target_pairs={{1,0},{2,1},{3,2},{4,3},{5,4},{6,5},{7,6},{9,8},{10,9},{11,10},{12... | collective-permute-start | bytes 12008 | tf_op jit(solution)/shard_map/ppermute | solution.py:37
  26.0 6.6 %collective-permute-start.5 = (f32[10,10,10,1]{2,3,1,0:T(1,128)S(1)}, f32[10,10,10,1]{2,3,1,0:T(1,128)S(1)}, u32[]{:S(2)}, u32[]{:S(2)}) collective-permute-start(f32[10,10,10,1]{2,3,1,0:T(1,128)S(1)} %copy.362), channel_id=1, source_target_pairs={{0,1},{1,2},{2,3},{3,4},{4,5},{5,6},{6,7},{8,9},{9,10},{10,11},{11... | collective-permute-start | bytes 12008 | tf_op jit(solution)/shard_map/ppermute | solution.py:35
  43.0 2.2 %copy-start.25 = (f32[8,8,128]{2,1,0:T(8,128)}, f32[8,8,128]{2,1,0:T(8,128)S(1)}, u32[]{:S(2)}) copy-start(f32[8,8,128]{2,1,0:T(8,128)S(1)} %get-tuple-element.266) | copy-start | bytes 98308
  52.4 4.8 %collective-permute-start.6 = (f32[6,1,10,130]{3,2,1,0:T(8,128)S(1)}, f32[6,1,10,130]{3,2,1,0:T(8,128)S(1)}, u32[]{:S(2)}, u32[]{:S(2)}) collective-permute-start(f32[6,1,10,130]{3,2,1,0:T(8,128)S(1)} %get-tuple-element.128), channel_id=1, source_target_pairs={{0,32},{32,64},{64,96},{1,33},{33,65},{65,97},{2,34},{34,66},{66,9... | collective-permute-start | bytes 93608 | tf_op jit(solution)/shard_map/ppermute | solution.py:35
  55.6 5.4 %collective-permute-start.7 = (f32[6,1,10,130]{3,2,1,0:T(8,128)S(1)}, f32[6,1,10,130]{3,2,1,0:T(8,128)S(1)}, u32[]{:S(2)}, u32[]{:S(2)}) collective-permute-start(f32[6,1,10,130]{3,2,1,0:T(8,128)S(1)} %get-tuple-element.129), channel_id=1, source_target_pairs={{32,0},{64,32},{96,64},{33,1},{65,33},{97,65},{34,2},{66,34},{98,6... | collective-permute-start | bytes 93608 | tf_op jit(solution)/shard_map/ppermute | solution.py:37
  61.1 9.7 %collective-permute-start.8 = (f32[6,12,1,130]{3,2,1,0:T(1,128)S(1)}, f32[6,12,1,130]{3,2,1,0:T(1,128)S(1)}, u32[]{:S(2)}, u32[]{:S(2)}) collective-permute-start(f32[6,12,1,130]{3,2,1,0:T(1,128)S(1)} %get-tuple-element.126), channel_id=1, source_target_pairs={{0,8},{8,16},{16,24},{1,9},{9,17},{17,25},{2,10},{10,18},{18,26},{... | collective-permute-start | bytes 112328 | tf_op jit(solution)/shard_map/ppermute | solution.py:35
  68.9 7.2 %collective-permute-start.9 = (f32[6,12,1,130]{3,2,1,0:T(1,128)S(1)}, f32[6,12,1,130]{3,2,1,0:T(1,128)S(1)}, u32[]{:S(2)}, u32[]{:S(2)}) collective-permute-start(f32[6,12,1,130]{3,2,1,0:T(1,128)S(1)} %get-tuple-element.127), channel_id=1, source_target_pairs={{8,0},{16,8},{24,16},{9,1},{17,9},{25,17},{10,2},{18,10},{26,18},{... | collective-permute-start | bytes 112328 | tf_op jit(solution)/shard_map/ppermute | solution.py:37
  77.0 9.7 %copy-start.9 = (f32[8,8,128]{2,1,0:T(8,128)S(1)}, f32[8,8,128]{2,1,0:T(8,128)}, u32[]{:S(2)}) copy-start(f32[8,8,128]{2,1,0:T(8,128)} %copy-done.8) | copy-start | bytes 98308
  80.2 7.7 %collective-permute-start.10 = (f32[6,12,12,1]{2,3,1,0:T(1,128)}, f32[6,12,12,1]{2,3,1,0:T(1,128)}, u32[]{:S(2)}, u32[]{:S(2)}) collective-permute-start(f32[6,12,12,1]{2,3,1,0:T(1,128)} %copy.346), channel_id=1, source_target_pairs={{0,1},{1,2},{2,3},{3,4},{4,5},{5,6},{6,7},{8,9},{9,10},{10,11},{11... | collective-permute-start | bytes 10376 | tf_op jit(solution)/shard_map/ppermute | solution.py:35
  85.3 5.8 %collective-permute-start.11 = (f32[6,12,12,1]{2,3,1,0:T(1,128)}, f32[6,12,12,1]{2,3,1,0:T(1,128)}, u32[]{:S(2)}, u32[]{:S(2)}) collective-permute-start(f32[6,12,12,1]{2,3,1,0:T(1,128)} %copy.347), channel_id=1, source_target_pairs={{1,0},{2,1},{3,2},{4,3},{5,4},{6,5},{7,6},{9,8},{10,9},{11,10},{12... | collective-permute-start | bytes 10376 | tf_op jit(solution)/shard_map/ppermute | solution.py:37
  87.6 4.9 %copy-start.6 = (f32[6,12,1,130]{3,2,1,0:T(1,128)S(1)}, f32[6,12,1,130]{3,2,1,0:T(1,128)}, u32[]{:S(2)}) copy-start(f32[6,12,1,130]{3,2,1,0:T(1,128)} %copy-done.5) | copy-start | bytes 112324
  94.6 1.2 %copy-start.20 = (f32[3,8,8,128]{3,2,1,0:T(8,128)S(1)}, f32[3,8,8,128]{3,2,1,0:T(8,128)}, u32[]{:S(2)}) copy-start(f32[3,8,8,128]{3,2,1,0:T(8,128)} %get-tuple-element.294) | copy-start | bytes 294916
  94.7 1.2 %copy-start.21 = (f32[3,8,8,128]{3,2,1,0:T(8,128)S(1)}, f32[3,8,8,128]{3,2,1,0:T(8,128)}, u32[]{:S(2)}) copy-start(f32[3,8,8,128]{3,2,1,0:T(8,128)} %get-tuple-element.255) | copy-start | bytes 294916
  94.7 1.2 %copy-start.22 = (f32[3,8,8,128]{3,2,1,0:T(8,128)S(1)}, f32[3,8,8,128]{3,2,1,0:T(8,128)}, u32[]{:S(2)}) copy-start(f32[3,8,8,128]{3,2,1,0:T(8,128)} %get-tuple-element.296) | copy-start | bytes 294916
  95.9 1.6 %copy-start.23 = (f32[3,8,8,2]{3,2,1,0:T(8,128)S(1)}, f32[3,8,8,2]{3,2,1,0:T(8,128)}, u32[]{:S(2)}) copy-start(f32[3,8,8,2]{3,2,1,0:T(8,128)} %copy.356) | copy-start | bytes 4612
  98.5 5.4 %collective-permute-start.12 = (f32[28,64]{1,0:T(8,128)S(1)}, f32[28,64]{1,0:T(8,128)S(1)}, u32[]{:S(2)}, u32[]{:S(2)}) collective-permute-start(f32[28,64]{1,0:T(8,128)S(1)} %fusion.54), channel_id=1, source_target_pairs={{1,0},{2,1},{3,2},{4,3},{5,4},{6,5},{7,6},{9,8},{10,9},{11,10},{12... | collective-permute-start | bytes 21512 | tf_op jit(solution)/shard_map/ppermute | solution.py:47
  (27 other events, 23.3 us)
where the time goes:
time: 106 us; the launch traced here: 104 us
  starting transfers between devices  39.8 us (38%)
  other arithmetic  30.3 us (29%)
  local copies, waits for them, and re-layouts  17 us (16%)
  waiting for transfers between devices  15.5 us (15%)
  between operations  1.69 us (2%)
    ppermute x6, starting transfers between devices, padded_2(): lax.ppermute(tail, axis, [(i, (i + 1) % count) for i in range(ends)])  28.2 us
    ppermute x6, waiting for transfers between devices, padded_2(): lax.ppermute(head, axis, [((i + 1) % count, i) for i in range(ends)])  10.9 us
    ppermute x6, starting transfers between devices, padded_2(): lax.ppermute(head, axis, [((i + 1) % count, i) for i in range(ends)])  10.3 us
    concatenate x5, other arithmetic, padded_2(): jnp.concatenate([lax.ppermute(tail, axis, [(i, (i + 1) % count) for i in...  4.87 us
    unnamed x79, local copies, waits for them, and re-layouts  4.59 us
    neg x6, other arithmetic, contact_terms(): -pair_force  3.99 us
    broadcast_in_dim x4, other arithmetic, contact_terms(): jnp.where(slot_live[None], jnp.concatenate([pair_force, torque_center], 0...  3.56 us
    slice x3, local copies, waits for them, and re-layouts, padded_2(): lax.slice_in_dim(cells, cells.shape[dim] - width, cells.shape[dim], axis=...  3.25 us
  transfers between devices with their start and end apart: 13, of which 6 were waited for; matrix products, arithmetic and copies ran while one was open for 12% of the time, Pallas kernels for 0%

commit v1 on v0

v1 whole, which is shorter than its diff:
```python
import functools

import jax
import jax.numpy as jnp
from jax import lax
from jax.experimental import pallas as pl
from jax.experimental.pallas import tpu as pltpu
from jax.sharding import PartitionSpec as P

MESH = pl.DeviceIdType.MESH
AXES = ("gx", "gy", "gz")
DIRS = (
    (1, 0, 0),
    (0, 1, 0),
    (0, 0, 1),
    (1, 1, 0),
    (1, -1, 0),
    (1, 0, 1),
    (1, 0, -1),
    (0, 1, 1),
    (0, 1, -1),
)
SLOTS = 6
FIELDS = 10
SHEAR = FIELDS
CODES = FIELDS + 3 * SLOTS
FULL = CODES + SLOTS
PACKS = (FULL * 8 + 127) // 128
STEP = 0.05
TINY = 1e-30

ROWS = 24
HEIGHT = 10 * ROWS

PACK_FROM = (
    (0, 0, -1),
    (0, 0, 1),
    (-1, 0, -1),
    (-1, 0, 1),
    (1, 0, -1),
    (1, 0, 1),
    (0, -1, -1),
    (0, -1, 1),
    (0, 1, -1),
    (0, 1, 1),
)
FLAT_FROM = (
    (-1, 0, 0),
    (1, 0, 0),
    (0, -1, 0),
    (0, 1, 0),
    (-1, -1, 0),
    (-1, 1, 0),
    (1, -1, 0),
    (1, 1, 0),
)
SENDERS = FLAT_FROM + PACK_FROM


def plane(x):
    return (x + 1) * ROWS + 8


def halo_kernel(
    off_hbm, vel_hbm, spin_hbm, rad_hbm, hist_hbm, con_hbm,
    xlo, xhi, ylo, yhi, edges, packs, own_packs,
    cells, codes, yrows, rows, local_sems, send_sems, recv_sems,
):
    here = [lax.axis_index(a) for a in AXES]
    size = [lax.axis_size(a) for a in AXES]

    def exists(step):
        ok = None
        for at, n, s in zip(here, size, step):
            if s == 0:
                continue
            test = at + s < n if s > 0 else at + s >= 0
            ok = test if ok is None else jnp.logical_and(ok, test)
        return ok

    def place(step):
        return tuple(at + s for at, s in zip(here, step))

    loads = [
        pltpu.make_async_copy(off_hbm, cells.at[0:3], local_sems.at[0]),
        pltpu.make_async_copy(vel_hbm, cells.at[3:6], local_sems.at[1]),
        pltpu.make_async_copy(spin_hbm, cells.at[6:9], local_sems.at[2]),
        pltpu.make_async_copy(rad_hbm, cells.at[9:10], local_sems.at[3]),
        pltpu.make_async_copy(hist_hbm, cells.at[SHEAR:CODES], local_sems.at[4]),
        pltpu.make_async_copy(con_hbm, codes, local_sems.at[5]),
    ]
    for load in loads:
        load.start()
    barrier = pltpu.get_barrier_semaphore()
    expected = jnp.int32(0)
    for step in SENDERS:
        there = exists(step)
        expected = expected + there.astype(jnp.int32)

        @pl.when(there)
        def _():
            pl.semaphore_signal(barrier, inc=1, device_id=place(step), device_id_type=MESH)

    for load in loads:
        load.wait()
    for s in range(SLOTS):
        cells[CODES + s] = codes[s].astype(jnp.float32)
    lane = lax.broadcasted_iota(jnp.int32, (8, 128), 1)
    for k in range(PACKS):
        low = jnp.zeros((8, 128), jnp.float32)
        top = jnp.zeros((8, 128), jnp.float32)
        for c in range(k * 16, min(FULL, k * 16 + 16)):
            for x in range(8):
                p = (c % 16) * 8 + x
                value = cells[c, x * 8 : x * 8 + 8, :]
                if p:
                    value = pltpu.roll(value, p, 1)
                low = jnp.where(lane == p, value, low)
                top = jnp.where(lane == (p - 1) % 128, value, top)
        own_packs[0, k] = low
        own_packs[1, k] = top
    for c in range(FULL):
        yrows[0, c] = cells[c, pl.ds(0, 8, stride=8), :]
        yrows[1, c] = cells[c, pl.ds(7, 8, stride=8), :]
    for which, row in enumerate((63, 56, 7, 0)):
        for c in range(FULL if which < 2 else FIELDS):
            rows[which, c : c + 1, :] = cells[c, row : row + 1, :]

    targets = [xlo, xhi, ylo, yhi] + [edges.at[k] for k in range(4)] + [
        packs.at[k] for k in range(len(PACK_FROM))
    ]
    sources = (
        [cells.at[:, 56:64, :], cells.at[0:FIELDS, 0:8, :], yrows.at[1], yrows.at[0]]
        + [rows.at[k] for k in range(4)]
        + [own_packs.at[0 if s[2] > 0 else 1] for s in PACK_FROM]
    )

    def copy(k):
        to = tuple(-s for s in SENDERS[k])
        return pltpu.make_async_remote_copy(
            src_ref=sources[k],
            dst_ref=targets[k],
            send_sem=send_sems.at[k],
            recv_sem=recv_sems.at[k],
            device_id=place(to),
            device_id_type=MESH,
        )

    for k, step in enumerate(SENDERS):

        @pl.when(jnp.logical_not(exists(step)))
        def _():
            targets[k][...] = jnp.zeros(targets[k].shape, jnp.float32)

    pl.semaphore_wait(barrier, expected)
    for k, step in enumerate(SENDERS):

        @pl.when(exists(tuple(-s for s in step)))
        def _():
            copy(k).start()

    for k, step in enumerate(SENDERS):

        @pl.when(exists(step))
        def _():
            copy(k).wait_recv()

        @pl.when(exists(tuple(-s for s in step)))
        def _():
            copy(k).wait_send()


def cross(a, b):
    return [
        a[1] * b[2] - a[2] * b[1],
        a[2] * b[0] - a[0] * b[2],
        a[0] * b[1] - a[1] * b[0],
    ]


def dot3(a, b):
    return a[0] * b[0] + a[1] * b[1] + a[2] * b[2]


def pair(first, second, direction, shear, live):
    sep = []
    for k in range(3):
        gap = second[k] - first[k]
        sep.append(gap + float(direction[k]) if direction[k] else gap)
    square = dot3(sep, sep)
    inverse = lax.rsqrt(square)
    normal = [s * inverse for s in sep]
    radii = first[9] + second[9]
    overlap = jnp.maximum(radii - square * inverse, 0.0)
    product = first[9] * second[9] * overlap
    contact = product * lax.rsqrt(jnp.maximum(product * radii, TINY))
    contact = jnp.where(live, contact, 0.0)
    surface = cross([first[6 + k] + second[6 + k] for k in range(3)], normal)
    relative = [second[3 + k] - first[3 + k] - surface[k] for k in range(3)]
    approach = dot3(relative, normal)
    sliding = [relative[k] - approach * normal[k] for k in range(3)]
    repulsion = contact * jnp.maximum(10.0 * overlap - 2.0 * approach, 0.0)
    along = dot3(shear, normal)
    spring = [shear[k] - along * normal[k] + STEP * sliding[k] for k in range(3)]
    pull = [8.0 * spring[k] + 1.5 * sliding[k] for k in range(3)]
    size = contact * contact * dot3(pull, pull)
    factor = jnp.minimum(1.0, 0.4 * repulsion * lax.rsqrt(jnp.maximum(size, 0.0025)))
    scale = factor * contact
    tangent = [scale * pull[k] for k in range(3)]
    force = [tangent[k] - repulsion * normal[k] for k in range(3)]
    return force, cross(normal, tangent), [factor * spring[k] for k in range(3)]


def pick_shear(load, code, number):
    masks = [code(s) == number for s in range(SLOTS)]
    live = masks[0]
    shear = [jnp.where(masks[0], load(k), 0.0) for k in range(3)]
    for s in range(1, SLOTS):
        live = jnp.logical_or(live, masks[s])
        shear = [jnp.where(masks[s], load(3 * s + k), shear[k]) for k in range(3)]
    return shear, live, masks


def compute_kernel(
    off, vel, spin, rad, hist, con, leaving, xlo, xhi, ylo, yhi, edges, packs, own_packs,
    new_off, new_vel, new_spin, new_hist, outbox,
    pad, pad_up, pad_down, level, rising, falling, side, zside,
):
    lane = lax.broadcasted_iota(jnp.int32, (8, 128), 1)
    sub = lax.broadcasted_iota(jnp.int32, (8, 128), 0)
    zero = jnp.zeros((8, 128), jnp.float32)

    def scaled(values):
        return values[:6] + [v * values[9] for v in values[6:9]] + [values[9]]

    for x in range(8):
        rows = pl.ds(plane(x), 8)
        here = slice(x * 8, x * 8 + 8)
        values = [off[k, here] for k in range(3)] + [vel[k, here] for k in range(3)]
        values += [spin[k, here] for k in range(3)] + [rad[0, here]]
        for c, v in enumerate(scaled(values)):
            pad[c, rows, :] = v
    for source, first in ((ylo, plane(0) - 1), (yhi, plane(0) + 8)):
        for c, v in enumerate(scaled([source[c] for c in range(FIELDS)])):
            pad[c, pl.ds(first, 8, stride=ROWS), :] = v
    for c, v in enumerate(scaled([xhi[c] for c in range(FIELDS)])):
        pad[c, pl.ds(plane(8), 8), :] = v
    for which, row in ((2, plane(8) - 1), (3, plane(8) + 8)):
        for c, v in enumerate(scaled([edges[which, c : c + 1, :] for c in range(FIELDS)])):
            pad[c, row : row + 1, :] = v

    def first_pack(pack):
        shift = [pltpu.roll(pack, 128 - 8 * (9 - c), 1) for c in (6, 7, 8)]
        group = lane // 8
        return jnp.where(
            group == 6, pack * shift[0],
            jnp.where(group == 7, pack * shift[1], jnp.where(group == 8, pack * shift[2], pack)),
        )

    def first_top(pack):
        shift = [pltpu.roll(pack, 128 - 8 * (9 - c), 1) for c in (6, 7, 8)]
        group = (lane + 1) // 8
        return jnp.where(
            group == 6, pack * shift[0],
            jnp.where(group == 7, pack * shift[1], jnp.where(group == 8, pack * shift[2], pack)),
        )

    above = [first_pack(packs[k, 0]) for k in (1, 5, 9)]
    below = [first_top(packs[k, 0]) for k in (0, 4, 8)]
    for c in range(FIELDS):
        for x in range(9):
            for tile in range(2 if x < 8 else 1):
                which = 1 if x == 8 else 2 * tile
                p = c * 8 + x % 8
                rows = pl.ds(plane(x) + 8 * tile, 8)
                value = pad[c, rows, :]
                up = pltpu.roll(value, 127, 1)
                pad_up[c, rows, :] = jnp.where(
                    lane == 127, pltpu.roll(above[which], 127 - p, 1), up
                )
                down = pltpu.roll(value, 1, 1)
                pad_down[c, rows, :] = jnp.where(
                    lane == 0, pltpu.roll(below[which], (129 - p) % 128, 1), down
                )

    for total in (level, rising, falling):
        for c in range(6):
            for x in range(9):
                total[c, pl.ds(plane(x), 8), :] = zero
                total[c, pl.ds(plane(x) - 8, 8), :] = zero
                total[c, pl.ds(plane(x) + 8, 8), :] = zero

    def add(total, rows, force, twist, sign):
        for k in range(3):
            total[k, rows, :] = total[k, rows, :] + (force[k] if sign > 0 else -force[k])
            total[3 + k, rows, :] = total[3 + k, rows, :] + twist[k]

    def body(x, carry):
        base = pl.multiple_of((x + 1) * ROWS + 8, 8)
        here = pl.ds(pl.multiple_of(x * 8, 8), 8)
        first = [pad[c, pl.ds(base, 8), :] for c in range(FIELDS)]
        forces = [zero] * 3
        twists = [zero] * 3
        springs = [zero] * (3 * SLOTS)
        for number, (dx, dy, dz) in enumerate(DIRS):
            rows = pl.ds(base + dx * ROWS + dy, 8)
            source = (pad, pad_up, pad_down)[dz]
            total = (level, rising, falling)[dz]
            second = [source[c, rows, :] for c in range(FIELDS)]
            shear, live, masks = pick_shear(
                lambda c: hist[c, here, :], lambda s: con[s, here, :], number
            )
            force, twist, spring = pair(first, second, (dx, dy, dz), shear, live)
            for k in range(3):
                forces[k] = forces[k] + force[k]
                twists[k] = twists[k] + twist[k]
                for s in range(SLOTS):
                    springs[3 * s + k] = jnp.where(masks[s], spring[k], springs[3 * s + k])
            add(total, rows, force, twist, -1)
        add(level, pl.ds(base, 8), forces, twists, 1)
        for c in range(3 * SLOTS):
            new_hist[c, here, :] = springs[c]
        return carry

    lax.fori_loop(0, 8, body, 0)

    def shifted(values, amount):
        return [pltpu.roll(v, amount, 1) for v in values]

    def outer(rows, load, number, second, dead=None, turn=0):
        first = scaled([load(c, rows) for c in range(FIELDS)])
        shear, live, _ = pick_shear(
            lambda c: load(SHEAR + c, rows), lambda s: load(CODES + s, rows), float(number)
        )
        if turn:
            alive = jnp.where(live, 1.0, 0.0)
            moved = shifted(first + shear + [alive], turn)
            first, shear, live = moved[:10], moved[10:13], moved[13] > 0.5
        if dead is not None:
            live = jnp.logical_and(live, jnp.logical_not(dead))
        force, twist, _ = pair(first, second, DIRS[number], shear, live)
        return force, twist

    def load_side(c, rows):
        return side[c, rows, :]

    for c in range(FULL):
        side[c, 8:16, :] = xlo[c]
        side[c, 7:8, :] = edges[0, c : c + 1, :]
        side[c, 16:17, :] = edges[1, c : c + 1, :]
    mine = pl.ds(plane(0), 8)
    second = [pad[c, mine, :] for c in range(FIELDS)]
    for number in (0, 3, 4, 5, 6):
        dx, dy, dz = DIRS[number]
        dead = None if dz == 0 else lane == (0 if dz > 0 else 127)
        force, twist = outer(
            pl.ds(8 - dy, 8), load_side, number, second, dead, (0, 1, 127)[dz]
        )
        add(level, mine, force, twist, -1)
    for c in range(FULL):
        side[c, 8:16, :] = ylo[c]
    mine = pl.ds(plane(0), 8, stride=ROWS)
    second = [pad[c, mine, :] for c in range(FIELDS)]
    for number in (1, 3, 7, 8):
        dx, dy, dz = DIRS[number]
        dead = sub == 0 if dx else (None if dz == 0 else lane == (0 if dz > 0 else 127))
        force, twist = outer(
            pl.ds(8 - dx, 8), load_side, number, second, dead, (0, 1, 127)[dz]
        )
        add(level, mine, force, twist, -1)
    for c in range(FULL):
        side[c, 8:16, :] = yhi[c]
    mine = pl.ds(plane(0) + 7, 8, stride=ROWS)
    second = [pad[c, mine, :] for c in range(FIELDS)]
    force, twist = outer(pl.ds(7, 8), load_side, 4, second, sub == 0)
    add(level, mine, force, twist, -1)

    def spread(pack, c, top):
        p = (c % 16) * 8 - top
        return pltpu.roll(pack, (128 - p) % 128, 1) if p % 128 else pack

    for end in range(2):
        top = 1 - end
        for k in range(PACKS):
            straight, behind, left = packs[end, k], packs[2 + end, k], packs[6 + end, k]
            for c in range(16 * k, min(FULL, 16 * k + 16)):
                before = pltpu.roll(spread(behind, c, top), 120, 1)
                zside[end, c, 8:16, :] = jnp.where(
                    lane == 127, before, spread(straight, c, top)
                )
                zside[end, c, 0:8, :] = spread(left, c, top)

    for end, numbers in ((0, (2, 5, 7)), (1, (6, 8))):
        mine = own_packs[end, 0]
        second = scaled([spread(mine, c, end) for c in range(FIELDS)])
        forces = [zero] * 3
        twists = [zero] * 3
        for number in numbers:
            dx, dy, dz = DIRS[number]
            force, twist = outer(
                pl.ds(8 - dy, 8), lambda c, rows: zside[end, c, rows, :], number, second,
                None, dx,
            )
            forces = [forces[k] + force[k] for k in range(3)]
            twists = [twists[k] + twist[k] for k in range(3)]
        edge = 127 * end
        for x in range(8):
            turn = (edge - x) % 128
            rows = pl.ds(plane(x), 8)
            hold = lane == edge
            add(
                level, rows,
                [jnp.where(hold, pltpu.roll(v, turn, 1) if turn else v, 0.0) for v in forces],
                [jnp.where(hold, pltpu.roll(v, turn, 1) if turn else v, 0.0) for v in twists],
                -1,
            )

    names = leaving[...]
    wide = jnp.broadcast_to(names, (8, 64))
    deep = lax.broadcasted_iota(jnp.int32, (8, 64), 0)
    starts = [(lax.axis_index(a) * n).astype(jnp.float32) for a, n in zip(AXES, (8, 8, 128))]
    boxes = [jnp.zeros((8, 64), jnp.float32) for _ in range(28)]
    for x in range(8):
        rows = pl.ds(plane(x), 8)
        here = slice(x * 8, x * 8 + 8)
        sums = []
        for c in range(6):
            up = jnp.where(lane == 0, 0.0, pltpu.roll(rising[c, rows, :], 1, 1))
            down = jnp.where(lane == 127, 0.0, pltpu.roll(falling[c, rows, :], 127, 1))
            sums.append(level[c, rows, :] + up + down)
        radius = rad[0, here, :]
        inverse = 1.0 / radius
        push = STEP * inverse * inverse * inverse
        turn = 0.125 * (inverse * inverse) * (inverse * inverse)
        velocity = [vel[k, here, :] + push * sums[k] for k in range(3)]
        velocity[2] = velocity[2] - STEP
        offset = [off[k, here, :] + STEP * velocity[k] for k in range(3)]
        rotation = [spin[k, here, :] + turn * sums[3 + k] for k in range(3)]
        springs = [new_hist[c, here, :] for c in range(3 * SLOTS)]
        bottom = [wide == (x * 8 + deep) * 128 + z for z in range(2)]
        left = [
            jnp.max(jnp.where(b, 1.0, 0.0), axis=1, keepdims=True) for b in bottom
        ]
        staying = 1.0 - jnp.where(lane == 0, left[0], jnp.where(lane == 1, left[1], 0.0))
        lanes = lane.astype(jnp.float32)
        position = [
            offset[0] + (starts[0] + float(x)),
            offset[1] + (starts[1] + sub.astype(jnp.float32)),
            offset[2] + (starts[2] + lanes),
        ]
        for c, v in enumerate(position + velocity + rotation + [radius] + springs):
            for z in range(2):
                value = jnp.broadcast_to(v[:, z : z + 1], (8, 64))
                boxes[c] = boxes[c] + jnp.where(bottom[z], value, 0.0)
        for k in range(3):
            new_off[k, here, :] = offset[k] * staying
            new_vel[k, here, :] = velocity[k] * staying
            new_spin[k, here, :] = rotation[k] * staying
        for c in range(3 * SLOTS):
            new_hist[c, here, :] = springs[c] * staying
    for c in range(28):
        outbox[c : c + 1, :] = jnp.sum(boxes[c], axis=0, keepdims=True)


def on_device(offset, velocity, spin, radius, history, contacts, leaving):
    f32 = jnp.float32
    off = offset.reshape(3, 64, 128)
    vel = velocity.reshape(3, 64, 128)
    spn = spin.reshape(3, 64, 128)
    rad = radius.reshape(1, 64, 128)
    hist = history.reshape(3 * SLOTS, 64, 128)
    con = contacts.reshape(SLOTS, 64, 128)
    vmem = pl.BlockSpec(memory_space=pltpu.VMEM)
    anywhere = pl.BlockSpec(memory_space=pl.ANY)
    halo_shapes = (
        (FULL, 8, 128),
        (FIELDS, 8, 128),
        (FULL, 8, 128),
        (FULL, 8, 128),
        (4, 40, 128),
        (len(PACK_FROM), PACKS, 8, 128),
        (2, PACKS, 8, 128),
    )
    halos = pl.pallas_call(
        halo_kernel,
        out_shape=[jax.ShapeDtypeStruct(s, f32) for s in halo_shapes],
        in_specs=[anywhere] * 6,
        out_specs=[vmem] * len(halo_shapes),
        scratch_shapes=[
            pltpu.VMEM((FULL, 64, 128), f32),
            pltpu.VMEM((SLOTS, 64, 128), jnp.int32),
            pltpu.VMEM((2, FULL, 8, 128), f32),
            pltpu.VMEM((4, 40, 128), f32),
            pltpu.SemaphoreType.DMA((6,)),
            pltpu.SemaphoreType.DMA((len(SENDERS),)),
            pltpu.SemaphoreType.DMA((len(SENDERS),)),
        ],
        compiler_params=pltpu.CompilerParams(collective_id=0, has_side_effects=True),
        name="halo",
    )(off, vel, spn, rad, hist, con)
    state = jax.ShapeDtypeStruct((3, 64, 128), f32)
    new_off, new_vel, new_spin, new_hist, outbox = pl.pallas_call(
        compute_kernel,
        out_shape=[
            state, state, state,
            jax.ShapeDtypeStruct((3 * SLOTS, 64, 128), f32),
            jax.ShapeDtypeStruct((28, 64), f32),
        ],
        in_specs=[vmem] * 14,
        out_specs=[vmem] * 5,
        scratch_shapes=[
            pltpu.VMEM((FIELDS, HEIGHT, 128), f32),
            pltpu.VMEM((FIELDS, HEIGHT, 128), f32),
            pltpu.VMEM((FIELDS, HEIGHT, 128), f32),
            pltpu.VMEM((6, HEIGHT, 128), f32),
            pltpu.VMEM((6, HEIGHT, 128), f32),
            pltpu.VMEM((6, HEIGHT, 128), f32),
            pltpu.VMEM((FULL, ROWS, 128), f32),
            pltpu.VMEM((2, FULL, ROWS, 128), f32),
        ],
        name="pairs",
    )(off, vel, spn, rad, hist, con, leaving.reshape(1, 64), *halos)
    count = lax.axis_size("gz")
    arrivals = lax.ppermute(outbox, "gz", [(i + 1, i) for i in range(count - 1)])
    return (
        new_off.reshape(3, 8, 8, 128),
        new_vel.reshape(3, 8, 8, 128),
        new_spin.reshape(3, 8, 8, 128),
        new_hist.reshape(SLOTS, 3, 8, 8, 128),
        arrivals.reshape(28, 1, 1, 1, 64),
    )


def solution(mesh):
    placed = (
        P(None, "gx", "gy", "gz"),
        P(None, "gx", "gy", "gz"),
        P(None, "gx", "gy", "gz"),
        P("gx", "gy", "gz"),
        P(None, None, "gx", "gy", "gz"),
        P(None, "gx", "gy", "gz"),
        P("gx", "gy", "gz", None),
    )
    return jax.shard_map(
        on_device,
        mesh=mesh,
        in_specs=placed,
        out_specs=(
            P(None, "gx", "gy", "gz"),
            P(None, "gx", "gy", "gz"),
            P(None, "gx", "gy", "gz"),
            P(None, None, "gx", "gy", "gz"),
            P(None, "gx", "gy", "gz", None),
        ),
        check_vma=False,
    )
```

time: 106 us -> 26.7 us (0.25)
  the two profiles are of different devices: /device:TPU:1 before, /device:TPU:10 now
where the time goes in v1:
time: 26.7 us; the launch traced here: 26.5 us
  Pallas kernels  18.5 us (69%)
  waiting for transfers between devices  4.68 us (18%)
  starting transfers between devices  2.04 us (8%)
  between operations  0.65 us (2%)
  local copies, waits for them, and re-layouts  0.62 us (2%)
    pallas_call x1, Pallas kernels, on_device(): pl.pallas_call(halo_kernel, out_shape=[jax.ShapeDtypeStruct(s, f32) for s...  11.4 us
    pallas_call x1, Pallas kernels, on_device(): pl.pallas_call(compute_kernel, out_shape=[state, state, state, jax.ShapeD...  7.11 us
    ppermute x1, waiting for transfers between devices, on_device(): lax.ppermute(outbox, 'gz', [(i + 1, i) for i in range(count - 1)])  4.68 us
    ppermute x1, starting transfers between devices, on_device(): lax.ppermute(outbox, 'gz', [(i + 1, i) for i in range(count - 1)])  2.04 us
    unnamed x1, local copies, waits for them, and re-layouts  0.62 us
  transfers between devices with their start and end apart: 1, of which 1 were waited for; matrix products, arithmetic and copies ran while one was open for 0% of the time, Pallas kernels for 0%

profile of v1, /device:TPU:10, one launch (start us, length us, event | category | flops | bytes accessed | tf_op | source)
XLA Modules:
  0.0 26.5 jit_solution(11511276407254660322)
XLA Ops:
  0.6 11.4 %halo.1 = (f32[34,8,128]{2,1,0:T(8,128)}, f32[10,8,128]{2,1,0:T(8,128)}, f32[34,8,128]{2,1,0:T(8,128)}, f32[34,8,128]{2,1,0:T(8,128)}, f32[4,40,128]{2,1,0:T(8,1...) custom-call(f32[3,64,128]{2,1,0:T(8,128)} %bitcast.16, f32[3,64,128]{2,1,0:T(8,128)} %bitcast.18, ...), custom_call_target="tpu_custom_call" | custom-call | tf_op jit(solution)/shard_map/halo/pallas_call | solution.py:484
  12.0 7.1 %pairs.1 = (f32[3,64,128]{2,1,0:T(8,128)}, f32[3,64,128]{2,1,0:T(8,128)}, f32[3,64,128]{2,1,0:T(8,128)}, f32[18,64,128]{2,1,0:T(8,128)}, f32[28,64]{1,0:T(8,128)}) custom-call(f32[3,64,128]{2,1,0:T(8,128)} %bitcast.17, f32[3,64,128]{2,1,0:T(8,128)} %bitcast.19, f32[3,64,128]{2,1,0:T(8,128)} %bitcast.21, f32[1,64,128]{2,1,0:T(8,128)} %bitcast.23, ...), custom_call_target="tpu_custom_call" | custom-call | tf_op jit(solution)/shard_map/pairs/pallas_call | solution.py:502
  19.2 2.0 %collective-permute-start = (f32[28,64]{1,0:T(8,128)}, f32[28,64]{1,0:T(8,128)S(1)}, u32[]{:S(2)}, u32[]{:S(2)}) collective-permute-start(f32[28,64]{1,0:T(8,128)} %get-tuple-element.28), channel_id=1, source_target_pairs={{1,0},{2,1},{3,2},{4,3},{5,4},{6,5},{7,6},{9,8},{10,9},{11,10},{12... | collective-permute-start | bytes 21512 | tf_op jit(solution)/shard_map/ppermute | solution.py:524
  21.2 4.7 %collective-permute-done = f32[28,64]{1,0:T(8,128)S(1)} collective-permute-done((f32[28,64]{1,0:T(8,128)}, f32[28,64]{1,0:T(8,128)S(1)}, u32[]{:S(2)}, u32[]{:S(2)}) %collective-permute-start) | collective-permute-done | bytes 7200 | tf_op jit(solution)/shard_map/ppermute | solution.py:524
  25.9 0.6 %copy.12 = f32[28,1,1,1,64]{4,3,2,1,0:T(1,128)} copy(f32[28,1,1,1,64]{4,0,3,2,1:T(8,128)S(1)} %bitcast.24) | data formatting | bytes 14336
Async XLA Ops:
  19.2 6.7 %collective-permute-start = (f32[28,64]{1,0:T(8,128)}, f32[28,64]{1,0:T(8,128)S(1)}, u32[]{:S(2)}, u32[]{:S(2)}) collective-permute-start(f32[28,64]{1,0:T(8,128)} %get-tuple-element.28), channel_id=1, source_target_pairs={{1,0},{2,1},{3,2},{4,3},{5,4},{6,5},{7,6},{9,8},{10,9},{11,10},{12... | collective-permute-start | bytes 21512 | tf_op jit(solution)/shard_map/ppermute | solution.py:524

commit v2 on v1

--- a/solution.py
+++ b/solution.py
@@ -1,5 +1,3 @@
-import functools
-
 import jax
 import jax.numpy as jnp
 from jax import lax
@@ -61,10 +59,12 @@
     return (x + 1) * ROWS + 8
 
 
-def halo_kernel(
-    off_hbm, vel_hbm, spin_hbm, rad_hbm, hist_hbm, con_hbm,
-    xlo, xhi, ylo, yhi, edges, packs, own_packs,
-    cells, codes, yrows, rows, local_sems, send_sems, recv_sems,
+def step_kernel(
+    off_hbm, vel_hbm, spin_hbm, rad_hbm, hist_hbm, con_hbm, leaving_hbm,
+    state, arrivals,
+    xlo, xhi, ylo, yhi, edges, packs, own_packs, cells, codes, leaving, yrows, rows, outbox,
+    pad, pad_up, pad_down, level, rising, falling, side, zside,
+    local_sems, send_sems, recv_sems,
 ):
     here = [lax.axis_index(a) for a in AXES]
     size = [lax.axis_size(a) for a in AXES]
@@ -88,6 +88,7 @@
         pltpu.make_async_copy(rad_hbm, cells.at[9:10], local_sems.at[3]),
         pltpu.make_async_copy(hist_hbm, cells.at[SHEAR:CODES], local_sems.at[4]),
         pltpu.make_async_copy(con_hbm, codes, local_sems.at[5]),
+        pltpu.make_async_copy(leaving_hbm, leaving, local_sems.at[6]),
     ]
     for load in loads:
         load.start()
@@ -168,6 +169,54 @@
         @pl.when(exists(tuple(-s for s in step)))
         def _():
             copy(k).wait_send()
+
+    compute(
+        cells.at[0:3], cells.at[3:6], cells.at[6:9], cells.at[9:10], cells.at[SHEAR:CODES],
+        codes, leaving, xlo, xhi, ylo, yhi, edges, packs, own_packs,
+        state.at[0:3], state.at[3:6], state.at[6:9], state.at[9:27], outbox,
+        pad, pad_up, pad_down, level, rising, falling, side, zside,
+    )
+
+    last = len(SENDERS)
+    fall = pltpu.make_async_remote_copy(
+        src_ref=outbox,
+        dst_ref=arrivals,
+        send_sem=send_sems.at[last],
+        recv_sem=recv_sems.at[last],
+        device_id=place((0, 0, -1)),
+        device_id_type=MESH,
+    )
+
+    @pl.when(exists((0, 0, -1)))
+    def _():
+        fall.start()
+
+    @pl.when(exists((0, 0, 1)))
+    def _():
+        fall.wait_recv()
+
+    @pl.when(jnp.logical_not(exists((0, 0, 1))))
+    def _():
+        arrivals[...] = jnp.zeros(arrivals.shape, jnp.float32)
+
+    @pl.when(exists((0, 0, -1)))
+    def _():
+        fall.wait_send()
+
+
+def write_kernel(state, arrivals, new_off, new_vel, new_spin, new_hist, entered, sems):
+    copies = [
+        pltpu.make_async_copy(state.at[9:27], new_hist, sems.at[0]),
+        pltpu.make_async_copy(state.at[0:3], new_off, sems.at[1]),
+        pltpu.make_async_copy(state.at[3:6], new_vel, sems.at[2]),
+        pltpu.make_async_copy(state.at[6:9], new_spin, sems.at[3]),
+    ]
+    for copy in copies:
+        copy.start()
+    for c in range(28):
+        entered[c] = arrivals[c : c + 1, 0:64]
+    for copy in copies:
+        copy.wait()
 
 
 def cross(a, b):
@@ -221,7 +270,7 @@
     return shear, live, masks
 
 
-def compute_kernel(
+def compute(
     off, vel, spin, rad, hist, con, leaving, xlo, xhi, ylo, yhi, edges, packs, own_packs,
     new_off, new_vel, new_spin, new_hist, outbox,
     pad, pad_up, pad_down, level, rising, falling, side, zside,
@@ -415,7 +464,7 @@
                 -1,
             )
 
-    names = leaving[...]
+    names = leaving[0:1, 0:64]
     wide = jnp.broadcast_to(names, (8, 64))
     deep = lax.broadcasted_iota(jnp.int32, (8, 64), 0)
     starts = [(lax.axis_index(a) * n).astype(jnp.float32) for a, n in zip(AXES, (8, 8, 128))]
@@ -459,7 +508,7 @@
         for c in range(3 * SLOTS):
             new_hist[c, here, :] = springs[c] * staying
     for c in range(28):
-        outbox[c : c + 1, :] = jnp.sum(boxes[c], axis=0, keepdims=True)
+        outbox[c : c + 1, 0:64] = jnp.sum(boxes[c], axis=0, keepdims=True)
 
 
 def on_device(offset, velocity, spin, radius, history, contacts, leaving):
@@ -471,7 +520,7 @@
     hist = history.reshape(3 * SLOTS, 64, 128)
     con = contacts.reshape(SLOTS, 64, 128)
     vmem = pl.BlockSpec(memory_space=pltpu.VMEM)
-    anywhere = pl.BlockSpec(memory_space=pl.ANY)
+    hbm = pl.BlockSpec(memory_space=pltpu.HBM)
     halo_shapes = (
         (FULL, 8, 128),
         (FIELDS, 8, 128),
@@ -481,34 +530,19 @@
         (len(PACK_FROM), PACKS, 8, 128),
         (2, PACKS, 8, 128),
     )
-    halos = pl.pallas_call(
-        halo_kernel,
-        out_shape=[jax.ShapeDtypeStruct(s, f32) for s in halo_shapes],
-        in_specs=[anywhere] * 6,
-        out_specs=[vmem] * len(halo_shapes),
-        scratch_shapes=[
+    state, arrivals = pl.pallas_call(
+        step_kernel,
+        out_shape=[pltpu.VMEM((27, 64, 128), f32), pltpu.VMEM((32, 128), f32)],
+        in_specs=[hbm] * 7,
+        out_specs=[vmem] * 2,
+        scratch_shapes=[pltpu.VMEM(s, f32) for s in halo_shapes]
+        + [
             pltpu.VMEM((FULL, 64, 128), f32),
             pltpu.VMEM((SLOTS, 64, 128), jnp.int32),
+            pltpu.VMEM((1, 64), jnp.int32),
             pltpu.VMEM((2, FULL, 8, 128), f32),
             pltpu.VMEM((4, 40, 128), f32),
-            pltpu.SemaphoreType.DMA((6,)),
-            pltpu.SemaphoreType.DMA((len(SENDERS),)),
-            pltpu.SemaphoreType.DMA((len(SENDERS),)),
-        ],
-        compiler_params=pltpu.CompilerParams(collective_id=0, has_side_effects=True),
-        name="halo",
-    )(off, vel, spn, rad, hist, con)
-    state = jax.ShapeDtypeStruct((3, 64, 128), f32)
-    new_off, new_vel, new_spin, new_hist, outbox = pl.pallas_call(
-        compute_kernel,
-        out_shape=[
-            state, state, state,
-            jax.ShapeDtypeStruct((3 * SLOTS, 64, 128), f32),
-            jax.ShapeDtypeStruct((28, 64), f32),
-        ],
-        in_specs=[vmem] * 14,
-        out_specs=[vmem] * 5,
-        scratch_shapes=[
+            pltpu.VMEM((32, 128), f32),
             pltpu.VMEM((FIELDS, HEIGHT, 128), f32),
             pltpu.VMEM((FIELDS, HEIGHT, 128), f32),
             pltpu.VMEM((FIELDS, HEIGHT, 128), f32),
@@ -517,11 +551,32 @@
             pltpu.VMEM((6, HEIGHT, 128), f32),
             pltpu.VMEM((FULL, ROWS, 128), f32),
             pltpu.VMEM((2, FULL, ROWS, 128), f32),
+            pltpu.SemaphoreType.DMA((7,)),
+            pltpu.SemaphoreType.DMA((len(SENDERS) + 1,)),
+            pltpu.SemaphoreType.DMA((len(SENDERS) + 1,)),
         ],
-        name="pairs",
-    )(off, vel, spn, rad, hist, con, leaving.reshape(1, 64), *halos)
-    count = lax.axis_size("gz")
-    arrivals = lax.ppermute(outbox, "gz", [(i + 1, i) for i in range(count - 1)])
+        compiler_params=pltpu.CompilerParams(
+            collective_id=0, has_side_effects=True, vmem_limit_bytes=24 << 20
+        ),
+        name="step",
+    )(*[
+        pltpu.with_memory_space_constraint(a, pltpu.HBM)
+        for a in (off, vel, spn, rad, hist, con, leaving.reshape(1, 64))
+    ])
+    moved = jax.ShapeDtypeStruct((3, 64, 128), f32)
+    new_off, new_vel, new_spin, new_hist, arrivals = pl.pallas_call(
+        write_kernel,
+        out_shape=[
+            moved, moved, moved,
+            jax.ShapeDtypeStruct((3 * SLOTS, 64, 128), f32),
+            jax.ShapeDtypeStruct((28, 1, 64), f32),
+        ],
+        in_specs=[vmem] * 2,
+        out_specs=[hbm] * 4 + [vmem],
+        scratch_shapes=[pltpu.SemaphoreType.DMA((4,))],
+        compiler_params=pltpu.CompilerParams(vmem_limit_bytes=8 << 20),
+        name="write",
+    )(state, arrivals)
     return (
         new_off.reshape(3, 8, 8, 128),
         new_vel.reshape(3, 8, 8, 128),

time: 26.7 us -> 21.8 us (0.82)
  the two profiles are of different devices: /device:TPU:10 before, /device:TPU:1 now
where the time goes in v2:
time: 21.8 us; the launch traced here: 21.7 us
  Pallas kernels  21.1 us (97%)
  between operations  0.64 us (3%)
    pallas_call x1, Pallas kernels, on_device(): pl.pallas_call(step_kernel, out_shape=[pltpu.VMEM((27, 64, 128), f32), pl...  19.5 us
    pallas_call x1, Pallas kernels, on_device(): pl.pallas_call(write_kernel, out_shape=[moved, moved, moved, jax.ShapeDty...  1.54 us

profile of v2, /device:TPU:1, one launch (start us, length us, event | category | flops | bytes accessed | tf_op | source)
XLA Modules:
  0.0 21.7 jit_solution(7506406265379851302)
XLA Ops:
  0.6 19.5 %step.1 = (f32[27,64,128]{2,1,0:T(8,128)S(1)}, f32[32,128]{1,0:T(8,128)S(1)}) custom-call(f32[3,64,128]{2,1,0:T(8,128)} %bitcast.16, f32[3,64,128]{2,1,0:T(8,128)} %bitcast.17, f32[3,64,128]{2,1,0:T(8,128)} %bitcast.18, f32[1,64,128]{2,1,0:T(8,128)} %bitcast.19, f32[18,64,128]{2,1,0:T(8,128)} %bitcast.14, s32[6,64,128]{2,1,0:T(8,128)} %bitcast.15, ...), custom_call_target="tpu_custom_call" | custom-call | tf_op jit(solution)/shard_map/step/pallas_call | solution.py:533
  20.2 1.5 %write.1 = (f32[3,64,128]{2,1,0:T(8,128)}, f32[3,64,128]{2,1,0:T(8,128)}, f32[3,64,128]{2,1,0:T(8,128)}, f32[18,64,128]{2,1,0:T(8,128)}, f32[28,1,64]{2,1,0:T(1,128)}) custom-call(f32[27,64,128]{2,1,0:T(8,128)S(1)} %get-tuple-element.12.state, f32[32,128]{1,0:T(8,128)S(1)} %get-tuple-element.13.arrivals), custom_call_target="tpu_custom_call" | custom-call | tf_op jit(solution)/shard_map/write/pallas_call | solution.py:567

commit v3 on v2

v3 whole, which is shorter than its diff:
```python
import jax
import jax.numpy as jnp
from jax import lax
from jax.experimental import pallas as pl
from jax.experimental.pallas import tpu as pltpu
from jax.sharding import PartitionSpec as P

MESH = pl.DeviceIdType.MESH
AXES = ("gx", "gy", "gz")
DIRS = (
    (1, 0, 0),
    (0, 1, 0),
    (0, 0, 1),
    (1, 1, 0),
    (1, -1, 0),
    (1, 0, 1),
    (1, 0, -1),
    (0, 1, 1),
    (0, 1, -1),
)
SLOTS = 6
FIELDS = 10
SHEAR = FIELDS
CODES = FIELDS + 3 * SLOTS
FULL = CODES + SLOTS
PACKS = (FULL * 8 + 127) // 128
STEP = 0.05
TINY = 1e-30

ROWS = 24
HEIGHT = 10 * ROWS

PACK_FROM = (
    (0, 0, -1),
    (0, 0, 1),
    (-1, 0, -1),
    (-1, 0, 1),
    (1, 0, -1),
    (1, 0, 1),
    (0, -1, -1),
    (0, -1, 1),
    (0, 1, -1),
    (0, 1, 1),
)
FLAT_FROM = (
    (-1, 0, 0),
    (1, 0, 0),
    (0, -1, 0),
    (0, 1, 0),
    (-1, -1, 0),
    (-1, 1, 0),
    (1, -1, 0),
    (1, 1, 0),
)
SENDERS = FLAT_FROM + PACK_FROM

ALONG_X = (0, 3, 4, 5, 6)
UP_Y = (1, 3, 7, 8)
DOWN_Y = (4,)


def plane(x):
    return (x + 1) * ROWS + 8


def step_kernel(
    off_hbm, vel_hbm, spin_hbm, rad_hbm, hist_hbm, con_hbm, leaving_hbm,
    state, arrivals,
    xlo, xhi, ylo, yhi, edges, packs, own_packs, cells, codes, leaving,
    xrow, ytop, ylow, rows, outbox,
    pad, pad_up, pad_down, level, rising, falling, behind, ahead, zside,
    local_sems, send_sems, recv_sems,
):
    here = [lax.axis_index(a) for a in AXES]
    size = [lax.axis_size(a) for a in AXES]

    def exists(step):
        ok = None
        for at, n, s in zip(here, size, step):
            if s == 0:
                continue
            test = at + s < n if s > 0 else at + s >= 0
            ok = test if ok is None else jnp.logical_and(ok, test)
        return ok

    def place(step):
        return tuple(at + s for at, s in zip(here, step))

    loads = [
        pltpu.make_async_copy(off_hbm, cells.at[0:3], local_sems.at[0]),
        pltpu.make_async_copy(vel_hbm, cells.at[3:6], local_sems.at[1]),
        pltpu.make_async_copy(spin_hbm, cells.at[6:9], local_sems.at[2]),
        pltpu.make_async_copy(rad_hbm, cells.at[9:10], local_sems.at[3]),
        pltpu.make_async_copy(hist_hbm, cells.at[SHEAR:CODES], local_sems.at[4]),
        pltpu.make_async_copy(con_hbm, codes, local_sems.at[5]),
        pltpu.make_async_copy(leaving_hbm, leaving, local_sems.at[6]),
    ]
    for load in loads:
        load.start()
    barrier = pltpu.get_barrier_semaphore()
    expected = jnp.int32(0)
    for step in SENDERS:
        there = exists(step)
        expected = expected + there.astype(jnp.int32)

        @pl.when(there)
        def _():
            pl.semaphore_signal(barrier, inc=1, device_id=place(step), device_id_type=MESH)

    with jax.named_scope("loadwait"):
        for load in loads:
            load.wait()
    with jax.named_scope("pack"):
        for s in range(SLOTS):
            cells[CODES + s] = codes[s].astype(jnp.float32)
        fill_sends(cells, own_packs, xrow, ytop, ylow, rows)

    targets = [xlo, xhi, ylo, yhi] + [edges.at[k] for k in range(4)]
    sources = [xrow, cells.at[0:FIELDS, 0:8, :], ytop, ylow] + [rows.at[k] for k in range(4)]
    for k, s in enumerate(PACK_FROM):
        own = own_packs.at[0 if s[2] > 0 else 1]
        fields_only = s[0] + s[1] > 0
        targets.append(packs.at[k, 0:1] if fields_only else packs.at[k])
        sources.append(own.at[0:1] if fields_only else own)

    def copy(k):
        to = tuple(-s for s in SENDERS[k])
        return pltpu.make_async_remote_copy(
            src_ref=sources[k],
            dst_ref=targets[k],
            send_sem=send_sems.at[k],
            recv_sem=recv_sems.at[k],
            device_id=place(to),
            device_id_type=MESH,
        )

    for k, step in enumerate(SENDERS):

        @pl.when(jnp.logical_not(exists(step)))
        def _():
            targets[k][...] = jnp.zeros(targets[k].shape, jnp.float32)

    with jax.named_scope("barrier"):
        pl.semaphore_wait(barrier, expected)
    for k, step in enumerate(SENDERS):

        @pl.when(exists(tuple(-s for s in step)))
        def _():
            copy(k).start()

    with jax.named_scope("inner"):
        inner_pairs(cells, state, pad, pad_up, pad_down, level, rising, falling)

    for k, step in enumerate(SENDERS):
        with jax.named_scope("recv%d" % k):

            @pl.when(exists(step))
            def _():
                copy(k).wait_recv()

    with jax.named_scope("outer"):
        ends = outer_pairs(
            cells, state, pad, level, behind, ahead, zside, xlo, xhi, ylo, yhi, edges, packs,
            own_packs, xrow, ytop, ylow,
        )
    with jax.named_scope("final"):
        finish(cells, state, leaving, outbox, level, rising, falling, ends)

    last = len(SENDERS)
    fall = pltpu.make_async_remote_copy(
        src_ref=outbox,
        dst_ref=arrivals,
        send_sem=send_sems.at[last],
        recv_sem=recv_sems.at[last],
        device_id=place((0, 0, -1)),
        device_id_type=MESH,
    )

    @pl.when(exists((0, 0, -1)))
    def _():
        fall.start()

    for k, step in enumerate(SENDERS):

        @pl.when(exists(tuple(-s for s in step)))
        def _():
            copy(k).wait_send()

    with jax.named_scope("fall"):

        @pl.when(exists((0, 0, 1)))
        def _():
            fall.wait_recv()

    @pl.when(jnp.logical_not(exists((0, 0, 1))))
    def _():
        arrivals[...] = jnp.zeros(arrivals.shape, jnp.float32)

    @pl.when(exists((0, 0, -1)))
    def _():
        fall.wait_send()


def write_kernel(state, arrivals, new_off, new_vel, new_spin, new_hist, entered, sems):
    copies = [
        pltpu.make_async_copy(state.at[9:27], new_hist, sems.at[0]),
        pltpu.make_async_copy(state.at[0:3], new_off, sems.at[1]),
        pltpu.make_async_copy(state.at[3:6], new_vel, sems.at[2]),
        pltpu.make_async_copy(state.at[6:9], new_spin, sems.at[3]),
    ]
    for copy in copies:
        copy.start()
    for c in range(28):
        entered[c] = arrivals[c : c + 1, 0:64]
    for copy in copies:
        copy.wait()


def cross(a, b):
    return [
        a[1] * b[2] - a[2] * b[1],
        a[2] * b[0] - a[0] * b[2],
        a[0] * b[1] - a[1] * b[0],
    ]


def dot3(a, b):
    return a[0] * b[0] + a[1] * b[1] + a[2] * b[2]


def pair(first, second, direction, shear, live):
    sep = []
    for k in range(3):
        gap = second[k] - first[k]
        sep.append(gap + float(direction[k]) if direction[k] else gap)
    square = dot3(sep, sep)
    inverse = lax.rsqrt(square)
    normal = [s * inverse for s in sep]
    radii = first[9] + second[9]
    overlap = jnp.maximum(radii - square * inverse, 0.0)
    product = first[9] * second[9] * overlap
    contact = product * lax.rsqrt(jnp.maximum(product * radii, TINY))
    contact = jnp.where(live, contact, 0.0)
    surface = cross([first[6 + k] + second[6 + k] for k in range(3)], normal)
    relative = [second[3 + k] - first[3 + k] - surface[k] for k in range(3)]
    approach = dot3(relative, normal)
    sliding = [relative[k] - approach * normal[k] for k in range(3)]
    repulsion = contact * jnp.maximum(10.0 * overlap - 2.0 * approach, 0.0)
    along = dot3(shear, normal)
    spring = [shear[k] - along * normal[k] + STEP * sliding[k] for k in range(3)]
    pull = [8.0 * spring[k] + 1.5 * sliding[k] for k in range(3)]
    size = contact * contact * dot3(pull, pull)
    factor = jnp.minimum(1.0, 0.4 * repulsion * lax.rsqrt(jnp.maximum(size, 0.0025)))
    scale = factor * contact
    tangent = [scale * pull[k] for k in range(3)]
    force = [tangent[k] - repulsion * normal[k] for k in range(3)]
    return force, cross(normal, tangent), [factor * spring[k] for k in range(3)]


def pick_shear(load, numbers):
    codes = [load(CODES + s) for s in range(SLOTS)]
    found = []
    for number in numbers:
        masks = [code == float(number) for code in codes]
        live = masks[0]
        shear = [jnp.where(masks[0], load(SHEAR + k), 0.0) for k in range(3)]
        for s in range(1, SLOTS):
            live = jnp.logical_or(live, masks[s])
            shear = [jnp.where(masks[s], load(SHEAR + 3 * s + k), shear[k]) for k in range(3)]
        found.append((shear, live, masks))
    return found


def scaled(values):
    return values[:6] + [v * values[9] for v in values[6:9]] + [values[9]]


def lanes():
    return lax.broadcasted_iota(jnp.int32, (8, 128), 1)


def fill_sends(cells, own_packs, xrow, ytop, ylow, rows):
    lane = lanes()
    for c in range(FIELDS):
        xrow[c] = cells[c, 56:64, :]
        ytop[c] = cells[c, pl.ds(7, 8, stride=8), :]
        ylow[c] = cells[c, pl.ds(0, 8, stride=8), :]
    for target, span, numbers in (
        (xrow, pl.ds(56, 8), ALONG_X),
        (ytop, pl.ds(7, 8, stride=8), UP_Y),
        (ylow, pl.ds(0, 8, stride=8), DOWN_Y),
    ):
        found = pick_shear(lambda c: cells[c, span, :], numbers)
        for n, (shear, live, _) in enumerate(found):
            for k in range(3):
                target[FIELDS + 4 * n + k] = shear[k]
            target[FIELDS + 4 * n + 3] = jnp.where(live, 1.0, 0.0)
    for which, row, at in ((0, 7, 1), (1, 0, 2)):
        for c in range(FIELDS):
            rows[which, c : c + 1, :] = xrow[c, row : row + 1, :]
        for k in range(4):
            rows[which, FIELDS + k : FIELDS + k + 1, :] = xrow[
                FIELDS + 4 * at + k, row : row + 1, :
            ]
    for which, row in ((2, 7), (3, 0)):
        for c in range(FIELDS):
            rows[which, c : c + 1, :] = cells[c, row : row + 1, :]
    for k in range(PACKS):
        low = jnp.zeros((8, 128), jnp.float32)
        top = jnp.zeros((8, 128), jnp.float32)
        for c in range(k * 16, min(FULL, k * 16 + 16)):
            for x in range(8):
                p = (c % 16) * 8 + x
                value = cells[c, x * 8 : x * 8 + 8, :]
                if p:
                    value = pltpu.roll(value, p, 1)
                low = jnp.where(lane == p, value, low)
                top = jnp.where(lane == (p - 1) % 128, value, top)
        own_packs[0, k] = low
        own_packs[1, k] = top


def inner_pairs(cells, state, pad, pad_up, pad_down, level, rising, falling):
    lane = lanes()
    zero = jnp.zeros((8, 128), jnp.float32)
    row = jnp.zeros((1, 128), jnp.float32)
    for x in range(8):
        here = slice(x * 8, x * 8 + 8)
        span = pl.ds(plane(x), 8)
        for c, v in enumerate(scaled([cells[c, here, :] for c in range(FIELDS)])):
            pad[c, span, :] = v
            pad_up[c, span, :] = jnp.where(lane == 127, 0.0, pltpu.roll(v, 127, 1))
            pad_down[c, span, :] = jnp.where(lane == 0, 0.0, pltpu.roll(v, 1, 1))
            pad[c, plane(x) - 1 : plane(x), :] = row
            for source in (pad, pad_up, pad_down):
                source[c, plane(x) + 8 : plane(x) + 9, :] = row
    for c in range(FIELDS):
        for source in (pad, pad_up, pad_down):
            source[c, pl.ds(plane(8), 8), :] = zero
        pad[c, plane(8) - 1 : plane(8), :] = row
        pad[c, plane(8) + 8 : plane(8) + 9, :] = row
    for total in (level, rising, falling):
        for c in range(6):
            for x in range(9):
                total[c, pl.ds(plane(x), 8), :] = zero
                total[c, plane(x) - 1 : plane(x), :] = row
                total[c, plane(x) + 8 : plane(x) + 9, :] = row

    def body(x, carry):
        base = pl.multiple_of((x + 1) * ROWS + 8, 8)
        here = pl.ds(pl.multiple_of(x * 8, 8), 8)
        first = [pad[c, pl.ds(base, 8), :] for c in range(FIELDS)]
        forces = [zero] * 3
        twists = [zero] * 3
        springs = [zero] * (3 * SLOTS)
        for number, (dx, dy, dz) in enumerate(DIRS):
            span = pl.ds(base + dx * ROWS + dy, 8)
            source = (pad, pad_up, pad_down)[dz]
            total = (level, rising, falling)[dz]
            second = [source[c, span, :] for c in range(FIELDS)]
            ((shear, live, masks),) = pick_shear(lambda c: cells[c, here, :], (number,))
            force, twist, spring = pair(first, second, (dx, dy, dz), shear, live)
            for k in range(3):
                forces[k] = forces[k] + force[k]
                twists[k] = twists[k] + twist[k]
                for s in range(SLOTS):
                    springs[3 * s + k] = jnp.where(masks[s], spring[k], springs[3 * s + k])
                total[k, span, :] = total[k, span, :] - force[k]
                total[3 + k, span, :] = total[3 + k, span, :] + twist[k]
        for k in range(3):
            level[k, pl.ds(base, 8), :] = level[k, pl.ds(base, 8), :] + forces[k]
            level[3 + k, pl.ds(base, 8), :] = level[3 + k, pl.ds(base, 8), :] + twists[k]
        for c in range(3 * SLOTS):
            state[9 + c, here, :] = springs[c]
        return carry

    lax.fori_loop(0, 8, body, 0)


def outer_pairs(
    cells, state, pad, level, behind, ahead, zside, xlo, xhi, ylo, yhi, edges, packs,
    own_packs, xrow, ytop, ylow,
):
    lane = lanes()
    sub = lax.broadcasted_iota(jnp.int32, (8, 128), 0)
    zero = jnp.zeros((8, 128), jnp.float32)

    class Sums:
        def __init__(self):
            self.total = [zero] * 6
            self.springs = [zero] * (3 * SLOTS)

        def own(self, result, masks):
            force, twist, spring = result
            for k in range(3):
                self.total[k] = self.total[k] + force[k]
                self.total[3 + k] = self.total[3 + k] + twist[k]
                for s in range(SLOTS):
                    self.springs[3 * s + k] = jnp.where(
                        masks[s], spring[k], self.springs[3 * s + k]
                    )

        def partner(self, result):
            force, twist, _ = result
            for k in range(3):
                self.total[k] = self.total[k] - force[k]
                self.total[3 + k] = self.total[3 + k] + twist[k]

        def store(self, rows, span):
            for c in range(6):
                level[c, rows, :] = level[c, rows, :] + self.total[c]
            if span is not None:
                for c in range(3 * SLOTS):
                    state[9 + c, span, :] = state[9 + c, span, :] + self.springs[c]

    def turned(values, amount, axis=1):
        return [pltpu.roll(v, amount, axis) for v in values]

    def masks_of(span, number):
        return [cells[CODES + s, span, :] == float(number) for s in range(SLOTS)]

    for c in range(FIELDS + 4 * len(ALONG_X)):
        behind[c, 8:16, :] = xlo[c]
    for c in range(FIELDS):
        behind[c, 7:8, :] = edges[0, c : c + 1, :]
        behind[c, 16:17, :] = edges[1, c : c + 1, :]
        ahead[c, 7:8, :] = edges[2, c : c + 1, :]
        ahead[c, 16:17, :] = edges[3, c : c + 1, :]
        ahead[c, 8:16, :] = xhi[c]
    for k in range(4):
        behind[FIELDS + 4 + k, 7:8, :] = edges[0, FIELDS + k : FIELDS + k + 1, :]
        behind[FIELDS + 8 + k, 16:17, :] = edges[1, FIELDS + k : FIELDS + k + 1, :]

    def pack_scaled(pack, top):
        group = (lane + top) // 8
        for c in (6, 7, 8):
            radius = pltpu.roll(pack, 128 - 8 * (9 - c), 1)
            pack = jnp.where(group == c, pack * radius, pack)
        return pack

    beyond_up = pack_scaled(packs[5, 0], 0)
    beyond_down = pack_scaled(packs[4, 0], 1)
    sums = Sums()
    first = [pad[c, pl.ds(plane(7), 8), :] for c in range(FIELDS)]
    for n, number in enumerate(ALONG_X):
        dx, dy, dz = DIRS[number]
        second = scaled([ahead[c, pl.ds(8 + dy, 8), :] for c in range(FIELDS)])
        if dz > 0:
            second = [
                jnp.where(
                    lane == 127, pltpu.roll(beyond_up, 127 - 8 * c, 1), pltpu.roll(v, 127, 1)
                )
                for c, v in enumerate(second)
            ]
        elif dz < 0:
            second = [
                jnp.where(
                    lane == 0, pltpu.roll(beyond_down, (129 - 8 * c) % 128, 1), pltpu.roll(v, 1, 1)
                )
                for c, v in enumerate(second)
            ]
        at = FIELDS + 4 * n
        shear = [xrow[at + k] for k in range(3)]
        result = pair(first, second, DIRS[number], shear, xrow[at + 3] > 0.5)
        sums.own(result, masks_of(pl.ds(56, 8), number))
    sums.store(pl.ds(plane(7), 8), pl.ds(56, 8))
    sums = Sums()
    second = [pad[c, pl.ds(plane(0), 8), :] for c in range(FIELDS)]
    for n, number in enumerate(ALONG_X):
        dx, dy, dz = DIRS[number]
        span = pl.ds(8 - dy, 8)
        first = scaled([behind[c, span, :] for c in range(FIELDS)])
        first += [behind[FIELDS + 4 * n + k, span, :] for k in range(4)]
        if dz:
            first = turned(first, dz % 128)
        live = first[13] > 0.5
        if dz:
            live = jnp.logical_and(live, lane != (0 if dz > 0 else 127))
        sums.partner(pair(first[:10], second, DIRS[number], first[10:13], live))
    sums.store(pl.ds(plane(0), 8), None)

    top_fields = scaled([yhi[c] for c in range(FIELDS)])
    low_fields = scaled([ylo[c] for c in range(FIELDS)])
    sums = Sums()
    mine_rows = pl.ds(plane(0) + 7, 8, stride=ROWS)
    span = pl.ds(7, 8, stride=8)
    mine = [pad[c, mine_rows, :] for c in range(FIELDS)]
    for n, number in enumerate(UP_Y):
        dx, dy, dz = DIRS[number]
        at = FIELDS + 4 * n
        live = ytop[at + 3] > 0.5
        second = top_fields
        if dx:
            second = turned(second, 7, 0)
            live = jnp.logical_and(live, sub != 7)
        if dz:
            second = turned(second, -dz % 128)
            live = jnp.logical_and(live, lane != (127 if dz > 0 else 0))
        shear = [ytop[at + k] for k in range(3)]
        sums.own(pair(mine, second, DIRS[number], shear, live), masks_of(span, number))
    first = turned(top_fields + [yhi[FIELDS + k] for k in range(4)], 1, 0)
    live = jnp.logical_and(first[13] > 0.5, sub != 0)
    sums.partner(pair(first[:10], mine, DIRS[4], first[10:13], live))
    sums.store(mine_rows, span)

    sums = Sums()
    mine_rows = pl.ds(plane(0), 8, stride=ROWS)
    span = pl.ds(0, 8, stride=8)
    mine = [pad[c, mine_rows, :] for c in range(FIELDS)]
    second = turned(low_fields, 7, 0)
    live = jnp.logical_and(ylow[FIELDS + 3] > 0.5, sub != 7)
    shear = [ylow[FIELDS + k] for k in range(3)]
    sums.own(pair(mine, second, DIRS[4], shear, live), masks_of(span, 4))
    for n, number in enumerate(UP_Y):
        dx, dy, dz = DIRS[number]
        first = low_fields + [ylo[FIELDS + 4 * n + k] for k in range(4)]
        if dx:
            first = turned(first, 1, 0)
        if dz:
            first = turned(first, dz % 128)
        live = first[13] > 0.5
        if dx:
            live = jnp.logical_and(live, sub != 0)
        if dz:
            live = jnp.logical_and(live, lane != (0 if dz > 0 else 127))
        sums.partner(pair(first[:10], mine, DIRS[number], first[10:13], live))
    sums.store(mine_rows, span)

    def spread(pack, c, top):
        p = (c % 16) * 8 - top
        return pltpu.roll(pack, (128 - p) % 128, 1) if p % 128 else pack

    ends = []
    for end, theirs, ours in ((0, (2, 5, 7), (6, 8)), (1, (6, 8), (2, 5, 7))):
        top = 1 - end
        for k in range(PACKS):
            straight, back, left = packs[end, k], packs[2 + end, k], packs[6 + end, k]
            for c in range(16 * k, min(FULL, 16 * k + 16)):
                before = pltpu.roll(spread(back, c, top), 120, 1)
                zside[end, c, 8:16, :] = jnp.where(lane == 127, before, spread(straight, c, top))
                zside[end, c, 0:8, :] = spread(left, c, top)
                if c < FIELDS:
                    zside[end, c, 16:24, :] = spread(packs[8 + end, 0], c, top)
        own = [spread(own_packs[end, c // 16], c, end) for c in range(FULL)]
        mine = scaled(own[:FIELDS])
        sums = Sums()
        for number, (shear, live, masks) in zip(ours, pick_shear(lambda c: own[c], ours)):
            dx, dy, dz = DIRS[number]
            second = scaled([zside[end, c, pl.ds(8 + dy, 8), :] for c in range(FIELDS)])
            if dx:
                second = [jnp.where(lane < 7, v, 0.0) for v in turned(second, 127)]
            sums.own(pair(mine, second, DIRS[number], shear, live), masks)
        for number in theirs:
            dx, dy, dz = DIRS[number]
            span = pl.ds(8 - dy, 8)
            first = scaled([zside[end, c, span, :] for c in range(FIELDS)])
            ((shear, live, _),) = pick_shear(lambda c: zside[end, c, span, :], (number,))
            first = first + shear + [jnp.where(live, 1.0, 0.0)]
            if dx:
                first = turned(first, 1)
            sums.partner(pair(first[:10], mine, DIRS[number], first[10:13], first[13] > 0.5))
        ends.append(sums.total + sums.springs)
    return ends


def finish(cells, state, leaving, outbox, level, rising, falling, ends):
    lane = lanes()
    sub = lax.broadcasted_iota(jnp.int32, (8, 128), 0)
    wide = jnp.broadcast_to(leaving[0:1, 0:64], (8, 64))
    deep = lax.broadcasted_iota(jnp.int32, (8, 64), 0)
    starts = [(lax.axis_index(a) * n).astype(jnp.float32) for a, n in zip(AXES, (8, 8, 128))]
    boxes = [jnp.zeros((8, 64), jnp.float32) for _ in range(28)]
    for x in range(8):
        rows = pl.ds(plane(x), 8)
        here = slice(x * 8, x * 8 + 8)

        def at_ends(c):
            low, top = ends[0][c], ends[1][c]
            low = pltpu.roll(low, 128 - x, 1) if x else low
            return jnp.where(
                lane == 0, low, jnp.where(lane == 127, pltpu.roll(top, 127 - x, 1), 0.0)
            )

        sums = []
        for c in range(6):
            up = jnp.where(lane == 0, 0.0, pltpu.roll(rising[c, rows, :], 1, 1))
            down = jnp.where(lane == 127, 0.0, pltpu.roll(falling[c, rows, :], 127, 1))
            sums.append(level[c, rows, :] + up + down + at_ends(c))
        radius = cells[9, here, :]
        inverse = 1.0 / radius
        push = STEP * inverse * inverse * inverse
        turn = 0.125 * (inverse * inverse) * (inverse * inverse)
        velocity = [cells[3 + k, here, :] + push * sums[k] for k in range(3)]
        velocity[2] = velocity[2] - STEP
        offset = [cells[k, here, :] + STEP * velocity[k] for k in range(3)]
        rotation = [cells[6 + k, here, :] + turn * sums[3 + k] for k in range(3)]
        springs = [state[9 + c, here, :] + at_ends(6 + c) for c in range(3 * SLOTS)]
        bottom = [wide == (x * 8 + deep) * 128 + z for z in range(2)]
        left = [jnp.max(jnp.where(b, 1.0, 0.0), axis=1, keepdims=True) for b in bottom]
        staying = 1.0 - jnp.where(lane == 0, left[0], jnp.where(lane == 1, left[1], 0.0))
        position = [
            offset[0] + (starts[0] + float(x)),
            offset[1] + (starts[1] + sub.astype(jnp.float32)),
            offset[2] + (starts[2] + lane.astype(jnp.float32)),
        ]
        for c, v in enumerate(position + velocity + rotation + [radius] + springs):
            for z in range(2):
                value = jnp.broadcast_to(v[:, z : z + 1], (8, 64))
                boxes[c] = boxes[c] + jnp.where(bottom[z], value, 0.0)
        for c, v in enumerate(offset + velocity + rotation + springs):
            state[c, here, :] = v * staying
    for c in range(28):
        outbox[c : c + 1, 0:64] = jnp.sum(boxes[c], axis=0, keepdims=True)


def on_device(offset, velocity, spin, radius, history, contacts, leaving):
    f32 = jnp.float32
    off = offset.reshape(3, 64, 128)
    vel = velocity.reshape(3, 64, 128)
    spn = spin.reshape(3, 64, 128)
    rad = radius.reshape(1, 64, 128)
    hist = history.reshape(3 * SLOTS, 64, 128)
    con = contacts.reshape(SLOTS, 64, 128)
    vmem = pl.BlockSpec(memory_space=pltpu.VMEM)
    hbm = pl.BlockSpec(memory_space=pltpu.HBM)
    halo_shapes = (
        (FIELDS + 4 * len(ALONG_X), 8, 128),
        (FIELDS, 8, 128),
        (FIELDS + 4 * len(UP_Y), 8, 128),
        (FIELDS + 4 * len(DOWN_Y), 8, 128),
        (4, 16, 128),
        (len(PACK_FROM), PACKS, 8, 128),
        (2, PACKS, 8, 128),
    )
    state, arrivals = pl.pallas_call(
        step_kernel,
        out_shape=[pltpu.VMEM((27, 64, 128), f32), pltpu.VMEM((32, 128), f32)],
        in_specs=[hbm] * 7,
        out_specs=[vmem] * 2,
        scratch_shapes=[pltpu.VMEM(s, f32) for s in halo_shapes]
        + [
            pltpu.VMEM((FULL, 64, 128), f32),
            pltpu.VMEM((SLOTS, 64, 128), jnp.int32),
            pltpu.VMEM((1, 64), jnp.int32),
            pltpu.VMEM((FIELDS + 4 * len(ALONG_X), 8, 128), f32),
            pltpu.VMEM((FIELDS + 4 * len(UP_Y), 8, 128), f32),
            pltpu.VMEM((FIELDS + 4 * len(DOWN_Y), 8, 128), f32),
            pltpu.VMEM((4, 16, 128), f32),
            pltpu.VMEM((32, 128), f32),
            pltpu.VMEM((FIELDS, HEIGHT, 128), f32),
            pltpu.VMEM((FIELDS, HEIGHT, 128), f32),
            pltpu.VMEM((FIELDS, HEIGHT, 128), f32),
            pltpu.VMEM((6, HEIGHT, 128), f32),
            pltpu.VMEM((6, HEIGHT, 128), f32),
            pltpu.VMEM((6, HEIGHT, 128), f32),
            pltpu.VMEM((FIELDS + 4 * len(ALONG_X), ROWS, 128), f32),
            pltpu.VMEM((FIELDS, ROWS, 128), f32),
            pltpu.VMEM((2, FULL, ROWS, 128), f32),
            pltpu.SemaphoreType.DMA((7,)),
            pltpu.SemaphoreType.DMA((len(SENDERS) + 1,)),
            pltpu.SemaphoreType.DMA((len(SENDERS) + 1,)),
        ],
        compiler_params=pltpu.CompilerParams(
            collective_id=0, has_side_effects=True, vmem_limit_bytes=24 << 20
        ),
        name="step",
    )(*[
        pltpu.with_memory_space_constraint(a, pltpu.HBM)
        for a in (off, vel, spn, rad, hist, con, leaving.reshape(1, 64))
    ])
    moved = jax.ShapeDtypeStruct((3, 64, 128), f32)
    new_off, new_vel, new_spin, new_hist, arrivals = pl.pallas_call(
        write_kernel,
        out_shape=[
            moved, moved, moved,
            jax.ShapeDtypeStruct((3 * SLOTS, 64, 128), f32),
            jax.ShapeDtypeStruct((28, 1, 64), f32),
        ],
        in_specs=[vmem] * 2,
        out_specs=[hbm] * 4 + [vmem],
        scratch_shapes=[pltpu.SemaphoreType.DMA((4,))],
        compiler_params=pltpu.CompilerParams(vmem_limit_bytes=8 << 20),
        name="write",
    )(state, arrivals)
    return (
        new_off.reshape(3, 8, 8, 128),
        new_vel.reshape(3, 8, 8, 128),
        new_spin.reshape(3, 8, 8, 128),
        new_hist.reshape(SLOTS, 3, 8, 8, 128),
        arrivals.reshape(28, 1, 1, 1, 64),
    )


def solution(mesh):
    placed = (
        P(None, "gx", "gy", "gz"),
        P(None, "gx", "gy", "gz"),
        P(None, "gx", "gy", "gz"),
        P("gx", "gy", "gz"),
        P(None, None, "gx", "gy", "gz"),
        P(None, "gx", "gy", "gz"),
        P("gx", "gy", "gz", None),
    )
    return jax.shard_map(
        on_device,
        mesh=mesh,
        in_specs=placed,
        out_specs=(
            P(None, "gx", "gy", "gz"),
            P(None, "gx", "gy", "gz"),
            P(None, "gx", "gy", "gz"),
            P(None, None, "gx", "gy", "gz"),
            P(None, "gx", "gy", "gz", None),
        ),
        check_vma=False,
    )
```

time: 21.8 us -> 19.3 us (0.89)
  Pallas kernels: 21.1 us -> 18.6 us
    pallas_call x1, Pallas kernels: 19.5 us -> 17 us  [on_device(): pl.pallas_call(step_kernel, out_shape=[pltpu.VMEM((27, 64, 128), f32), pl...]
where the time goes in v3:
time: 19.3 us; the launch traced here: 19.2 us
  Pallas kernels  18.6 us (96%)
  between operations  0.64 us (3%)
    pallas_call x1, Pallas kernels, on_device(): pl.pallas_call(step_kernel, out_shape=[pltpu.VMEM((27, 64, 128), f32), pl...  17 us
    pallas_call x1, Pallas kernels, on_device(): pl.pallas_call(write_kernel, out_shape=[moved, moved, moved, jax.ShapeDty...  1.54 us

profile of v3, /device:TPU:1, one launch (start us, length us, event | category | flops | bytes accessed | tf_op | source)
XLA Modules:
  0.0 19.2 jit_solution(14191709194310084221)
XLA Ops:
  0.6 17.0 %step.1 = (f32[27,64,128]{2,1,0:T(8,128)S(1)}, f32[32,128]{1,0:T(8,128)S(1)}) custom-call(f32[3,64,128]{2,1,0:T(8,128)} %bitcast.16, f32[3,64,128]{2,1,0:T(8,128)} %bitcast.17, f32[3,64,128]{2,1,0:T(8,128)} %bitcast.18, f32[1,64,128]{2,1,0:T(8,128)} %bitcast.19, f32[18,64,128]{2,1,0:T(8,128)} %bitcast.14, s32[6,64,128]{2,1,0:T(8,128)} %bitcast.15, ...), custom_call_target="tpu_custom_call" | custom-call | tf_op jit(solution)/shard_map/step/pallas_call | solution.py:635
  17.7 1.5 %write.1 = (f32[3,64,128]{2,1,0:T(8,128)}, f32[3,64,128]{2,1,0:T(8,128)}, f32[3,64,128]{2,1,0:T(8,128)}, f32[18,64,128]{2,1,0:T(8,128)}, f32[28,1,64]{2,1,0:T(1,128)}) custom-call(f32[27,64,128]{2,1,0:T(8,128)S(1)} %get-tuple-element.12.state, f32[32,128]{1,0:T(8,128)S(1)} %get-tuple-element.13.arrivals), custom_call_target="tpu_custom_call" | custom-call | tf_op jit(solution)/shard_map/write/pallas_call | solution.py:672

commit v4 on v3

--- a/solution.py
+++ b/solution.py
@@ -58,6 +58,8 @@
 UP_Y = (1, 3, 7, 8)
 DOWN_Y = (4,)
 
+SEND_ORDER = (8, 9, 14, 15, 16, 17, 10, 11, 12, 13, 4, 5, 6, 7, 2, 3, 0, 1)
+
 
 def plane(x):
     return (x + 1) * ROWS + 8
@@ -142,29 +144,38 @@
 
     with jax.named_scope("barrier"):
         pl.semaphore_wait(barrier, expected)
-    for k, step in enumerate(SENDERS):
-
-        @pl.when(exists(tuple(-s for s in step)))
+    for k in SEND_ORDER:
+
+        @pl.when(exists(tuple(-s for s in SENDERS[k])))
         def _():
             copy(k).start()
 
     with jax.named_scope("inner"):
         inner_pairs(cells, state, pad, pad_up, pad_down, level, rising, falling)
 
-    for k, step in enumerate(SENDERS):
-        with jax.named_scope("recv%d" % k):
-
-            @pl.when(exists(step))
+    def receive(which):
+        for k in which:
+
+            @pl.when(exists(SENDERS[k]))
             def _():
                 copy(k).wait_recv()
 
-    with jax.named_scope("outer"):
-        ends = outer_pairs(
-            cells, state, pad, level, behind, ahead, zside, xlo, xhi, ylo, yhi, edges, packs,
-            own_packs, xrow, ytop, ylow,
-        )
-    with jax.named_scope("final"):
-        finish(cells, state, leaving, outbox, level, rising, falling, ends)
+    with jax.named_scope("fold"):
+        fold(level, rising, falling)
+    with jax.named_scope("recvz"):
+        receive(range(8, 18, 2))
+    with jax.named_scope("floor"):
+        end_pairs(0, level, state, zside, packs, own_packs)
+    with jax.named_scope("recvy"):
+        receive((2, 3))
+    with jax.named_scope("ypairs"):
+        y_pairs(cells, state, pad, level, ylo, yhi, ytop, ylow)
+    with jax.named_scope("recvx"):
+        receive((0, 1, 4, 5, 6, 7, 13))
+    with jax.named_scope("xpairs"):
+        x_pairs(cells, state, pad, level, behind, ahead, xlo, xhi, edges, packs, xrow)
+    with jax.named_scope("outbox"):
+        fill_outbox(cells, state, leaving, outbox, level)
 
     last = len(SENDERS)
     fall = pltpu.make_async_remote_copy(
@@ -179,6 +190,13 @@
     @pl.when(exists((0, 0, -1)))
     def _():
         fall.start()
+
+    with jax.named_scope("recvtop"):
+        receive((9, 11, 15, 17))
+    with jax.named_scope("ceiling"):
+        end_pairs(1, level, state, zside, packs, own_packs)
+    with jax.named_scope("final"):
+        finish(cells, state, leaving, level)
 
     for k, step in enumerate(SENDERS):
 
@@ -377,48 +395,54 @@
     lax.fori_loop(0, 8, body, 0)
 
 
-def outer_pairs(
-    cells, state, pad, level, behind, ahead, zside, xlo, xhi, ylo, yhi, edges, packs,
-    own_packs, xrow, ytop, ylow,
-):
+class Sums:
+    def __init__(self):
+        zero = jnp.zeros((8, 128), jnp.float32)
+        self.total = [zero] * 6
+        self.springs = [zero] * (3 * SLOTS)
+
+    def own(self, result, masks):
+        force, twist, spring = result
+        for k in range(3):
+            self.total[k] = self.total[k] + force[k]
+            self.total[3 + k] = self.total[3 + k] + twist[k]
+            for s in range(SLOTS):
+                self.springs[3 * s + k] = jnp.where(masks[s], spring[k], self.springs[3 * s + k])
+
+    def partner(self, result):
+        force, twist, _ = result
+        for k in range(3):
+            self.total[k] = self.total[k] - force[k]
+            self.total[3 + k] = self.total[3 + k] + twist[k]
+
+    def store(self, level, rows, state, span):
+        for c in range(6):
+            level[c, rows, :] = level[c, rows, :] + self.total[c]
+        if span is not None:
+            for c in range(3 * SLOTS):
+                state[9 + c, span, :] = state[9 + c, span, :] + self.springs[c]
+
+
+def turned(values, amount, axis=1):
+    return [pltpu.roll(v, amount, axis) for v in values]
+
+
+def masks_of(cells, span, number):
+    return [cells[CODES + s, span, :] == float(number) for s in range(SLOTS)]
+
+
+def fold(level, rising, falling):
     lane = lanes()
-    sub = lax.broadcasted_iota(jnp.int32, (8, 128), 0)
-    zero = jnp.zeros((8, 128), jnp.float32)
-
-    class Sums:
-        def __init__(self):
-            self.total = [zero] * 6
-            self.springs = [zero] * (3 * SLOTS)
-
-        def own(self, result, masks):
-            force, twist, spring = result
-            for k in range(3):
-                self.total[k] = self.total[k] + force[k]
-                self.total[3 + k] = self.total[3 + k] + twist[k]
-                for s in range(SLOTS):
-                    self.springs[3 * s + k] = jnp.where(
-                        masks[s], spring[k], self.springs[3 * s + k]
-                    )
-
-        def partner(self, result):
-            force, twist, _ = result
-            for k in range(3):
-                self.total[k] = self.total[k] - force[k]
-                self.total[3 + k] = self.total[3 + k] + twist[k]
-
-        def store(self, rows, span):
-            for c in range(6):
-                level[c, rows, :] = level[c, rows, :] + self.total[c]
-            if span is not None:
-                for c in range(3 * SLOTS):
-                    state[9 + c, span, :] = state[9 + c, span, :] + self.springs[c]
-
-    def turned(values, amount, axis=1):
-        return [pltpu.roll(v, amount, axis) for v in values]
-
-    def masks_of(span, number):
-        return [cells[CODES + s, span, :] == float(number) for s in range(SLOTS)]
-
+    for x in range(8):
+        rows = pl.ds(plane(x), 8)
+        for c in range(6):
+            up = jnp.where(lane == 0, 0.0, pltpu.roll(rising[c, rows, :], 1, 1))
+            down = jnp.where(lane == 127, 0.0, pltpu.roll(falling[c, rows, :], 127, 1))
+            level[c, rows, :] = level[c, rows, :] + up + down
+
+
+def x_pairs(cells, state, pad, level, behind, ahead, xlo, xhi, edges, packs, xrow):
+    lane = lanes()
     for c in range(FIELDS + 4 * len(ALONG_X)):
         behind[c, 8:16, :] = xlo[c]
     for c in range(FIELDS):
@@ -462,8 +486,8 @@
         at = FIELDS + 4 * n
         shear = [xrow[at + k] for k in range(3)]
         result = pair(first, second, DIRS[number], shear, xrow[at + 3] > 0.5)
-        sums.own(result, masks_of(pl.ds(56, 8), number))
-    sums.store(pl.ds(plane(7), 8), pl.ds(56, 8))
+        sums.own(result, masks_of(cells, pl.ds(56, 8), number))
+    sums.store(level, pl.ds(plane(7), 8), state, pl.ds(56, 8))
     sums = Sums()
     second = [pad[c, pl.ds(plane(0), 8), :] for c in range(FIELDS)]
     for n, number in enumerate(ALONG_X):
@@ -477,8 +501,12 @@
         if dz:
             live = jnp.logical_and(live, lane != (0 if dz > 0 else 127))
         sums.partner(pair(first[:10], second, DIRS[number], first[10:13], live))
-    sums.store(pl.ds(plane(0), 8), None)
-
+    sums.store(level, pl.ds(plane(0), 8), state, None)
+
+
+def y_pairs(cells, state, pad, level, ylo, yhi, ytop, ylow):
+    lane = lanes()
+    sub = lax.broadcasted_iota(jnp.int32, (8, 128), 0)
     top_fields = scaled([yhi[c] for c in range(FIELDS)])
     low_fields = scaled([ylo[c] for c in range(FIELDS)])
     sums = Sums()
@@ -497,11 +525,11 @@
             second = turned(second, -dz % 128)
             live = jnp.logical_and(live, lane != (127 if dz > 0 else 0))
         shear = [ytop[at + k] for k in range(3)]
-        sums.own(pair(mine, second, DIRS[number], shear, live), masks_of(span, number))
+        sums.own(pair(mine, second, DIRS[number], shear, live), masks_of(cells, span, number))
     first = turned(top_fields + [yhi[FIELDS + k] for k in range(4)], 1, 0)
     live = jnp.logical_and(first[13] > 0.5, sub != 0)
     sums.partner(pair(first[:10], mine, DIRS[4], first[10:13], live))
-    sums.store(mine_rows, span)
+    sums.store(level, mine_rows, state, span)
 
     sums = Sums()
     mine_rows = pl.ds(plane(0), 8, stride=ROWS)
@@ -510,7 +538,7 @@
     second = turned(low_fields, 7, 0)
     live = jnp.logical_and(ylow[FIELDS + 3] > 0.5, sub != 7)
     shear = [ylow[FIELDS + k] for k in range(3)]
-    sums.own(pair(mine, second, DIRS[4], shear, live), masks_of(span, 4))
+    sums.own(pair(mine, second, DIRS[4], shear, live), masks_of(cells, span, 4))
     for n, number in enumerate(UP_Y):
         dx, dy, dz = DIRS[number]
         first = low_fields + [ylo[FIELDS + 4 * n + k] for k in range(4)]
@@ -524,93 +552,118 @@
         if dz:
             live = jnp.logical_and(live, lane != (0 if dz > 0 else 127))
         sums.partner(pair(first[:10], mine, DIRS[number], first[10:13], live))
-    sums.store(mine_rows, span)
-
-    def spread(pack, c, top):
-        p = (c % 16) * 8 - top
-        return pltpu.roll(pack, (128 - p) % 128, 1) if p % 128 else pack
-
-    ends = []
-    for end, theirs, ours in ((0, (2, 5, 7), (6, 8)), (1, (6, 8), (2, 5, 7))):
-        top = 1 - end
-        for k in range(PACKS):
-            straight, back, left = packs[end, k], packs[2 + end, k], packs[6 + end, k]
-            for c in range(16 * k, min(FULL, 16 * k + 16)):
-                before = pltpu.roll(spread(back, c, top), 120, 1)
-                zside[end, c, 8:16, :] = jnp.where(lane == 127, before, spread(straight, c, top))
-                zside[end, c, 0:8, :] = spread(left, c, top)
-                if c < FIELDS:
-                    zside[end, c, 16:24, :] = spread(packs[8 + end, 0], c, top)
-        own = [spread(own_packs[end, c // 16], c, end) for c in range(FULL)]
-        mine = scaled(own[:FIELDS])
-        sums = Sums()
-        for number, (shear, live, masks) in zip(ours, pick_shear(lambda c: own[c], ours)):
-            dx, dy, dz = DIRS[number]
-            second = scaled([zside[end, c, pl.ds(8 + dy, 8), :] for c in range(FIELDS)])
-            if dx:
-                second = [jnp.where(lane < 7, v, 0.0) for v in turned(second, 127)]
-            sums.own(pair(mine, second, DIRS[number], shear, live), masks)
-        for number in theirs:
-            dx, dy, dz = DIRS[number]
-            span = pl.ds(8 - dy, 8)
-            first = scaled([zside[end, c, span, :] for c in range(FIELDS)])
-            ((shear, live, _),) = pick_shear(lambda c: zside[end, c, span, :], (number,))
-            first = first + shear + [jnp.where(live, 1.0, 0.0)]
-            if dx:
-                first = turned(first, 1)
-            sums.partner(pair(first[:10], mine, DIRS[number], first[10:13], first[13] > 0.5))
-        ends.append(sums.total + sums.springs)
-    return ends
-
-
-def finish(cells, state, leaving, outbox, level, rising, falling, ends):
+    sums.store(level, mine_rows, state, span)
+
+
+def end_pairs(end, level, state, zside, packs, own_packs):
+    lane = lanes()
+    theirs, ours = (((2, 5, 7), (6, 8)), ((6, 8), (2, 5, 7)))[end]
+    top = 1 - end
+
+    def spread(pack, c, top, at=0):
+        p = (c % 16) * 8 - top - at
+        return pltpu.roll(pack, -p % 128, 1) if p % 128 else pack
+
+    for k in range(PACKS):
+        straight, back, left = packs[end, k], packs[2 + end, k], packs[6 + end, k]
+        for c in range(16 * k, min(FULL, 16 * k + 16)):
+            zside[end, c, 8:16, :] = jnp.where(
+                lane == 127, spread(back, c, top, 120), spread(straight, c, top)
+            )
+            zside[end, c, 0:8, :] = spread(left, c, top)
+            if c < FIELDS:
+                zside[end, c, 16:24, :] = spread(packs[8 + end, 0], c, top)
+    own = [spread(own_packs[end, c // 16], c, end) for c in range(FULL)]
+    mine = scaled(own[:FIELDS])
+    sums = Sums()
+    for number, (shear, live, masks) in zip(ours, pick_shear(lambda c: own[c], ours)):
+        dx, dy, dz = DIRS[number]
+        second = scaled([zside[end, c, pl.ds(8 + dy, 8), :] for c in range(FIELDS)])
+        if dx:
+            second = [jnp.where(lane < 7, v, 0.0) for v in turned(second, 127)]
+        sums.own(pair(mine, second, DIRS[number], shear, live), masks)
+    for number in theirs:
+        dx, dy, dz = DIRS[number]
+        span = pl.ds(8 - dy, 8)
+        first = scaled([zside[end, c, span, :] for c in range(FIELDS)])
+        ((shear, live, _),) = pick_shear(lambda c: zside[end, c, span, :], (number,))
+        first = first + shear + [jnp.where(live, 1.0, 0.0)]
+        if dx:
+            first = turned(first, 1)
+        sums.partner(pair(first[:10], mine, DIRS[number], first[10:13], first[13] > 0.5))
+    edge = 127 * end
+    hold = lane == edge
+    for x in range(8):
+        turn = (edge - x) % 128
+
+        def put(v):
+            return jnp.where(hold, pltpu.roll(v, turn, 1) if turn else v, 0.0)
+
+        rows = pl.ds(plane(x), 8)
+        here = slice(x * 8, x * 8 + 8)
+        for c in range(6):
+            level[c, rows, :] = level[c, rows, :] + put(sums.total[c])
+        for c in range(3 * SLOTS):
+            state[9 + c, here, :] = state[9 + c, here, :] + put(sums.springs[c])
+
+
+def moved(cells, level, x):
+    rows = pl.ds(plane(x), 8)
+    here = slice(x * 8, x * 8 + 8)
+    sums = [level[c, rows, :] for c in range(6)]
+    radius = cells[9, here, :]
+    inverse = 1.0 / radius
+    push = STEP * inverse * inverse * inverse
+    turn = 0.125 * (inverse * inverse) * (inverse * inverse)
+    velocity = [cells[3 + k, here, :] + push * sums[k] for k in range(3)]
+    velocity[2] = velocity[2] - STEP
+    offset = [cells[k, here, :] + STEP * velocity[k] for k in range(3)]
+    rotation = [cells[6 + k, here, :] + turn * sums[3 + k] for k in range(3)]
+    return offset, velocity, rotation, radius
+
+
+def fill_outbox(cells, state, leaving, outbox, level):
     lane = lanes()
     sub = lax.broadcasted_iota(jnp.int32, (8, 128), 0)
-    wide = jnp.broadcast_to(leaving[0:1, 0:64], (8, 64))
-    deep = lax.broadcasted_iota(jnp.int32, (8, 64), 0)
+    names = leaving[0:1, 0:64]
+    names = jnp.concatenate([names, jnp.full((1, 64), -1, jnp.int32)], axis=1)
+    names = jnp.broadcast_to(names, (8, 128))
+    height = jnp.where(names >= 0, names % 128, 0)
+    column = jnp.where(names >= 0, names // 128, -1)
     starts = [(lax.axis_index(a) * n).astype(jnp.float32) for a, n in zip(AXES, (8, 8, 128))]
-    boxes = [jnp.zeros((8, 64), jnp.float32) for _ in range(28)]
+    boxes = [jnp.zeros((8, 128), jnp.float32) for _ in range(28)]
     for x in range(8):
-        rows = pl.ds(plane(x), 8)
         here = slice(x * 8, x * 8 + 8)
-
-        def at_ends(c):
-            low, top = ends[0][c], ends[1][c]
-            low = pltpu.roll(low, 128 - x, 1) if x else low
-            return jnp.where(
-                lane == 0, low, jnp.where(lane == 127, pltpu.roll(top, 127 - x, 1), 0.0)
-            )
-
-        sums = []
-        for c in range(6):
-            up = jnp.where(lane == 0, 0.0, pltpu.roll(rising[c, rows, :], 1, 1))
-            down = jnp.where(lane == 127, 0.0, pltpu.roll(falling[c, rows, :], 127, 1))
-            sums.append(level[c, rows, :] + up + down + at_ends(c))
-        radius = cells[9, here, :]
-        inverse = 1.0 / radius
-        push = STEP * inverse * inverse * inverse
-        turn = 0.125 * (inverse * inverse) * (inverse * inverse)
-        velocity = [cells[3 + k, here, :] + push * sums[k] for k in range(3)]
-        velocity[2] = velocity[2] - STEP
-        offset = [cells[k, here, :] + STEP * velocity[k] for k in range(3)]
-        rotation = [cells[6 + k, here, :] + turn * sums[3 + k] for k in range(3)]
-        springs = [state[9 + c, here, :] + at_ends(6 + c) for c in range(3 * SLOTS)]
-        bottom = [wide == (x * 8 + deep) * 128 + z for z in range(2)]
-        left = [jnp.max(jnp.where(b, 1.0, 0.0), axis=1, keepdims=True) for b in bottom]
-        staying = 1.0 - jnp.where(lane == 0, left[0], jnp.where(lane == 1, left[1], 0.0))
+        offset, velocity, rotation, radius = moved(cells, level, x)
+        springs = [state[9 + c, here, :] for c in range(3 * SLOTS)]
         position = [
             offset[0] + (starts[0] + float(x)),
             offset[1] + (starts[1] + sub.astype(jnp.float32)),
             offset[2] + (starts[2] + lane.astype(jnp.float32)),
         ]
+        chosen = column == x * 8 + sub
         for c, v in enumerate(position + velocity + rotation + [radius] + springs):
-            for z in range(2):
-                value = jnp.broadcast_to(v[:, z : z + 1], (8, 64))
-                boxes[c] = boxes[c] + jnp.where(bottom[z], value, 0.0)
-        for c, v in enumerate(offset + velocity + rotation + springs):
+            boxes[c] = jnp.where(chosen, jnp.take_along_axis(v, height, axis=1), boxes[c])
+    for c in range(28):
+        outbox[c : c + 1, :] = jnp.sum(boxes[c], axis=0, keepdims=True)
+
+
+def finish(cells, state, leaving, level):
+    lane = lanes()
+    wide = jnp.broadcast_to(leaving[0:1, 0:64], (8, 64))
+    deep = lax.broadcasted_iota(jnp.int32, (8, 64), 0)
+    for x in range(8):
+        here = slice(x * 8, x * 8 + 8)
+        offset, velocity, rotation, _ = moved(cells, level, x)
+        left = [
+            jnp.max(jnp.where(wide == (x * 8 + deep) * 128 + z, 1.0, 0.0), axis=1, keepdims=True)
+            for z in range(2)
+        ]
+        staying = 1.0 - jnp.where(lane == 0, left[0], jnp.where(lane == 1, left[1], 0.0))
+        for c, v in enumerate(offset + velocity + rotation):
             state[c, here, :] = v * staying
-    for c in range(28):
-        outbox[c : c + 1, 0:64] = jnp.sum(boxes[c], axis=0, keepdims=True)
+        for c in range(9, 27):
+            state[c, here, :] = state[c, here, :] * staying
 
 
 def on_device(offset, velocity, spin, radius, history, contacts, leaving):

time: 19.3 us -> 16 us (0.83)
  the two profiles are of different devices: /device:TPU:1 before, /device:TPU:34 now
where the time goes in v4:
time: 16 us; the launch traced here: 15.9 us
  Pallas kernels  15.2 us (95%)
  between operations  0.64 us (4%)
    pallas_call x1, Pallas kernels, on_device(): pl.pallas_call(step_kernel, out_shape=[pltpu.VMEM((27, 64, 128), f32), pl...  13.7 us
    pallas_call x1, Pallas kernels, on_device(): pl.pallas_call(write_kernel, out_shape=[moved, moved, moved, jax.ShapeDty...  1.54 us

profile of v4, /device:TPU:34, one launch (start us, length us, event | category | flops | bytes accessed | tf_op | source)
XLA Modules:
  0.0 15.9 jit_solution(15792116612062198444)
XLA Ops:
  0.6 13.7 %step.1 = (f32[27,64,128]{2,1,0:T(8,128)S(1)}, f32[32,128]{1,0:T(8,128)S(1)}) custom-call(f32[3,64,128]{2,1,0:T(8,128)} %bitcast.16, f32[3,64,128]{2,1,0:T(8,128)} %bitcast.17, f32[3,64,128]{2,1,0:T(8,128)} %bitcast.18, f32[1,64,128]{2,1,0:T(8,128)} %bitcast.19, f32[18,64,128]{2,1,0:T(8,128)} %bitcast.14, s32[6,64,128]{2,1,0:T(8,128)} %bitcast.15, ...), custom_call_target="tpu_custom_call" | custom-call | tf_op jit(solution)/shard_map/step/pallas_call | solution.py:688
  14.3 1.5 %write.1 = (f32[3,64,128]{2,1,0:T(8,128)}, f32[3,64,128]{2,1,0:T(8,128)}, f32[3,64,128]{2,1,0:T(8,128)}, f32[18,64,128]{2,1,0:T(8,128)}, f32[28,1,64]{2,1,0:T(1,128)}) custom-call(f32[27,64,128]{2,1,0:T(8,128)S(1)} %get-tuple-element.12.state, f32[32,128]{1,0:T(8,128)S(1)} %get-tuple-element.13.arrivals), custom_call_target="tpu_custom_call" | custom-call | tf_op jit(solution)/shard_map/write/pallas_call | solution.py:725

commit v5 on v4

--- a/solution.py
+++ b/solution.py
@@ -69,8 +69,7 @@
     off_hbm, vel_hbm, spin_hbm, rad_hbm, hist_hbm, con_hbm, leaving_hbm,
     state, arrivals,
     xlo, xhi, ylo, yhi, edges, packs, own_packs, cells, codes, leaving,
-    xrow, ytop, ylow, rows, outbox,
-    pad, pad_up, pad_down, level, rising, falling, behind, ahead, zside,
+    xrow, ytop, ylow, rows, corner_x, corner_y, outbox, pad, pad_up, pad_down, level, rising, falling, behind, ahead, zside,
     local_sems, send_sems, recv_sems,
 ):
     here = [lax.axis_index(a) for a in AXES]
@@ -110,20 +109,31 @@
             pl.semaphore_signal(barrier, inc=1, device_id=place(step), device_id_type=MESH)
 
     with jax.named_scope("loadwait"):
-        for load in loads:
+        for load in loads[:4]:
             load.wait()
     with jax.named_scope("pack"):
+        first_pack = fill_fields(cells, xrow, ytop, ylow, rows)
+    with jax.named_scope("loadwait2"):
+        for load in loads[4:]:
+            load.wait()
+    with jax.named_scope("pack2"):
         for s in range(SLOTS):
             cells[CODES + s] = codes[s].astype(jnp.float32)
-        fill_sends(cells, own_packs, xrow, ytop, ylow, rows)
+        fill_sends(cells, own_packs, xrow, ytop, ylow, rows, corner_x, corner_y, first_pack)
 
     targets = [xlo, xhi, ylo, yhi] + [edges.at[k] for k in range(4)]
     sources = [xrow, cells.at[0:FIELDS, 0:8, :], ytop, ylow] + [rows.at[k] for k in range(4)]
     for k, s in enumerate(PACK_FROM):
-        own = own_packs.at[0 if s[2] > 0 else 1]
-        fields_only = s[0] + s[1] > 0
-        targets.append(packs.at[k, 0:1] if fields_only else packs.at[k])
-        sources.append(own.at[0:1] if fields_only else own)
+        end = 0 if s[2] > 0 else 1
+        if s[0] + s[1] == 0:
+            targets.append(packs.at[k])
+            sources.append(own_packs.at[end])
+            continue
+        targets.append(packs.at[k, 0:1])
+        if s[0] + s[1] > 0:
+            sources.append(own_packs.at[end, 0:1])
+        else:
+            sources.append((corner_x if s[0] else corner_y).at[end])
 
     def copy(k):
         to = tuple(-s for s in SENDERS[k])
@@ -219,17 +229,22 @@
         fall.wait_send()
 
 
-def write_kernel(state, arrivals, new_off, new_vel, new_spin, new_hist, entered, sems):
+def write_kernel(
+    state, arrivals, new_off, new_vel, new_spin, new_hist, entered, unpacked, sems
+):
     copies = [
         pltpu.make_async_copy(state.at[9:27], new_hist, sems.at[0]),
         pltpu.make_async_copy(state.at[0:3], new_off, sems.at[1]),
         pltpu.make_async_copy(state.at[3:6], new_vel, sems.at[2]),
         pltpu.make_async_copy(state.at[6:9], new_spin, sems.at[3]),
+        pltpu.make_async_copy(unpacked, entered, sems.at[4]),
     ]
-    for copy in copies:
+    for copy in copies[:4]:
         copy.start()
-    for c in range(28):
-        entered[c] = arrivals[c : c + 1, 0:64]
+    for c in range(14):
+        unpacked[c] = arrivals[c : c + 1, 0:64]
+        unpacked[14 + c] = arrivals[c : c + 1, 64:128]
+    copies[4].start()
     for copy in copies:
         copy.wait()
 
@@ -297,12 +312,32 @@
     return lax.broadcasted_iota(jnp.int32, (8, 128), 1)
 
 
-def fill_sends(cells, own_packs, xrow, ytop, ylow, rows):
+def add_packed(cells, channels, low, top):
     lane = lanes()
+    for c in channels:
+        for x in range(8):
+            p = (c % 16) * 8 + x
+            value = cells[c, x * 8 : x * 8 + 8, :]
+            if p:
+                value = pltpu.roll(value, p, 1)
+            low = jnp.where(lane == p, value, low)
+            top = jnp.where(lane == (p - 1) % 128, value, top)
+    return low, top
+
+
+def fill_fields(cells, xrow, ytop, ylow, rows):
     for c in range(FIELDS):
         xrow[c] = cells[c, 56:64, :]
         ytop[c] = cells[c, pl.ds(7, 8, stride=8), :]
         ylow[c] = cells[c, pl.ds(0, 8, stride=8), :]
+        for which, row in enumerate((63, 56, 7, 0)):
+            rows[which, c : c + 1, :] = cells[c, row : row + 1, :]
+    zero = jnp.zeros((8, 128), jnp.float32)
+    return add_packed(cells, range(FIELDS), zero, zero)
+
+
+def fill_sends(cells, own_packs, xrow, ytop, ylow, rows, corner_x, corner_y, first_pack):
+    lane = lanes()
     for target, span, numbers in (
         (xrow, pl.ds(56, 8), ALONG_X),
         (ytop, pl.ds(7, 8, stride=8), UP_Y),
@@ -314,28 +349,29 @@
                 target[FIELDS + 4 * n + k] = shear[k]
             target[FIELDS + 4 * n + 3] = jnp.where(live, 1.0, 0.0)
     for which, row, at in ((0, 7, 1), (1, 0, 2)):
-        for c in range(FIELDS):
-            rows[which, c : c + 1, :] = xrow[c, row : row + 1, :]
         for k in range(4):
             rows[which, FIELDS + k : FIELDS + k + 1, :] = xrow[
                 FIELDS + 4 * at + k, row : row + 1, :
             ]
-    for which, row in ((2, 7), (3, 0)):
-        for c in range(FIELDS):
-            rows[which, c : c + 1, :] = cells[c, row : row + 1, :]
+    for end, at in ((0, 4), (1, 3)):
+        corner = jnp.zeros((8, 128), jnp.float32)
+        for j in range(FIELDS + 4):
+            value = xrow[j if j < FIELDS else j + 4 * at]
+            turn = j + end
+            corner = jnp.where(lane == j, pltpu.roll(value, turn, 1) if turn else value, corner)
+        corner_x[end, 0] = corner
     for k in range(PACKS):
-        low = jnp.zeros((8, 128), jnp.float32)
-        top = jnp.zeros((8, 128), jnp.float32)
-        for c in range(k * 16, min(FULL, k * 16 + 16)):
-            for x in range(8):
-                p = (c % 16) * 8 + x
-                value = cells[c, x * 8 : x * 8 + 8, :]
-                if p:
-                    value = pltpu.roll(value, p, 1)
-                low = jnp.where(lane == p, value, low)
-                top = jnp.where(lane == (p - 1) % 128, value, top)
-        own_packs[0, k] = low
-        own_packs[1, k] = top
+        if k:
+            low = top = jnp.zeros((8, 128), jnp.float32)
+        else:
+            low, top = first_pack
+        channels = range(max(16 * k, FIELDS), min(FULL, 16 * k + 16))
+        low, top = add_packed(cells, channels, low, top)
+        for end, pack in enumerate((low, top)):
+            own_packs[end, k] = pack
+            corner_y[end, 0, k : k + 1, :] = pack[7:8, :]
+    for end in range(2):
+        corner_y[end, 0, PACKS:8, :] = jnp.zeros((8 - PACKS, 128), jnp.float32)
 
 
 def inner_pairs(cells, state, pad, pad_up, pad_down, level, rising, falling):
@@ -560,16 +596,19 @@
     theirs, ours = (((2, 5, 7), (6, 8)), ((6, 8), (2, 5, 7)))[end]
     top = 1 - end
 
-    def spread(pack, c, top, at=0):
-        p = (c % 16) * 8 - top - at
+    def spread(pack, c, top):
+        p = (c % 16) * 8 - top
         return pltpu.roll(pack, -p % 128, 1) if p % 128 else pack
 
+    back = [
+        pltpu.roll(packs[2 + end, 0], -j % 128, 1) if j else packs[2 + end, 0]
+        for j in range(FIELDS + 4)
+    ]
+    back = scaled(back[:FIELDS]) + back[FIELDS:]
     for k in range(PACKS):
-        straight, back, left = packs[end, k], packs[2 + end, k], packs[6 + end, k]
+        straight, left = packs[end, k], pltpu.roll(packs[6 + end, 0], 7 - k, 0)
         for c in range(16 * k, min(FULL, 16 * k + 16)):
-            zside[end, c, 8:16, :] = jnp.where(
-                lane == 127, spread(back, c, top, 120), spread(straight, c, top)
-            )
+            zside[end, c, 8:16, :] = spread(straight, c, top)
             zside[end, c, 0:8, :] = spread(left, c, top)
             if c < FIELDS:
                 zside[end, c, 16:24, :] = spread(packs[8 + end, 0], c, top)
@@ -589,7 +628,7 @@
         ((shear, live, _),) = pick_shear(lambda c: zside[end, c, span, :], (number,))
         first = first + shear + [jnp.where(live, 1.0, 0.0)]
         if dx:
-            first = turned(first, 1)
+            first = [jnp.where(lane == 0, b, v) for b, v in zip(back, turned(first, 1))]
         sums.partner(pair(first[:10], mine, DIRS[number], first[10:13], first[13] > 0.5))
     edge = 127 * end
     hold = lane == edge
@@ -626,12 +665,12 @@
     lane = lanes()
     sub = lax.broadcasted_iota(jnp.int32, (8, 128), 0)
     names = leaving[0:1, 0:64]
-    names = jnp.concatenate([names, jnp.full((1, 64), -1, jnp.int32)], axis=1)
+    names = jnp.concatenate([names, names], axis=1)
     names = jnp.broadcast_to(names, (8, 128))
     height = jnp.where(names >= 0, names % 128, 0)
     column = jnp.where(names >= 0, names // 128, -1)
     starts = [(lax.axis_index(a) * n).astype(jnp.float32) for a, n in zip(AXES, (8, 8, 128))]
-    boxes = [jnp.zeros((8, 128), jnp.float32) for _ in range(28)]
+    boxes = [jnp.zeros((8, 128), jnp.float32) for _ in range(14)]
     for x in range(8):
         here = slice(x * 8, x * 8 + 8)
         offset, velocity, rotation, radius = moved(cells, level, x)
@@ -642,9 +681,11 @@
             offset[2] + (starts[2] + lane.astype(jnp.float32)),
         ]
         chosen = column == x * 8 + sub
+        halves = [jnp.logical_and(chosen, lane < 64), jnp.logical_and(chosen, lane >= 64)]
         for c, v in enumerate(position + velocity + rotation + [radius] + springs):
-            boxes[c] = jnp.where(chosen, jnp.take_along_axis(v, height, axis=1), boxes[c])
-    for c in range(28):
+            values = jnp.take_along_axis(v, height, axis=1)
+            boxes[c % 14] = jnp.where(halves[c // 14], values, boxes[c % 14])
+    for c in range(14):
         outbox[c : c + 1, :] = jnp.sum(boxes[c], axis=0, keepdims=True)
 
 
@@ -687,7 +728,7 @@
     )
     state, arrivals = pl.pallas_call(
         step_kernel,
-        out_shape=[pltpu.VMEM((27, 64, 128), f32), pltpu.VMEM((32, 128), f32)],
+        out_shape=[pltpu.VMEM((27, 64, 128), f32), pltpu.VMEM((16, 128), f32)],
         in_specs=[hbm] * 7,
         out_specs=[vmem] * 2,
         scratch_shapes=[pltpu.VMEM(s, f32) for s in halo_shapes]
@@ -699,7 +740,9 @@
             pltpu.VMEM((FIELDS + 4 * len(UP_Y), 8, 128), f32),
             pltpu.VMEM((FIELDS + 4 * len(DOWN_Y), 8, 128), f32),
             pltpu.VMEM((4, 16, 128), f32),
-            pltpu.VMEM((32, 128), f32),
+            pltpu.VMEM((2, 1, 8, 128), f32),
+            pltpu.VMEM((2, 1, 8, 128), f32),
+            pltpu.VMEM((16, 128), f32),
             pltpu.VMEM((FIELDS, HEIGHT, 128), f32),
             pltpu.VMEM((FIELDS, HEIGHT, 128), f32),
             pltpu.VMEM((FIELDS, HEIGHT, 128), f32),
@@ -730,8 +773,8 @@
             jax.ShapeDtypeStruct((28, 1, 64), f32),
         ],
         in_specs=[vmem] * 2,
-        out_specs=[hbm] * 4 + [vmem],
-        scratch_shapes=[pltpu.SemaphoreType.DMA((4,))],
+        out_specs=[hbm] * 5,
+        scratch_shapes=[pltpu.VMEM((28, 1, 64), f32), pltpu.SemaphoreType.DMA((5,))],
         compiler_params=pltpu.CompilerParams(vmem_limit_bytes=8 << 20),
         name="write",
     )(state, arrivals)

time: 16 us -> 14.6 us (0.912)
  the two profiles are of different devices: /device:TPU:34 before, /device:TPU:1 now
where the time goes in v5:
time: 14.6 us; the launch traced here: 14.5 us
  Pallas kernels  13.9 us (95%)
  between operations  0.64 us (4%)
    pallas_call x1, Pallas kernels, on_device(): pl.pallas_call(step_kernel, out_shape=[pltpu.VMEM((27, 64, 128), f32), pl...  12.9 us
    pallas_call x1, Pallas kernels, on_device(): pl.pallas_call(write_kernel, out_shape=[moved, moved, moved, jax.ShapeDty...  0.95 us

profile of v5, /device:TPU:1, one launch (start us, length us, event | category | flops | bytes accessed | tf_op | source)
XLA Modules:
  0.0 14.5 jit_solution(4675065851885222466)
XLA Ops:
  0.6 12.9 %step.1 = (f32[27,64,128]{2,1,0:T(8,128)S(1)}, f32[16,128]{1,0:T(8,128)S(1)}) custom-call(f32[3,64,128]{2,1,0:T(8,128)} %bitcast.16, f32[3,64,128]{2,1,0:T(8,128)} %bitcast.17, f32[3,64,128]{2,1,0:T(8,128)} %bitcast.18, f32[1,64,128]{2,1,0:T(8,128)} %bitcast.19, f32[18,64,128]{2,1,0:T(8,128)} %bitcast.14, s32[6,64,128]{2,1,0:T(8,128)} %bitcast.15, ...), custom_call_target="tpu_custom_call" | custom-call | tf_op jit(solution)/shard_map/step/pallas_call | solution.py:729
  13.5 1.0 %write.1 = (f32[3,64,128]{2,1,0:T(8,128)}, f32[3,64,128]{2,1,0:T(8,128)}, f32[3,64,128]{2,1,0:T(8,128)}, f32[18,64,128]{2,1,0:T(8,128)}, f32[28,1,64]{2,1,0:T(1,128)}) custom-call(f32[27,64,128]{2,1,0:T(8,128)S(1)} %get-tuple-element.12.state, f32[16,128]{1,0:T(8,128)S(1)} %get-tuple-element.13.arrivals), custom_call_target="tpu_custom_call" | custom-call | tf_op jit(solution)/shard_map/write/pallas_call | solution.py:768

commit v6 on v5

--- a/solution.py
+++ b/solution.py
@@ -58,19 +58,27 @@
 UP_Y = (1, 3, 7, 8)
 DOWN_Y = (4,)
 
-SEND_ORDER = (8, 9, 14, 15, 16, 17, 10, 11, 12, 13, 4, 5, 6, 7, 2, 3, 0, 1)
+SEND_ORDER = (10, 12, 14, 16, 4, 5, 6, 7, 8, 2, 0, 3, 1, 11, 13, 15, 17, 9)
 
 
 def plane(x):
     return (x + 1) * ROWS + 8
 
 
-def step_kernel(
+def step_kernel(*refs):
+    pl.run_scoped(
+        lambda local_sems, send_sems: step_body(*refs, local_sems, send_sems),
+        pltpu.SemaphoreType.DMA((7,)),
+        pltpu.SemaphoreType.DMA((len(SENDERS) + 1,)),
+    )
+
+
+def step_body(
     off_hbm, vel_hbm, spin_hbm, rad_hbm, hist_hbm, con_hbm, leaving_hbm,
     state, arrivals,
     xlo, xhi, ylo, yhi, edges, packs, own_packs, cells, codes, leaving,
     xrow, ytop, ylow, rows, corner_x, corner_y, outbox, pad, pad_up, pad_down, level, rising, falling, behind, ahead, zside,
-    local_sems, send_sems, recv_sems,
+    recv_sems, local_sems, send_sems,
 ):
     here = [lax.axis_index(a) for a in AXES]
     size = [lax.axis_size(a) for a in AXES]
@@ -96,11 +104,9 @@
         pltpu.make_async_copy(con_hbm, codes, local_sems.at[5]),
         pltpu.make_async_copy(leaving_hbm, leaving, local_sems.at[6]),
     ]
-    for load in loads:
-        load.start()
     barrier = pltpu.get_barrier_semaphore()
     expected = jnp.int32(0)
-    for step in SENDERS:
+    for step in SENDERS[4:] + SENDERS[:4]:
         there = exists(step)
         expected = expected + there.astype(jnp.int32)
 
@@ -108,6 +114,8 @@
         def _():
             pl.semaphore_signal(barrier, inc=1, device_id=place(step), device_id_type=MESH)
 
+    for load in loads:
+        load.start()
     with jax.named_scope("loadwait"):
         for load in loads[:4]:
             load.wait()
@@ -179,13 +187,20 @@
     with jax.named_scope("recvy"):
         receive((2, 3))
     with jax.named_scope("ypairs"):
-        y_pairs(cells, state, pad, level, ylo, yhi, ytop, ylow)
+        y_high(cells, state, pad, level, yhi, ytop)
+        y_low(cells, state, pad, level, ylo, ylow)
+    with jax.named_scope("outbox"):
+        boxes = [jnp.zeros((8, 128), jnp.float32)] * 14
+        boxes = gather_leaving(boxes, range(1, 7), cells, state, leaving, level)
     with jax.named_scope("recvx"):
-        receive((0, 1, 4, 5, 6, 7, 13))
+        receive((0, 1, 4, 5, 6, 7))
     with jax.named_scope("xpairs"):
-        x_pairs(cells, state, pad, level, behind, ahead, xlo, xhi, edges, packs, xrow)
-    with jax.named_scope("outbox"):
-        fill_outbox(cells, state, leaving, outbox, level)
+        x_ahead(cells, state, pad, level, ahead, xhi, edges, xrow)
+        x_behind(pad, level, behind, xlo, edges)
+    with jax.named_scope("outbox2"):
+        boxes = gather_leaving(boxes, (0, 7), cells, state, leaving, level)
+        for c in range(14):
+            outbox[c : c + 1, :] = jnp.sum(boxes[c], axis=0, keepdims=True)
 
     last = len(SENDERS)
     fall = pltpu.make_async_remote_copy(
@@ -202,7 +217,7 @@
         fall.start()
 
     with jax.named_scope("recvtop"):
-        receive((9, 11, 15, 17))
+        receive((9, 11, 13, 15, 17))
     with jax.named_scope("ceiling"):
         end_pairs(1, level, state, zside, packs, own_packs)
     with jax.named_scope("final"):
@@ -477,53 +492,38 @@
             level[c, rows, :] = level[c, rows, :] + up + down
 
 
-def x_pairs(cells, state, pad, level, behind, ahead, xlo, xhi, edges, packs, xrow):
+def x_ahead(cells, state, pad, level, ahead, xhi, edges, xrow):
+    lane = lanes()
+    for c in range(FIELDS):
+        ahead[c, 7:8, :] = edges[2, c : c + 1, :]
+        ahead[c, 16:17, :] = edges[3, c : c + 1, :]
+        ahead[c, 8:16, :] = xhi[c]
+
+    sums = Sums()
+    first = [pad[c, pl.ds(plane(7), 8), :] for c in range(FIELDS)]
+    for n, number in enumerate(ALONG_X):
+        dx, dy, dz = DIRS[number]
+        second = scaled([ahead[c, pl.ds(8 + dy, 8), :] for c in range(FIELDS)])
+        if dz:
+            edge = 127 if dz > 0 else 0
+            second = [jnp.where(lane == edge, 0.0, v) for v in turned(second, -dz % 128)]
+        at = FIELDS + 4 * n
+        shear = [xrow[at + k] for k in range(3)]
+        result = pair(first, second, DIRS[number], shear, xrow[at + 3] > 0.5)
+        sums.own(result, masks_of(cells, pl.ds(56, 8), number))
+    sums.store(level, pl.ds(plane(7), 8), state, pl.ds(56, 8))
+
+
+def x_behind(pad, level, behind, xlo, edges):
     lane = lanes()
     for c in range(FIELDS + 4 * len(ALONG_X)):
         behind[c, 8:16, :] = xlo[c]
     for c in range(FIELDS):
         behind[c, 7:8, :] = edges[0, c : c + 1, :]
         behind[c, 16:17, :] = edges[1, c : c + 1, :]
-        ahead[c, 7:8, :] = edges[2, c : c + 1, :]
-        ahead[c, 16:17, :] = edges[3, c : c + 1, :]
-        ahead[c, 8:16, :] = xhi[c]
     for k in range(4):
         behind[FIELDS + 4 + k, 7:8, :] = edges[0, FIELDS + k : FIELDS + k + 1, :]
         behind[FIELDS + 8 + k, 16:17, :] = edges[1, FIELDS + k : FIELDS + k + 1, :]
-
-    def pack_scaled(pack, top):
-        group = (lane + top) // 8
-        for c in (6, 7, 8):
-            radius = pltpu.roll(pack, 128 - 8 * (9 - c), 1)
-            pack = jnp.where(group == c, pack * radius, pack)
-        return pack
-
-    beyond_up = pack_scaled(packs[5, 0], 0)
-    beyond_down = pack_scaled(packs[4, 0], 1)
-    sums = Sums()
-    first = [pad[c, pl.ds(plane(7), 8), :] for c in range(FIELDS)]
-    for n, number in enumerate(ALONG_X):
-        dx, dy, dz = DIRS[number]
-        second = scaled([ahead[c, pl.ds(8 + dy, 8), :] for c in range(FIELDS)])
-        if dz > 0:
-            second = [
-                jnp.where(
-                    lane == 127, pltpu.roll(beyond_up, 127 - 8 * c, 1), pltpu.roll(v, 127, 1)
-                )
-                for c, v in enumerate(second)
-            ]
-        elif dz < 0:
-            second = [
-                jnp.where(
-                    lane == 0, pltpu.roll(beyond_down, (129 - 8 * c) % 128, 1), pltpu.roll(v, 1, 1)
-                )
-                for c, v in enumerate(second)
-            ]
-        at = FIELDS + 4 * n
-        shear = [xrow[at + k] for k in range(3)]
-        result = pair(first, second, DIRS[number], shear, xrow[at + 3] > 0.5)
-        sums.own(result, masks_of(cells, pl.ds(56, 8), number))
-    sums.store(level, pl.ds(plane(7), 8), state, pl.ds(56, 8))
     sums = Sums()
     second = [pad[c, pl.ds(plane(0), 8), :] for c in range(FIELDS)]
     for n, number in enumerate(ALONG_X):
@@ -537,14 +537,13 @@
         if dz:
             live = jnp.logical_and(live, lane != (0 if dz > 0 else 127))
         sums.partner(pair(first[:10], second, DIRS[number], first[10:13], live))
-    sums.store(level, pl.ds(plane(0), 8), state, None)
-
-
-def y_pairs(cells, state, pad, level, ylo, yhi, ytop, ylow):
+    sums.store(level, pl.ds(plane(0), 8), None, None)
+
+
+def y_high(cells, state, pad, level, yhi, ytop):
     lane = lanes()
     sub = lax.broadcasted_iota(jnp.int32, (8, 128), 0)
     top_fields = scaled([yhi[c] for c in range(FIELDS)])
-    low_fields = scaled([ylo[c] for c in range(FIELDS)])
     sums = Sums()
     mine_rows = pl.ds(plane(0) + 7, 8, stride=ROWS)
     span = pl.ds(7, 8, stride=8)
@@ -567,6 +566,11 @@
     sums.partner(pair(first[:10], mine, DIRS[4], first[10:13], live))
     sums.store(level, mine_rows, state, span)
 
+
+def y_low(cells, state, pad, level, ylo, ylow):
+    lane = lanes()
+    sub = lax.broadcasted_iota(jnp.int32, (8, 128), 0)
+    low_fields = scaled([ylo[c] for c in range(FIELDS)])
     sums = Sums()
     mine_rows = pl.ds(plane(0), 8, stride=ROWS)
     span = pl.ds(0, 8, stride=8)
@@ -605,6 +609,9 @@
         for j in range(FIELDS + 4)
     ]
     back = scaled(back[:FIELDS]) + back[FIELDS:]
+    beyond = scaled(
+        [pltpu.roll(packs[4 + end, 0], (7 - 8 * c + top) % 128, 1) for c in range(FIELDS)]
+    )
     for k in range(PACKS):
         straight, left = packs[end, k], pltpu.roll(packs[6 + end, 0], 7 - k, 0)
         for c in range(16 * k, min(FULL, 16 * k + 16)):
@@ -619,7 +626,10 @@
         dx, dy, dz = DIRS[number]
         second = scaled([zside[end, c, pl.ds(8 + dy, 8), :] for c in range(FIELDS)])
         if dx:
-            second = [jnp.where(lane < 7, v, 0.0) for v in turned(second, 127)]
+            second = [
+                jnp.where(lane < 7, v, jnp.where(lane == 7, b, 0.0))
+                for b, v in zip(beyond, turned(second, 127))
+            ]
         sums.own(pair(mine, second, DIRS[number], shear, live), masks)
     for number in theirs:
         dx, dy, dz = DIRS[number]
@@ -661,7 +671,8 @@
     return offset, velocity, rotation, radius
 
 
-def fill_outbox(cells, state, leaving, outbox, level):
+def gather_leaving(boxes, planes, cells, state, leaving, level):
+    boxes = list(boxes)
     lane = lanes()
     sub = lax.broadcasted_iota(jnp.int32, (8, 128), 0)
     names = leaving[0:1, 0:64]
@@ -670,8 +681,7 @@
     height = jnp.where(names >= 0, names % 128, 0)
     column = jnp.where(names >= 0, names // 128, -1)
     starts = [(lax.axis_index(a) * n).astype(jnp.float32) for a, n in zip(AXES, (8, 8, 128))]
-    boxes = [jnp.zeros((8, 128), jnp.float32) for _ in range(14)]
-    for x in range(8):
+    for x in planes:
         here = slice(x * 8, x * 8 + 8)
         offset, velocity, rotation, radius = moved(cells, level, x)
         springs = [state[9 + c, here, :] for c in range(3 * SLOTS)]
@@ -685,8 +695,7 @@
         for c, v in enumerate(position + velocity + rotation + [radius] + springs):
             values = jnp.take_along_axis(v, height, axis=1)
             boxes[c % 14] = jnp.where(halves[c // 14], values, boxes[c % 14])
-    for c in range(14):
-        outbox[c : c + 1, :] = jnp.sum(boxes[c], axis=0, keepdims=True)
+    return boxes
 
 
 def finish(cells, state, leaving, level):
@@ -752,8 +761,6 @@
             pltpu.VMEM((FIELDS + 4 * len(ALONG_X), ROWS, 128), f32),
             pltpu.VMEM((FIELDS, ROWS, 128), f32),
             pltpu.VMEM((2, FULL, ROWS, 128), f32),
-            pltpu.SemaphoreType.DMA((7,)),
-            pltpu.SemaphoreType.DMA((len(SENDERS) + 1,)),
             pltpu.SemaphoreType.DMA((len(SENDERS) + 1,)),
         ],
         compiler_params=pltpu.CompilerParams(

time: 14.6 us -> 13.8 us (0.945)
  Pallas kernels: 13.9 us -> 12.9 us
    pallas_call x1, Pallas kernels: 12.9 us -> 12 us  [on_device(): pl.pallas_call(step_kernel, out_shape=[pltpu.VMEM((27, 64, 128), f32), pl...]
where the time goes in v6:
time: 13.8 us; the launch traced here: 13.6 us
  Pallas kernels  12.9 us (93%)
  between operations  0.64 us (5%)
    pallas_call x1, Pallas kernels, on_device(): pl.pallas_call(step_kernel, out_shape=[pltpu.VMEM((27, 64, 128), f32), pl...  12 us
    pallas_call x1, Pallas kernels, on_device(): pl.pallas_call(write_kernel, out_shape=[moved, moved, moved, jax.ShapeDty...  0.95 us

profile of v6, /device:TPU:1, one launch (start us, length us, event | category | flops | bytes accessed | tf_op | source)
XLA Modules:
  0.0 13.6 jit_solution(7358271374063624770)
XLA Ops:
  0.6 12.0 %step.1 = (f32[27,64,128]{2,1,0:T(8,128)S(1)}, f32[16,128]{1,0:T(8,128)S(1)}) custom-call(f32[3,64,128]{2,1,0:T(8,128)} %bitcast.16, f32[3,64,128]{2,1,0:T(8,128)} %bitcast.17, f32[3,64,128]{2,1,0:T(8,128)} %bitcast.18, f32[1,64,128]{2,1,0:T(8,128)} %bitcast.19, f32[18,64,128]{2,1,0:T(8,128)} %bitcast.14, s32[6,64,128]{2,1,0:T(8,128)} %bitcast.15, ...), custom_call_target="tpu_custom_call" | custom-call | tf_op jit(solution)/shard_map/step/pallas_call | solution.py:738
  12.6 1.0 %write.1 = (f32[3,64,128]{2,1,0:T(8,128)}, f32[3,64,128]{2,1,0:T(8,128)}, f32[3,64,128]{2,1,0:T(8,128)}, f32[18,64,128]{2,1,0:T(8,128)}, f32[28,1,64]{2,1,0:T(1,128)}) custom-call(f32[27,64,128]{2,1,0:T(8,128)S(1)} %get-tuple-element.12.state, f32[16,128]{1,0:T(8,128)S(1)} %get-tuple-element.13.arrivals), custom_call_target="tpu_custom_call" | custom-call | tf_op jit(solution)/shard_map/write/pallas_call | solution.py:775

commit v7 on v6

--- a/solution.py
+++ b/solution.py
@@ -77,7 +77,7 @@
     off_hbm, vel_hbm, spin_hbm, rad_hbm, hist_hbm, con_hbm, leaving_hbm,
     state, arrivals,
     xlo, xhi, ylo, yhi, edges, packs, own_packs, cells, codes, leaving,
-    xrow, ytop, ylow, rows, corner_x, corner_y, outbox, pad, pad_up, pad_down, level, rising, falling, behind, ahead, zside,
+    xrow, ytop, ylow, rows, corner_x, corner_y, outbox, found, pad, pad_up, pad_down, level, rising, falling, behind, ahead, zside,
     recv_sems, local_sems, send_sems,
 ):
     here = [lax.axis_index(a) for a in AXES]
@@ -160,6 +160,8 @@
         def _():
             targets[k][...] = jnp.zeros(targets[k].shape, jnp.float32)
 
+    with jax.named_scope("fill"):
+        fill_padded(cells, pad, pad_up, pad_down, level, rising, falling)
     with jax.named_scope("barrier"):
         pl.semaphore_wait(barrier, expected)
     for k in SEND_ORDER:
@@ -180,27 +182,27 @@
 
     with jax.named_scope("fold"):
         fold(level, rising, falling)
+    with jax.named_scope("gather"):
+        who = leaving_cells(leaving)
+        gather_inner(found, cells, state, level, who)
     with jax.named_scope("recvz"):
         receive(range(8, 18, 2))
     with jax.named_scope("floor"):
-        end_pairs(0, level, state, zside, packs, own_packs)
+        floor = end_pairs(0, zside, packs, own_packs)
+        x, y, z, live = who
+        floor.collect(found, x, (y == below()) & (z == 0) & live)
     with jax.named_scope("recvy"):
         receive((2, 3))
     with jax.named_scope("ypairs"):
-        y_high(cells, state, pad, level, yhi, ytop)
-        y_low(cells, state, pad, level, ylo, ylow)
-    with jax.named_scope("outbox"):
-        boxes = [jnp.zeros((8, 128), jnp.float32)] * 14
-        boxes = gather_leaving(boxes, range(1, 7), cells, state, leaving, level)
+        y_high(cells, state, pad, level, yhi, ytop, found, who)
+        y_low(cells, state, pad, level, ylo, ylow, found, who)
     with jax.named_scope("recvx"):
         receive((0, 1, 4, 5, 6, 7))
     with jax.named_scope("xpairs"):
-        x_ahead(cells, state, pad, level, ahead, xhi, edges, xrow)
-        x_behind(pad, level, behind, xlo, edges)
-    with jax.named_scope("outbox2"):
-        boxes = gather_leaving(boxes, (0, 7), cells, state, leaving, level)
-        for c in range(14):
-            outbox[c : c + 1, :] = jnp.sum(boxes[c], axis=0, keepdims=True)
+        x_ahead(cells, state, pad, level, ahead, xhi, edges, xrow, found, who)
+        x_behind(pad, level, behind, xlo, edges, found, who)
+    with jax.named_scope("outbox"):
+        fill_outbox(found, outbox, who)
 
     last = len(SENDERS)
     fall = pltpu.make_async_remote_copy(
@@ -216,10 +218,12 @@
     def _():
         fall.start()
 
+    with jax.named_scope("spread"):
+        spread_end(0, floor, level, state)
     with jax.named_scope("recvtop"):
         receive((9, 11, 13, 15, 17))
     with jax.named_scope("ceiling"):
-        end_pairs(1, level, state, zside, packs, own_packs)
+        spread_end(1, end_pairs(1, zside, packs, own_packs), level, state)
     with jax.named_scope("final"):
         finish(cells, state, leaving, level)
 
@@ -389,7 +393,7 @@
         corner_y[end, 0, PACKS:8, :] = jnp.zeros((8 - PACKS, 128), jnp.float32)
 
 
-def inner_pairs(cells, state, pad, pad_up, pad_down, level, rising, falling):
+def fill_padded(cells, pad, pad_up, pad_down, level, rising, falling):
     lane = lanes()
     zero = jnp.zeros((8, 128), jnp.float32)
     row = jnp.zeros((1, 128), jnp.float32)
@@ -414,6 +418,10 @@
                 total[c, pl.ds(plane(x), 8), :] = zero
                 total[c, plane(x) - 1 : plane(x), :] = row
                 total[c, plane(x) + 8 : plane(x) + 9, :] = row
+
+
+def inner_pairs(cells, state, pad, pad_up, pad_down, level, rising, falling):
+    zero = jnp.zeros((8, 128), jnp.float32)
 
     def body(x, carry):
         base = pl.multiple_of((x + 1) * ROWS + 8, 8)
@@ -466,6 +474,11 @@
             self.total[k] = self.total[k] - force[k]
             self.total[3 + k] = self.total[3 + k] + twist[k]
 
+    def collect(self, found, index, mask):
+        for c, v in enumerate(self.total + self.springs):
+            value = jnp.take_along_axis(v, index, axis=1)
+            found[FIELDS + c] = found[FIELDS + c] + jnp.where(mask, value, 0.0)
+
     def store(self, level, rows, state, span):
         for c in range(6):
             level[c, rows, :] = level[c, rows, :] + self.total[c]
@@ -492,7 +505,7 @@
             level[c, rows, :] = level[c, rows, :] + up + down
 
 
-def x_ahead(cells, state, pad, level, ahead, xhi, edges, xrow):
+def x_ahead(cells, state, pad, level, ahead, xhi, edges, xrow, found, who):
     lane = lanes()
     for c in range(FIELDS):
         ahead[c, 7:8, :] = edges[2, c : c + 1, :]
@@ -512,9 +525,11 @@
         result = pair(first, second, DIRS[number], shear, xrow[at + 3] > 0.5)
         sums.own(result, masks_of(cells, pl.ds(56, 8), number))
     sums.store(level, pl.ds(plane(7), 8), state, pl.ds(56, 8))
-
-
-def x_behind(pad, level, behind, xlo, edges):
+    x, y, z, live = who
+    sums.collect(found, z, ((y == below()) & (x == 7)) & live)
+
+
+def x_behind(pad, level, behind, xlo, edges, found, who):
     lane = lanes()
     for c in range(FIELDS + 4 * len(ALONG_X)):
         behind[c, 8:16, :] = xlo[c]
@@ -538,9 +553,11 @@
             live = jnp.logical_and(live, lane != (0 if dz > 0 else 127))
         sums.partner(pair(first[:10], second, DIRS[number], first[10:13], live))
     sums.store(level, pl.ds(plane(0), 8), None, None)
-
-
-def y_high(cells, state, pad, level, yhi, ytop):
+    x, y, z, live = who
+    sums.collect(found, z, ((y == below()) & (x == 0)) & live)
+
+
+def y_high(cells, state, pad, level, yhi, ytop, found, who):
     lane = lanes()
     sub = lax.broadcasted_iota(jnp.int32, (8, 128), 0)
     top_fields = scaled([yhi[c] for c in range(FIELDS)])
@@ -565,9 +582,11 @@
     live = jnp.logical_and(first[13] > 0.5, sub != 0)
     sums.partner(pair(first[:10], mine, DIRS[4], first[10:13], live))
     sums.store(level, mine_rows, state, span)
-
-
-def y_low(cells, state, pad, level, ylo, ylow):
+    x, y, z, live = who
+    sums.collect(found, z, ((x == below()) & (y == 7)) & live)
+
+
+def y_low(cells, state, pad, level, ylo, ylow, found, who):
     lane = lanes()
     sub = lax.broadcasted_iota(jnp.int32, (8, 128), 0)
     low_fields = scaled([ylo[c] for c in range(FIELDS)])
@@ -593,9 +612,11 @@
             live = jnp.logical_and(live, lane != (0 if dz > 0 else 127))
         sums.partner(pair(first[:10], mine, DIRS[number], first[10:13], live))
     sums.store(level, mine_rows, state, span)
-
-
-def end_pairs(end, level, state, zside, packs, own_packs):
+    x, y, z, live = who
+    sums.collect(found, z, ((x == below()) & (y == 0)) & live)
+
+
+def end_pairs(end, zside, packs, own_packs):
     lane = lanes()
     theirs, ours = (((2, 5, 7), (6, 8)), ((6, 8), (2, 5, 7)))[end]
     top = 1 - end
@@ -640,6 +661,11 @@
         if dx:
             first = [jnp.where(lane == 0, b, v) for b, v in zip(back, turned(first, 1))]
         sums.partner(pair(first[:10], mine, DIRS[number], first[10:13], first[13] > 0.5))
+    return sums
+
+
+def spread_end(end, sums, level, state):
+    lane = lanes()
     edge = 127 * end
     hold = lane == edge
     for x in range(8):
@@ -671,31 +697,57 @@
     return offset, velocity, rotation, radius
 
 
-def gather_leaving(boxes, planes, cells, state, leaving, level):
-    boxes = list(boxes)
-    lane = lanes()
-    sub = lax.broadcasted_iota(jnp.int32, (8, 128), 0)
+def below():
+    return lax.broadcasted_iota(jnp.int32, (8, 128), 0)
+
+
+def leaving_cells(leaving):
     names = leaving[0:1, 0:64]
-    names = jnp.concatenate([names, names], axis=1)
-    names = jnp.broadcast_to(names, (8, 128))
-    height = jnp.where(names >= 0, names % 128, 0)
-    column = jnp.where(names >= 0, names // 128, -1)
+    names = jnp.broadcast_to(jnp.concatenate([names, names], axis=1), (8, 128))
+    live = names >= 0
+    names = jnp.where(live, names, 0)
+    return names // 1024, names // 128 % 8, names % 128, live
+
+
+def gather_inner(found, cells, state, level, who):
+    x_of, y_of, z_of, live = who
+    row = (y_of == below()) & live
+    zero = jnp.zeros((8, 128), jnp.float32)
+    values = [zero] * (FIELDS + 6 + 3 * SLOTS)
+    for x in range(8):
+        here = slice(x * 8, x * 8 + 8)
+        chosen = row & (x_of == x)
+        parts = [cells[c, here, :] for c in range(FIELDS)]
+        parts += [level[c, pl.ds(plane(x), 8), :] for c in range(6)]
+        parts += [state[9 + c, here, :] for c in range(3 * SLOTS)]
+        for c, v in enumerate(parts):
+            values[c] = jnp.where(chosen, jnp.take_along_axis(v, z_of, axis=1), values[c])
+    for c, v in enumerate(values):
+        found[c] = v
+
+
+def fill_outbox(found, outbox, who):
+    lane = lanes()[0:1]
+    rows = [
+        jnp.sum(found[c], axis=0, keepdims=True) for c in range(FIELDS + 6 + 3 * SLOTS)
+    ]
+    live = who[3][0:1]
+    cell = [w[0:1].astype(jnp.float32) for w in who[:3]]
     starts = [(lax.axis_index(a) * n).astype(jnp.float32) for a, n in zip(AXES, (8, 8, 128))]
-    for x in planes:
-        here = slice(x * 8, x * 8 + 8)
-        offset, velocity, rotation, radius = moved(cells, level, x)
-        springs = [state[9 + c, here, :] for c in range(3 * SLOTS)]
-        position = [
-            offset[0] + (starts[0] + float(x)),
-            offset[1] + (starts[1] + sub.astype(jnp.float32)),
-            offset[2] + (starts[2] + lane.astype(jnp.float32)),
-        ]
-        chosen = column == x * 8 + sub
-        halves = [jnp.logical_and(chosen, lane < 64), jnp.logical_and(chosen, lane >= 64)]
-        for c, v in enumerate(position + velocity + rotation + [radius] + springs):
-            values = jnp.take_along_axis(v, height, axis=1)
-            boxes[c % 14] = jnp.where(halves[c // 14], values, boxes[c % 14])
-    return boxes
+    radius = rows[9]
+    inverse = 1.0 / jnp.where(live, radius, 1.0)
+    push = STEP * inverse * inverse * inverse
+    turn = 0.125 * (inverse * inverse) * (inverse * inverse)
+    velocity = [rows[3 + k] + push * rows[10 + k] for k in range(3)]
+    velocity[2] = jnp.where(live, velocity[2] - STEP, 0.0)
+    position = [
+        jnp.where(live, rows[k] + STEP * velocity[k] + (starts[k] + cell[k]), 0.0)
+        for k in range(3)
+    ]
+    rotation = [rows[6 + k] + turn * rows[13 + k] for k in range(3)]
+    values = position + velocity + rotation + [radius] + rows[16:]
+    for c in range(14):
+        outbox[c : c + 1, :] = jnp.where(lane < 64, values[c], values[14 + c])
 
 
 def finish(cells, state, leaving, level):
@@ -752,6 +804,7 @@
             pltpu.VMEM((2, 1, 8, 128), f32),
             pltpu.VMEM((2, 1, 8, 128), f32),
             pltpu.VMEM((16, 128), f32),
+            pltpu.VMEM((FIELDS + 6 + 3 * SLOTS, 8, 128), f32),
             pltpu.VMEM((FIELDS, HEIGHT, 128), f32),
             pltpu.VMEM((FIELDS, HEIGHT, 128), f32),
             pltpu.VMEM((FIELDS, HEIGHT, 128), f32),

time: 13.8 us -> 13.6 us (0.986)
  no operation moved by 1% of the time
where the time goes in v7:
time: 13.6 us; the launch traced here: 13.5 us
  Pallas kernels  12.8 us (94%)
  between operations  0.64 us (5%)
    pallas_call x1, Pallas kernels, on_device(): pl.pallas_call(step_kernel, out_shape=[pltpu.VMEM((27, 64, 128), f32), pl...  11.9 us
    pallas_call x1, Pallas kernels, on_device(): pl.pallas_call(write_kernel, out_shape=[moved, moved, moved, jax.ShapeDty...  0.95 us

profile of v7, /device:TPU:1, one launch (start us, length us, event | category | flops | bytes accessed | tf_op | source)
XLA Modules:
  0.0 13.5 jit_solution(8954609549893752139)
XLA Ops:
  0.6 11.9 %step.1 = (f32[27,64,128]{2,1,0:T(8,128)S(1)}, f32[16,128]{1,0:T(8,128)S(1)}) custom-call(f32[3,64,128]{2,1,0:T(8,128)} %bitcast.16, f32[3,64,128]{2,1,0:T(8,128)} %bitcast.17, f32[3,64,128]{2,1,0:T(8,128)} %bitcast.18, f32[1,64,128]{2,1,0:T(8,128)} %bitcast.19, f32[18,64,128]{2,1,0:T(8,128)} %bitcast.14, s32[6,64,128]{2,1,0:T(8,128)} %bitcast.15, ...), custom_call_target="tpu_custom_call" | custom-call | tf_op jit(solution)/shard_map/step/pallas_call | solution.py:790
  12.5 1.0 %write.1 = (f32[3,64,128]{2,1,0:T(8,128)}, f32[3,64,128]{2,1,0:T(8,128)}, f32[3,64,128]{2,1,0:T(8,128)}, f32[18,64,128]{2,1,0:T(8,128)}, f32[28,1,64]{2,1,0:T(1,128)}) custom-call(f32[27,64,128]{2,1,0:T(8,128)S(1)} %get-tuple-element.12.state, f32[16,128]{1,0:T(8,128)S(1)} %get-tuple-element.13.arrivals), custom_call_target="tpu_custom_call" | custom-call | tf_op jit(solution)/shard_map/write/pallas_call | solution.py:828

commit v8 on v7

--- a/solution.py
+++ b/solution.py
@@ -77,7 +77,7 @@
     off_hbm, vel_hbm, spin_hbm, rad_hbm, hist_hbm, con_hbm, leaving_hbm,
     state, arrivals,
     xlo, xhi, ylo, yhi, edges, packs, own_packs, cells, codes, leaving,
-    xrow, ytop, ylow, rows, corner_x, corner_y, outbox, found, pad, pad_up, pad_down, level, rising, falling, behind, ahead, zside,
+    xrow, ytop, ylow, rows, corner_x, corner_y, outbox, found, marks, pad, pad_up, pad_down, level, rising, falling, behind, ahead, zside,
     recv_sems, local_sems, send_sems,
 ):
     here = [lax.axis_index(a) for a in AXES]
@@ -162,6 +162,7 @@
 
     with jax.named_scope("fill"):
         fill_padded(cells, pad, pad_up, pad_down, level, rising, falling)
+        gather_fields(found, cells, leaving, marks)
     with jax.named_scope("barrier"):
         pl.semaphore_wait(barrier, expected)
     for k in SEND_ORDER:
@@ -171,7 +172,7 @@
             copy(k).start()
 
     with jax.named_scope("inner"):
-        inner_pairs(cells, state, pad, pad_up, pad_down, level, rising, falling)
+        inner_pairs(cells, state, pad, pad_up, pad_down, level, rising, falling, found, marks)
 
     def receive(which):
         for k in which:
@@ -181,10 +182,8 @@
                 copy(k).wait_recv()
 
     with jax.named_scope("fold"):
-        fold(level, rising, falling)
-    with jax.named_scope("gather"):
+        fold(level, rising, falling, found, marks)
         who = leaving_cells(leaving)
-        gather_inner(found, cells, state, level, who)
     with jax.named_scope("recvz"):
         receive(range(8, 18, 2))
     with jax.named_scope("floor"):
@@ -420,7 +419,7 @@
                 total[c, plane(x) + 8 : plane(x) + 9, :] = row
 
 
-def inner_pairs(cells, state, pad, pad_up, pad_down, level, rising, falling):
+def inner_pairs(cells, state, pad, pad_up, pad_down, level, rising, falling, found, marks):
     zero = jnp.zeros((8, 128), jnp.float32)
 
     def body(x, carry):
@@ -447,8 +446,11 @@
         for k in range(3):
             level[k, pl.ds(base, 8), :] = level[k, pl.ds(base, 8), :] + forces[k]
             level[3 + k, pl.ds(base, 8), :] = level[3 + k, pl.ds(base, 8), :] + twists[k]
+        height, chosen = marks[0], marks[1] == x
         for c in range(3 * SLOTS):
             state[9 + c, here, :] = springs[c]
+            value = jnp.take_along_axis(springs[c], height, axis=1)
+            found[FIELDS + 6 + c] = jnp.where(chosen, value, found[FIELDS + 6 + c])
         return carry
 
     lax.fori_loop(0, 8, body, 0)
@@ -495,14 +497,20 @@
     return [cells[CODES + s, span, :] == float(number) for s in range(SLOTS)]
 
 
-def fold(level, rising, falling):
-    lane = lanes()
+def fold(level, rising, falling, found, marks):
+    lane = lanes()
+    sums = [jnp.zeros((8, 128), jnp.float32)] * 6
     for x in range(8):
         rows = pl.ds(plane(x), 8)
         for c in range(6):
             up = jnp.where(lane == 0, 0.0, pltpu.roll(rising[c, rows, :], 1, 1))
             down = jnp.where(lane == 127, 0.0, pltpu.roll(falling[c, rows, :], 127, 1))
-            level[c, rows, :] = level[c, rows, :] + up + down
+            total = level[c, rows, :] + up + down
+            level[c, rows, :] = total
+            value = jnp.take_along_axis(total, marks[0], axis=1)
+            sums[c] = jnp.where(marks[1] == x, value, sums[c])
+    for c in range(6):
+        found[FIELDS + c] = sums[c]
 
 
 def x_ahead(cells, state, pad, level, ahead, xhi, edges, xrow, found, who):
@@ -709,21 +717,22 @@
     return names // 1024, names // 128 % 8, names % 128, live
 
 
-def gather_inner(found, cells, state, level, who):
-    x_of, y_of, z_of, live = who
-    row = (y_of == below()) & live
+def gather_fields(found, cells, leaving, marks):
+    x_of, y_of, z_of, live = leaving_cells(leaving)
+    plane_of = jnp.where((y_of == below()) & live, x_of, -1)
+    marks[0] = z_of
+    marks[1] = plane_of
     zero = jnp.zeros((8, 128), jnp.float32)
-    values = [zero] * (FIELDS + 6 + 3 * SLOTS)
+    values = [zero] * FIELDS
     for x in range(8):
         here = slice(x * 8, x * 8 + 8)
-        chosen = row & (x_of == x)
-        parts = [cells[c, here, :] for c in range(FIELDS)]
-        parts += [level[c, pl.ds(plane(x), 8), :] for c in range(6)]
-        parts += [state[9 + c, here, :] for c in range(3 * SLOTS)]
-        for c, v in enumerate(parts):
-            values[c] = jnp.where(chosen, jnp.take_along_axis(v, z_of, axis=1), values[c])
-    for c, v in enumerate(values):
-        found[c] = v
+        for c in range(FIELDS):
+            value = jnp.take_along_axis(cells[c, here, :], z_of, axis=1)
+            values[c] = jnp.where(plane_of == x, value, values[c])
+    for c in range(FIELDS):
+        found[c] = values[c]
+    for c in range(3 * SLOTS):
+        found[FIELDS + 6 + c] = zero
 
 
 def fill_outbox(found, outbox, who):
@@ -805,6 +814,7 @@
             pltpu.VMEM((2, 1, 8, 128), f32),
             pltpu.VMEM((16, 128), f32),
             pltpu.VMEM((FIELDS + 6 + 3 * SLOTS, 8, 128), f32),
+            pltpu.VMEM((2, 8, 128), jnp.int32),
             pltpu.VMEM((FIELDS, HEIGHT, 128), f32),
             pltpu.VMEM((FIELDS, HEIGHT, 128), f32),
             pltpu.VMEM((FIELDS, HEIGHT, 128), f32),

time: 13.6 us -> 13.6 us (level)
  no operation moved by 1% of the time
where the time goes in v8:
time: 13.6 us; the launch traced here: 13.5 us
  Pallas kernels  12.8 us (94%)
  between operations  0.64 us (5%)
    pallas_call x1, Pallas kernels, on_device(): pl.pallas_call(step_kernel, out_shape=[pltpu.VMEM((27, 64, 128), f32), pl...  11.9 us
    pallas_call x1, Pallas kernels, on_device(): pl.pallas_call(write_kernel, out_shape=[moved, moved, moved, jax.ShapeDty...  0.95 us

profile of v8, /device:TPU:1, one launch (start us, length us, event | category | flops | bytes accessed | tf_op | source)
XLA Modules:
  0.0 13.5 jit_solution(10929277406708889617)
XLA Ops:
  0.6 11.9 %step.1 = (f32[27,64,128]{2,1,0:T(8,128)S(1)}, f32[16,128]{1,0:T(8,128)S(1)}) custom-call(f32[3,64,128]{2,1,0:T(8,128)} %bitcast.16, f32[3,64,128]{2,1,0:T(8,128)} %bitcast.17, f32[3,64,128]{2,1,0:T(8,128)} %bitcast.18, f32[1,64,128]{2,1,0:T(8,128)} %bitcast.19, f32[18,64,128]{2,1,0:T(8,128)} %bitcast.14, s32[6,64,128]{2,1,0:T(8,128)} %bitcast.15, ...), custom_call_target="tpu_custom_call" | custom-call | tf_op jit(solution)/shard_map/step/pallas_call | solution.py:799
  12.5 1.0 %write.1 = (f32[3,64,128]{2,1,0:T(8,128)}, f32[3,64,128]{2,1,0:T(8,128)}, f32[3,64,128]{2,1,0:T(8,128)}, f32[18,64,128]{2,1,0:T(8,128)}, f32[28,1,64]{2,1,0:T(1,128)}) custom-call(f32[27,64,128]{2,1,0:T(8,128)S(1)} %get-tuple-element.12.state, f32[16,128]{1,0:T(8,128)S(1)} %get-tuple-element.13.arrivals), custom_call_target="tpu_custom_call" | custom-call | tf_op jit(solution)/shard_map/write/pallas_call | solution.py:838

commit v9 on v8

--- a/solution.py
+++ b/solution.py
@@ -67,7 +67,8 @@
 
 def step_kernel(*refs):
     pl.run_scoped(
-        lambda local_sems, send_sems: step_body(*refs, local_sems, send_sems),
+        lambda *sems: step_body(*refs, *sems),
+        pltpu.SemaphoreType.DMA((len(SENDERS) + 1,)),
         pltpu.SemaphoreType.DMA((7,)),
         pltpu.SemaphoreType.DMA((len(SENDERS) + 1,)),
     )
@@ -247,7 +248,11 @@
         fall.wait_send()
 
 
-def write_kernel(
+def write_kernel(*refs):
+    pl.run_scoped(lambda sems: write_body(*refs, sems), pltpu.SemaphoreType.DMA((5,)))
+
+
+def write_body(
     state, arrivals, new_off, new_vel, new_spin, new_hist, entered, unpacked, sems
 ):
     copies = [
@@ -824,7 +829,6 @@
             pltpu.VMEM((FIELDS + 4 * len(ALONG_X), ROWS, 128), f32),
             pltpu.VMEM((FIELDS, ROWS, 128), f32),
             pltpu.VMEM((2, FULL, ROWS, 128), f32),
-            pltpu.SemaphoreType.DMA((len(SENDERS) + 1,)),
         ],
         compiler_params=pltpu.CompilerParams(
             collective_id=0, has_side_effects=True, vmem_limit_bytes=24 << 20
@@ -844,7 +848,7 @@
         ],
         in_specs=[vmem] * 2,
         out_specs=[hbm] * 5,
-        scratch_shapes=[pltpu.VMEM((28, 1, 64), f32), pltpu.SemaphoreType.DMA((5,))],
+        scratch_shapes=[pltpu.VMEM((28, 1, 64), f32)],
         compiler_params=pltpu.CompilerParams(vmem_limit_bytes=8 << 20),
         name="write",
     )(state, arrivals)

time: 13.6 us -> 13.4 us (0.985)
  Pallas kernels: 12.8 us -> 12.6 us
    pallas_call x1, Pallas kernels: 11.9 us -> 11.7 us  [on_device(): pl.pallas_call(step_kernel, out_shape=[pltpu.VMEM((27, 64, 128), f32), pl...]
where the time goes in v9:
time: 13.4 us; the launch traced here: 13.2 us
  Pallas kernels  12.6 us (94%)
  between operations  0.63 us (5%)
    pallas_call x1, Pallas kernels, on_device(): pl.pallas_call(step_kernel, out_shape=[pltpu.VMEM((27, 64, 128), f32), pl...  11.7 us
    pallas_call x1, Pallas kernels, on_device(): pl.pallas_call(write_kernel, out_shape=[moved, moved, moved, jax.ShapeDty...  0.9 us

profile of v9, /device:TPU:1, one launch (start us, length us, event | category | flops | bytes accessed | tf_op | source)
XLA Modules:
  0.0 13.2 jit_solution(8974971761140266148)
XLA Ops:
  0.6 11.7 %step.1 = (f32[27,64,128]{2,1,0:T(8,128)S(1)}, f32[16,128]{1,0:T(8,128)S(1)}) custom-call(f32[3,64,128]{2,1,0:T(8,128)} %bitcast.16, f32[3,64,128]{2,1,0:T(8,128)} %bitcast.17, f32[3,64,128]{2,1,0:T(8,128)} %bitcast.18, f32[1,64,128]{2,1,0:T(8,128)} %bitcast.19, f32[18,64,128]{2,1,0:T(8,128)} %bitcast.14, s32[6,64,128]{2,1,0:T(8,128)} %bitcast.15, ...), custom_call_target="tpu_custom_call" | custom-call | tf_op jit(solution)/shard_map/step/pallas_call | solution.py:804
  12.3 0.9 %write.1 = (f32[3,64,128]{2,1,0:T(8,128)}, f32[3,64,128]{2,1,0:T(8,128)}, f32[3,64,128]{2,1,0:T(8,128)}, f32[18,64,128]{2,1,0:T(8,128)}, f32[28,1,64]{2,1,0:T(1,128)}) custom-call(f32[27,64,128]{2,1,0:T(8,128)S(1)} %get-tuple-element.12.refs_0_, f32[16,128]{1,0:T(8,128)S(1)} %get-tuple-element.13.refs_1_), custom_call_target="tpu_custom_call" | custom-call | tf_op jit(solution)/shard_map/write/pallas_call | solution.py:842

commit v10 on v9

--- a/solution.py
+++ b/solution.py
@@ -512,6 +512,9 @@
             down = jnp.where(lane == 127, 0.0, pltpu.roll(falling[c, rows, :], 127, 1))
             total = level[c, rows, :] + up + down
             level[c, rows, :] = total
+    for x in range(8):
+        for c in range(6):
+            total = level[c, pl.ds(plane(x), 8), :]
             value = jnp.take_along_axis(total, marks[0], axis=1)
             sums[c] = jnp.where(marks[1] == x, value, sums[c])
     for c in range(6):

time: 13.4 us -> 13.4 us (level)
  no operation moved by 1% of the time
where the time goes in v10:
time: 13.4 us; the launch traced here: 13.2 us
  Pallas kernels  12.6 us (94%)
  between operations  0.63 us (5%)
    pallas_call x1, Pallas kernels, on_device(): pl.pallas_call(step_kernel, out_shape=[pltpu.VMEM((27, 64, 128), f32), pl...  11.7 us
    pallas_call x1, Pallas kernels, on_device(): pl.pallas_call(write_kernel, out_shape=[moved, moved, moved, jax.ShapeDty...  0.9 us

profile of v10, /device:TPU:1, one launch (start us, length us, event | category | flops | bytes accessed | tf_op | source)
XLA Modules:
  0.0 13.2 jit_solution(11246371050778480376)
XLA Ops:
  0.6 11.7 %step.1 = (f32[27,64,128]{2,1,0:T(8,128)S(1)}, f32[16,128]{1,0:T(8,128)S(1)}) custom-call(f32[3,64,128]{2,1,0:T(8,128)} %bitcast.16, f32[3,64,128]{2,1,0:T(8,128)} %bitcast.17, f32[3,64,128]{2,1,0:T(8,128)} %bitcast.18, f32[1,64,128]{2,1,0:T(8,128)} %bitcast.19, f32[18,64,128]{2,1,0:T(8,128)} %bitcast.14, s32[6,64,128]{2,1,0:T(8,128)} %bitcast.15, ...), custom_call_target="tpu_custom_call" | custom-call | tf_op jit(solution)/shard_map/step/pallas_call | solution.py:807
  12.3 0.9 %write.1 = (f32[3,64,128]{2,1,0:T(8,128)}, f32[3,64,128]{2,1,0:T(8,128)}, f32[3,64,128]{2,1,0:T(8,128)}, f32[18,64,128]{2,1,0:T(8,128)}, f32[28,1,64]{2,1,0:T(1,128)}) custom-call(f32[27,64,128]{2,1,0:T(8,128)S(1)} %get-tuple-element.12.refs_0_, f32[16,128]{1,0:T(8,128)S(1)} %get-tuple-element.13.refs_1_), custom_call_target="tpu_custom_call" | custom-call | tf_op jit(solution)/shard_map/write/pallas_call | solution.py:845

commit v11 on v10

--- a/solution.py
+++ b/solution.py
@@ -194,8 +194,10 @@
     with jax.named_scope("recvy"):
         receive((2, 3))
     with jax.named_scope("ypairs"):
-        y_high(cells, state, pad, level, yhi, ytop, found, who)
-        y_low(cells, state, pad, level, ylo, ylow, found, who)
+        later = [
+            y_high(cells, state, pad, level, yhi, ytop, found, who),
+            y_low(cells, state, pad, level, ylo, ylow, found, who),
+        ]
     with jax.named_scope("recvx"):
         receive((0, 1, 4, 5, 6, 7))
     with jax.named_scope("xpairs"):
@@ -219,6 +221,8 @@
         fall.start()
 
     with jax.named_scope("spread"):
+        for sums, *where in later:
+            sums.store(*where)
         spread_end(0, floor, level, state)
     with jax.named_scope("recvtop"):
         receive((9, 11, 13, 15, 17))
@@ -597,9 +601,9 @@
     first = turned(top_fields + [yhi[FIELDS + k] for k in range(4)], 1, 0)
     live = jnp.logical_and(first[13] > 0.5, sub != 0)
     sums.partner(pair(first[:10], mine, DIRS[4], first[10:13], live))
-    sums.store(level, mine_rows, state, span)
     x, y, z, live = who
     sums.collect(found, z, ((x == below()) & (y == 7)) & live)
+    return sums, level, mine_rows, state, span
 
 
 def y_low(cells, state, pad, level, ylo, ylow, found, who):
@@ -627,9 +631,9 @@
         if dz:
             live = jnp.logical_and(live, lane != (0 if dz > 0 else 127))
         sums.partner(pair(first[:10], mine, DIRS[number], first[10:13], live))
-    sums.store(level, mine_rows, state, span)
     x, y, z, live = who
     sums.collect(found, z, ((x == below()) & (y == 0)) & live)
+    return sums, level, mine_rows, state, span
 
 
 def end_pairs(end, zside, packs, own_packs):

time: 13.4 us -> 13.4 us (level)
  no operation moved by 1% of the time
where the time goes in v11:
time: 13.4 us; the launch traced here: 13.2 us
  Pallas kernels  12.6 us (94%)
  between operations  0.63 us (5%)
    pallas_call x1, Pallas kernels, on_device(): pl.pallas_call(step_kernel, out_shape=[pltpu.VMEM((27, 64, 128), f32), pl...  11.7 us
    pallas_call x1, Pallas kernels, on_device(): pl.pallas_call(write_kernel, out_shape=[moved, moved, moved, jax.ShapeDty...  0.9 us

profile of v11, /device:TPU:1, one launch (start us, length us, event | category | flops | bytes accessed | tf_op | source)
XLA Modules:
  0.0 13.2 jit_solution(16157501628977167523)
XLA Ops:
  0.6 11.7 %step.1 = (f32[27,64,128]{2,1,0:T(8,128)S(1)}, f32[16,128]{1,0:T(8,128)S(1)}) custom-call(f32[3,64,128]{2,1,0:T(8,128)} %bitcast.16, f32[3,64,128]{2,1,0:T(8,128)} %bitcast.17, f32[3,64,128]{2,1,0:T(8,128)} %bitcast.18, f32[1,64,128]{2,1,0:T(8,128)} %bitcast.19, f32[18,64,128]{2,1,0:T(8,128)} %bitcast.14, s32[6,64,128]{2,1,0:T(8,128)} %bitcast.15, ...), custom_call_target="tpu_custom_call" | custom-call | tf_op jit(solution)/shard_map/step/pallas_call | solution.py:811
  12.3 0.9 %write.1 = (f32[3,64,128]{2,1,0:T(8,128)}, f32[3,64,128]{2,1,0:T(8,128)}, f32[3,64,128]{2,1,0:T(8,128)}, f32[18,64,128]{2,1,0:T(8,128)}, f32[28,1,64]{2,1,0:T(1,128)}) custom-call(f32[27,64,128]{2,1,0:T(8,128)S(1)} %get-tuple-element.12.refs_0_, f32[16,128]{1,0:T(8,128)S(1)} %get-tuple-element.13.refs_1_), custom_call_target="tpu_custom_call" | custom-call | tf_op jit(solution)/shard_map/write/pallas_call | solution.py:849

commit v12 on v10

--- a/solution.py
+++ b/solution.py
@@ -418,10 +418,8 @@
         pad[c, plane(8) + 8 : plane(8) + 9, :] = row
     for total in (level, rising, falling):
         for c in range(6):
-            for x in range(9):
+            for x in range(8):
                 total[c, pl.ds(plane(x), 8), :] = zero
-                total[c, plane(x) - 1 : plane(x), :] = row
-                total[c, plane(x) + 8 : plane(x) + 9, :] = row
 
 
 def inner_pairs(cells, state, pad, pad_up, pad_down, level, rising, falling, found, marks):

time: 13.4 us -> 13.4 us (level)
  no operation moved by 1% of the time
where the time goes in v12:
time: 13.4 us; the launch traced here: 13.2 us
  Pallas kernels  12.6 us (94%)
  between operations  0.63 us (5%)
    pallas_call x1, Pallas kernels, on_device(): pl.pallas_call(step_kernel, out_shape=[pltpu.VMEM((27, 64, 128), f32), pl...  11.7 us
    pallas_call x1, Pallas kernels, on_device(): pl.pallas_call(write_kernel, out_shape=[moved, moved, moved, jax.ShapeDty...  0.9 us

profile of v12, /device:TPU:1, one launch (start us, length us, event | category | flops | bytes accessed | tf_op | source)
XLA Modules:
  0.0 13.2 jit_solution(10831262281048884280)
XLA Ops:
  0.6 11.7 %step.1 = (f32[27,64,128]{2,1,0:T(8,128)S(1)}, f32[16,128]{1,0:T(8,128)S(1)}) custom-call(f32[3,64,128]{2,1,0:T(8,128)} %bitcast.16, f32[3,64,128]{2,1,0:T(8,128)} %bitcast.17, f32[3,64,128]{2,1,0:T(8,128)} %bitcast.18, f32[1,64,128]{2,1,0:T(8,128)} %bitcast.19, f32[18,64,128]{2,1,0:T(8,128)} %bitcast.14, s32[6,64,128]{2,1,0:T(8,128)} %bitcast.15, ...), custom_call_target="tpu_custom_call" | custom-call | tf_op jit(solution)/shard_map/step/pallas_call | solution.py:805
  12.3 0.9 %write.1 = (f32[3,64,128]{2,1,0:T(8,128)}, f32[3,64,128]{2,1,0:T(8,128)}, f32[3,64,128]{2,1,0:T(8,128)}, f32[18,64,128]{2,1,0:T(8,128)}, f32[28,1,64]{2,1,0:T(1,128)}) custom-call(f32[27,64,128]{2,1,0:T(8,128)S(1)} %get-tuple-element.12.refs_0_, f32[16,128]{1,0:T(8,128)S(1)} %get-tuple-element.13.refs_1_), custom_call_target="tpu_custom_call" | custom-call | tf_op jit(solution)/shard_map/write/pallas_call | solution.py:843
